TPU v7x, 32 devices: a whole 2x2x4 slice. The times are simulated.
32 devices in a mesh: leaf: 8 (over z, y), sub: 4 (over x, core).
Axes of the slice: x: 2, y: 2, z: 4, core: 2. Of those that a mesh axis runs over, the one named last changes fastest.
Arguments:
- vectors: bfloat16 [64, 8192], P('sub', 'leaf'), may hold values from -6 to 6
- near_blocks: bfloat16 [32, 9, 256, 256], P(('leaf', 'sub')), may hold values from -0.125 to 0.125
- near_cols: int32 [32, 9], P(('leaf', 'sub')), may hold values from 0 to 31, as said below
- near_mask: int32 [32, 9], P(('leaf', 'sub')), may hold values from 0 to 1, as said below
- leaf_basis: bfloat16 [32, 32, 256], P('leaf'), may hold values from -0.375 to 0.375
- transfer: bfloat16 [48, 32, 32], P('leaf'), may hold values from -1 to 1
- coupling: bfloat16 [56, 27, 32, 32], P('leaf'), may hold values from -0.3125 to 0.3125
- far_targets: int32 [56, 27], P('leaf'), may hold values from 0 to 55, as said below
- far_mask: int32 [56, 27], P('leaf'), may hold values from 0 to 1
Outputs:
- result: bfloat16 [64, 8192], P('sub', 'leaf')
Inputs may be any that keep to these rules, and one draw needn't show every extreme that they name: `near_cols`: row i names 9 leaves; its first entry is leaf i; every entry is a leaf of the subtree of leaf i or of the subtree just before or after it; the entries marked live are distinct. `near_mask`: the first entry of each row is 1. `far_targets`: entry (c, k) names a cluster on the same level as cluster c, in any subtree. The 189 entries of one subtree's rows, masked ones included, name clusters of any one subtree at most 32 times; in every draw some subtree is named exactly 32 times, by live entries, from every subtree.
All inputs are finite; a program needn't handle non-finite values.
Results may differ from a plain program's by a relative error of at most 0.0065.
Values may be sent and summed in bfloat16 or wider, within the bound.
No kernel may reach another device: no remote copies, remote signals or barrier semaphores. Data moves between devices by JAX's collectives and lax.ppermute only.
A program may use at most 64 MiB of HBM per device.

v0:
```python
import jax
import jax.numpy as jnp
from jax import lax
from jax.sharding import PartitionSpec as P


def with_halo(cells, sides, width):
    for axis, dim in sides:
        count = lax.axis_size(axis)
        ends = count - 1
        head = lax.slice_in_dim(cells, 0, width, axis=dim)
        tail = lax.slice_in_dim(cells, cells.shape[dim] - width, cells.shape[dim], axis=dim)
        cells = jnp.concatenate(
            [
                lax.ppermute(tail, axis, [(i, (i + 1) % count) for i in range(ends)]),
                cells,
                lax.ppermute(head, axis, [((i + 1) % count, i) for i in range(ends)]),
            ],
            axis=dim,
        )
    return cells


def near_field(window, blocks, columns, alive_mask, first_leaf, leaf_size):
    row_count = window.shape[0]
    pieces = window.reshape(row_count, window.shape[1] // leaf_size, leaf_size)
    relative = (columns - first_leaf).reshape(-1)
    taken = jnp.take(pieces, relative, axis=1)
    taken = taken.reshape(row_count, columns.shape[0], columns.shape[1], leaf_size)
    taken = taken * alive_mask.astype(jnp.bfloat16)[None, :, :, None]
    product = jnp.einsum("vjkp,jkpq->vjq", taken, blocks, preferred_element_type=jnp.float32)
    return product.reshape(row_count, columns.shape[0] * leaf_size)


def pack_slots(values, owners, places, peer_count, capacity):
    highest = lax.Precision.HIGHEST
    peer_ids = jnp.arange(peer_count, dtype=jnp.int32)
    onehot = (owners[:, None] == peer_ids[None, :]).astype(jnp.int32)
    rank_within = jnp.sum(onehot * (jnp.cumsum(onehot, axis=0) - 1), axis=1)
    slot_of = owners * capacity + rank_within
    slot_ids = jnp.arange(peer_count * capacity, dtype=jnp.int32)
    select = slot_ids[:, None] == slot_of[None, :]
    send_values = jnp.dot(select.astype(jnp.float32), values, precision=highest)
    send_places = jnp.sum(jnp.where(select, places[None, :], 0), axis=1)
    return (send_values, send_places)


def sum_slots(got_values, got_places, clusters):
    cluster_ids = jnp.arange(clusters, dtype=jnp.int32)
    hits = (got_places[None, :] == cluster_ids[:, None]).astype(jnp.float32)
    return jnp.dot(hits, got_values, precision=lax.Precision.HIGHEST)


def local(
    vectors,
    near_blocks,
    near_cols,
    near_mask,
    leaf_basis,
    transfer,
    coupling,
    far_targets,
    far_mask,
):
    highest = lax.Precision.HIGHEST
    leaf_size = leaf_basis.shape[2]
    subtree = leaf_basis.shape[0]
    clusters = coupling.shape[0]
    far_count = coupling.shape[1]
    rank_size = coupling.shape[2]
    own_vecs = vectors.shape[0]
    peer_count = lax.axis_size("leaf")
    tree_index = lax.axis_index("leaf")
    window_first = (tree_index - 1) * subtree
    padded = with_halo(vectors, (("leaf", 1),), subtree * leaf_size)
    window = lax.all_gather(padded, "sub", axis=0, tiled=True)
    near_part = near_field(window, near_blocks, near_cols, near_mask, window_first, leaf_size)
    near_total = lax.all_to_all(
        near_part.astype(jnp.bfloat16), "sub", split_axis=0, concat_axis=1, tiled=True
    ).astype(near_part.dtype)
    sizes_all = []
    level_size = subtree
    while level_size >= 1:
        sizes_all.append(level_size)
        level_size = level_size // 2
    starts_all = [sum(sizes_all[:number]) for number in range(len(sizes_all))]
    maps_all = transfer.astype(jnp.float32)
    leaf_pieces = vectors.reshape(own_vecs, subtree, leaf_size)
    coeffs = jnp.einsum("vsp,srp->svr", leaf_pieces, leaf_basis, preferred_element_type=jnp.float32)
    hats = [coeffs]
    for level_no in range(len(sizes_all) - 1):
        level_size = sizes_all[level_no]
        level_start = starts_all[level_no]
        child = hats[-1].reshape(level_size // 2, 2, own_vecs, rank_size)
        level_maps = maps_all[level_start : level_start + level_size].reshape(
            level_size // 2, 2, rank_size, rank_size
        )
        hats.append(jnp.einsum("pcvr,pcrq->pvq", child, level_maps, precision=highest))
    all_hats = jnp.concatenate(hats, axis=0)
    terms = jnp.einsum("cvr,ckrq->ckvq", all_hats, coupling.astype(jnp.float32), precision=highest)
    terms = terms * far_mask.astype(jnp.float32)[:, :, None, None]
    terms = terms.reshape(clusters * far_count, own_vecs * rank_size)
    owners = (far_targets // clusters).reshape(-1)
    places = (far_targets % clusters).reshape(-1)
    capacity = max(2, (4 * clusters * far_count + 3 * peer_count - 1) // (3 * peer_count))
    send_values, send_places = pack_slots(terms, owners, places, peer_count, capacity)
    got_values, got_places = (
        lax.all_to_all(send_values, "leaf", split_axis=0, concat_axis=0, tiled=True),
        lax.all_to_all(send_places, "leaf", split_axis=0, concat_axis=0, tiled=True),
    )
    incoming = sum_slots(got_values, got_places, clusters)
    incoming = incoming.reshape(clusters, own_vecs, rank_size)
    downward = [
        incoming[starts_all[number] : starts_all[number] + sizes_all[number]]
        for number in range(len(sizes_all))
    ]
    for level_no in range(len(sizes_all) - 2, -1, -1):
        level_size = sizes_all[level_no]
        level_start = starts_all[level_no]
        level_maps = maps_all[level_start : level_start + level_size].reshape(
            level_size // 2, 2, rank_size, rank_size
        )
        pushed = jnp.einsum("pvq,pcrq->pcvr", downward[level_no + 1], level_maps, precision=highest)
        downward[level_no] = downward[level_no] + pushed.reshape(level_size, own_vecs, rank_size)
    far_out = jnp.einsum(
        "svr,srp->vsp", downward[0], leaf_basis.astype(jnp.float32), precision=highest
    )
    far_out = far_out.reshape(own_vecs, subtree * leaf_size)
    return (near_total + far_out).astype(jnp.bfloat16)


def solution(mesh):
    return jax.shard_map(
        local,
        mesh=mesh,
        in_specs=(
            P("sub", "leaf"),
            P(("leaf", "sub"), None, None, None),
            P(("leaf", "sub"), None),
            P(("leaf", "sub"), None),
            P("leaf", None, None),
            P("leaf", None, None),
            P("leaf", None, None, None),
            P("leaf", None),
            P("leaf", None),
        ),
        out_specs=P("sub", "leaf"),
        check_vma=False,
    )
```

profile of v0, /device:TPU:0, one launch (start us, length us, event | category | flops | bytes accessed | tf_op | source)
XLA Modules:
  0.0 52.0 jit_solution(10137854719792980306)
XLA Ops:
  0.0 1.4 %collective-permute-start.1 = (bf16[16,1024]{1,0:T(8,128)(2,1)}, bf16[16,1024]{1,0:T(8,128)(2,1)}, u32[]{:S(2)}, u32[]{:S(2)}) collective-permute-start(bf16[16,1024]{1,0:T(8,128)(2,1)} %param.9), channel_id=1, source_target_pairs={{4,0},{8,4},{12,8},{16,12},{20,16},{24,20},{28,24},{5,1},{9,5},{13... | collective-permute-start | bytes 98312 | tf_op jit(solution)/shard_map/ppermute | solution.py:17
  1.4 6.1 %collective-permute-start = (bf16[16,1024]{1,0:T(8,128)(2,1)}, bf16[16,1024]{1,0:T(8,128)(2,1)}, u32[]{:S(2)}, u32[]{:S(2)}) collective-permute-start(bf16[16,1024]{1,0:T(8,128)(2,1)} %param.9), channel_id=1, source_target_pairs={{0,4},{4,8},{8,12},{12,16},{16,20},{20,24},{24,28},{1,5},{5,9},{9,... | collective-permute-start | bytes 98312 | tf_op jit(solution)/shard_map/ppermute | solution.py:15
  7.6 0.7 %add_select_fusion = (s32[7,27]{1,0:T(8,128)S(1)}, s32[7,27]{1,0:T(8,128)S(1)}) fusion(s32[7,27]{1,0:T(8,128)} %param.16), kind=kLoop, calls=%fused_computation.49 | loop fusion | flops 2268 | bytes 2268 | tf_op jit(solution)/shard_map/jit(remainder)/select_n | solution.py:104
  8.4 0.6 %reduce-window.6 = s32[8,2,128]{2,0,1:T(8,128)S(1)} reduce-window(s32[8,2,128]{2,0,1:T(8,128)S(1)} %convert_bitcast_fusion, s32[]{:T(128)} %constant.49.clone.1), window={size=1x1x128 pad=0_0x0_0x127_0}, to_apply=%region_0.1 | reduce-window | flops 260096 | bytes 16388 | tf_op jit(solution)/shard_map/reduce-window
  9.0 0.2 slice_reduce_fusion
  9.5 0.7 %all_to_all.21 = s32[8,32,1]{1,0,2:T(8,128)} reshape(s32[256]{0:T(256)S(1)} %select_reduce_fusion) | data formatting | bytes 2048 | tf_op jit(solution)/shard_map/all_to_all | solution.py:109
  10.2 5.6 %all-to-all-start.1 = ((s32[8,32,1]{1,2,0:T(1,128)}), s32[8,32,1]{1,2,0:T(1,128)}, u32[]{:S(2)}, u32[]{:S(2)}) async-start(s32[8,32,1]{1,2,0:T(1,128)} %bitcast.14), calls=%async_computation.1 | async-start | bytes 8192 | tf_op jit(solution)/shard_map/all_to_all | solution.py:109
  15.8 0.6 %multiply_add_fusion = s32[8,32]{1,0:T(8,128)} fusion(), kind=kLoop, calls=%fused_computation.52 | loop fusion | flops 512 | bytes 1024 | tf_op jit(solution)/shard_map/eq | solution.py:42
  16.4 0.7 %convert_element_type.50 = f32[7,27]{1,0:T(8,128)S(1)} convert(s32[7,27]{1,0:T(8,128)} %param.17) | non-fusion elementwise | flops 189 | bytes 1512 | tf_op jit(solution)/shard_map/convert_element_type | solution.py:101
  17.1 0.8 %slice.36 = bf16[4,32,32]{2,1,0:T(8,128)(2,1)S(1)} slice(bf16[6,32,32]{2,1,0:T(8,128)(2,1)} %param.14), slice={[0:4], [0:32], [0:32]} | slice | bytes 16384 | tf_op jit(solution)/shard_map/slice | solution.py:95
  17.9 1.0 %fusion.26 = f32[4,16,32]{2,1,0:T(8,128)S(1)} fusion(bf16[4,32,256]{2,1,0:T(8,128)(2,1)} %param.13, bf16[2,4,8,256]{3,2,1,0:T(8,128)(2,1)} %bitcast.105), kind=kOutput, calls=%fused_computation.33 | convolution fusion | flops 1048576 | bytes 106496 | tf_op jit(solution)/shard_map/vsp,srp->svr/dot_general | solution.py:89
  18.9 0.2 convolution_bitcast_fusion.1
  19.1 0.9 %convolution_bitcast_fusion.2 = f32[1,16,32]{2,1,0:T(8,128)S(1)} fusion(f32[2,16,32]{2,1,0:T(8,128)S(1)} %convolution_bitcast_fusion.1, bf16[6,32,32]{2,1,0:T(8,128)(2,1)} %param.14), kind=kOutput, calls=%fused_computation.13 | convolution fusion | flops 393216 | bytes 22528 | tf_op jit(solution)/shard_map/pcvr,pcrq->pvq/dot_general | solution.py:98
  20.0 0.8 %multiply_bitcast_fusion = f32[7,27,16,32]{3,2,1,0:T(8,128)S(1)} fusion(bf16[7,27,32,32]{3,2,1,0:T(8,128)(2,1)S(1)} %copy-done, f32[7,27]{1,0:T(8,128)S(1)} %convert_element_type.50, f32[1,16,32]{2,1,0:T(8,128)S(1)} %convolution_bitcast_fusion.2, f32[2,16,32]{2,1,0:T(8,128)S(1)} %convolution_bitcast_fusion.1, f32[4,16,32]{2,1,0:T(8,128)S(1)} %fusion.26), kind=kOutput, calls=%fused_computation.1 | convolution fusion | flops 37262848 | bytes 789236 | tf_op jit(solution)/shard_map/cvr,ckrq->ckvq/dot_general | solution.py:100
  20.9 0.6 %reshape.180 = f32[189,512,1]{1,0,2:T(8,128)S(1)} reshape(f32[7,27,16,32]{3,2,1,0:T(8,128)S(1)} %multiply_bitcast_fusion) | data formatting | bytes 774144 | tf_op jit(solution)/shard_map/reshape | solution.py:102
  21.5 1.9 %fusion.16 = f32[8,32,512]{2,1,0:T(8,128)} fusion(f32[189,512,1]{1,0,2:T(8,128)S(1)} %reshape.180, s32[189]{0:T(256)} %copy-done.3, s32[8,32]{1,0:T(8,128)} %multiply_add_fusion), kind=kOutput, calls=%fused_computation.19 | convolution fusion | flops 297319680 | bytes 913140 | tf_op jit(solution)/shard_map/dot_general | solution.py:43
  23.4 0.7 %fusion.36 = s32[9]{0:T(128)S(1)} fusion(s32[1,9]{1,0:T(1,128)} %param.11, s32[]{:T(128)S(6)} %mul.40), kind=kLoop, calls=%fused_computation.62 | loop fusion | flops 36 | bytes 76 | tf_op jit(solution)/shard_map/jit(_take)/jit(_where)/select_n | solution.py:28
  24.0 0.7 %compare_and_fusion = pred[9]{0:T(512)(128)(4,1)S(1)} fusion(s32[1,9]{1,0:T(1,128)} %param.11, s32[]{:T(128)S(6)} %mul.40), kind=kLoop, calls=%fused_computation.60 | loop fusion | flops 63 | bytes 49 | tf_op jit(solution)/shard_map/jit(_take)/and | solution.py:28
  24.7 6.0 %all-to-all-start.2 = ((f32[8,32,512]{2,1,0:T(8,128)}), f32[8,32,512]{2,1,0:T(8,128)S(1)}, u32[]{:S(2)}, u32[]{:S(2)}) async-start(f32[8,32,512]{2,1,0:T(8,128)} %fusion.16), calls=%async_computation.2 | async-start | bytes 1048576 | tf_op jit(solution)/shard_map/all_to_all | solution.py:108
  30.7 0.5 broadcast.118
  31.2 1.3 %reduce.9 = s32[8,32]{1,0:T(8,128)S(1)} reduce(s32[8,32,1]{1,2,0:T(1,128)} %all-to-all-done.1, s32[]{:T(128)} %broadcast.118), dimensions={2}, to_apply=%all_to_all.22.reduce_sub_computation.3 | reduce | bytes 2052 | tf_op jit(solution)/shard_map/all_to_all | solution.py:109
  32.7 0.8 %pad_maximum_fusion = bf16[16,3072]{1,0:T(8,128)(2,1)S(1)} fusion(bf16[16,1024]{1,0:T(8,128)(2,1)} %collective-permute-done.1, bf16[16,1024]{1,0:T(8,128)(2,1)S(1)} %copy-done.2, bf16[16,1024]{1,0:T(8,128)(2,1)} %collective-permute-done), kind=kLoop, calls=%fused_computation.27 | loop fusion | flops 294912 | bytes 196608 | tf_op jit(solution)/shard_map/concatenate | solution.py:13
  33.5 6.4 %all_gather.3 = bf16[64,3072]{1,0:T(8,128)(2,1)S(1)} all-gather(bf16[16,3072]{1,0:T(8,128)(2,1)S(1)} %pad_maximum_fusion), channel_id=1, replica_groups=mesh['leaf'=8,'sub'=4] {'sub'}, dimensions={0}, use_global_device_ids=true | all-gather | bytes 491520 | tf_op jit(solution)/shard_map/all_gather | solution.py:76
  39.9 0.6 %gather_fusion = bf16[9,64,256]{2,1,0:T(8,128)(2,1)S(1)} fusion(bf16[64,12,256]{2,0,1:T(8,128)(2,1)S(1)} %bitcast.99, s32[1024]{0:T(1024)S(1)} %pad_clamp_fusion), kind=kCustom, calls=%fused_computation | custom fusion | bytes 589860 | tf_op jit(solution)/shard_map/jit(_take)/gather | solution.py:28
  40.5 2.3 %fusion.5 = bf16[64,256]{1,0:T(8,128)(2,1)} fusion(bf16[1,9,256,256]{3,2,1,0:T(8,128)(2,1)} %param.10, bf16[9,64,256]{2,1,0:T(8,128)(2,1)S(1)} %gather_fusion, pred[9]{0:T(512)(128)(4,1)S(1)} %compare_and_fusion, bf16[9]{0:T(256)(128)(2,1)S(1)} %convert_bitcast_fusion.1), kind=kOutput, calls=%fused_computation.6 | convolution fusion | flops 75808768 | bytes 1507355 | tf_op jit(solution)/shard_map/vjkp,jkpq->vjq/dot_general | solution.py:31
  42.8 1.3 %all-to-all-done.2 = f32[8,32,512]{2,1,0:T(8,128)S(1)} async-done(((f32[8,32,512]{2,1,0:T(8,128)}), f32[8,32,512]{2,1,0:T(8,128)S(1)}, u32[]{:S(2)}, u32[]{:S(2)}) %all-to-all-start.2) | async-done | bytes 524320 | tf_op jit(solution)/shard_map/all_to_all | solution.py:108
  44.1 3.3 %all-to-all-start = ((bf16[4,16,256]{2,1,0:T(8,128)(2,1)}), bf16[4,16,256]{2,1,0:T(8,128)(2,1)S(1)}, u32[]{:S(2)}, u32[]{:S(2)}) async-start(bf16[4,16,256]{2,1,0:T(8,128)(2,1)} %bitcast.10), calls=%async_computation | async-start | bytes 65536 | tf_op jit(solution)/shard_map/all_to_all | solution.py:78
  47.3 0.3 fusion.33
  47.9 0.9 %fusion.11 = f32[2,16,32,1]{2,1,3,0:T(8,128)S(1)} fusion(f32[2,16,32]{2,1,0:T(8,128)S(1)} %slice.41, f32[16,32,1]{1,0,2:T(8,128)S(1)} %reshape.181, bf16[6,32,32]{2,1,0:T(8,128)(2,1)} %param.14), kind=kOutput, calls=%fused_computation.11 | convolution fusion | flops 394240 | bytes 26624 | tf_op jit(solution)/shard_map/pvq,pcrq->pcvr/dot_general | solution.py:123
  48.8 0.3 fusion.39
  49.1 2.2 %all-to-all-done = bf16[4,16,256]{2,1,0:T(8,128)(2,1)S(1)} async-done(((bf16[4,16,256]{2,1,0:T(8,128)(2,1)}), bf16[4,16,256]{2,1,0:T(8,128)(2,1)S(1)}, u32[]{:S(2)}, u32[]{:S(2)}) %all-to-all-start) | async-done | bytes 32800 | tf_op jit(solution)/shard_map/all_to_all | solution.py:78
  51.4 0.6 %copy.27 = bf16[4,2,8,256]{3,2,0,1:T(8,128)(2,1)} copy(bf16[4,2,8,256]{3,2,1,0:T(8,128)(2,1)S(1)} %fusion.9) | data formatting | bytes 65536 | tf_op jit(solution)/shard_map/convert_element_type | solution.py:129
  (35 shorter events, 1.1 us)
Async XLA Ops:
  0.0 20.0 %copy-start = (bf16[7,27,32,32]{3,2,1,0:T(8,128)(2,1)S(1)}, bf16[7,27,32,32]{3,2,1,0:T(8,128)(2,1)}, u32[]{:S(2)}) copy-start(bf16[7,27,32,32]{3,2,1,0:T(8,128)(2,1)} %param.15) | copy-start | bytes 1161220
  0.0 32.7 %collective-permute-start.1 = (bf16[16,1024]{1,0:T(8,128)(2,1)}, bf16[16,1024]{1,0:T(8,128)(2,1)}, u32[]{:S(2)}, u32[]{:S(2)}) collective-permute-start(bf16[16,1024]{1,0:T(8,128)(2,1)} %param.9), channel_id=1, source_target_pairs={{4,0},{8,4},{12,8},{16,12},{20,16},{24,20},{28,24},{5,1},{9,5},{13... | collective-permute-start | bytes 98312 | tf_op jit(solution)/shard_map/ppermute | solution.py:17
  1.4 31.2 %collective-permute-start = (bf16[16,1024]{1,0:T(8,128)(2,1)}, bf16[16,1024]{1,0:T(8,128)(2,1)}, u32[]{:S(2)}, u32[]{:S(2)}) collective-permute-start(bf16[16,1024]{1,0:T(8,128)(2,1)} %param.9), channel_id=1, source_target_pairs={{0,4},{4,8},{8,12},{12,16},{16,20},{20,24},{24,28},{1,5},{5,9},{9,... | collective-permute-start | bytes 98312 | tf_op jit(solution)/shard_map/ppermute | solution.py:15
  9.3 10.7 %copy-start.3 = (s32[189]{0:T(256)}, s32[189]{0:T(256)S(1)}, u32[]{:S(2)}) copy-start(s32[189]{0:T(256)S(1)} %multiply_add_fusion.1) | copy-start | bytes 2272
  10.2 14.5 %all-to-all-start.1 = ((s32[8,32,1]{1,2,0:T(1,128)}), s32[8,32,1]{1,2,0:T(1,128)}, u32[]{:S(2)}, u32[]{:S(2)}) async-start(s32[8,32,1]{1,2,0:T(1,128)} %bitcast.14), calls=%async_computation.1 | async-start | bytes 8192 | tf_op jit(solution)/shard_map/all_to_all | solution.py:109
  20.8 11.8 %copy-start.2 = (bf16[16,1024]{1,0:T(8,128)(2,1)S(1)}, bf16[16,1024]{1,0:T(8,128)(2,1)}, u32[]{:S(2)}) copy-start(bf16[16,1024]{1,0:T(8,128)(2,1)} %param.9) | copy-start | bytes 98308
  21.4 9.2 %copy-start.4 = (s32[1,9]{1,0:T(1,128)S(1)}, s32[1,9]{1,0:T(1,128)}, u32[]{:S(2)}) copy-start(s32[1,9]{1,0:T(1,128)} %param.12) | copy-start | bytes 112
  24.7 19.4 %all-to-all-start.2 = ((f32[8,32,512]{2,1,0:T(8,128)}), f32[8,32,512]{2,1,0:T(8,128)S(1)}, u32[]{:S(2)}, u32[]{:S(2)}) async-start(f32[8,32,512]{2,1,0:T(8,128)} %fusion.16), calls=%async_computation.2 | async-start | bytes 1048576 | tf_op jit(solution)/shard_map/all_to_all | solution.py:108
  39.9 11.3 %copy-start.1 = (bf16[4,32,256]{2,1,0:T(8,128)(2,1)S(1)}, bf16[4,32,256]{2,1,0:T(8,128)(2,1)}, u32[]{:S(2)}) copy-start(bf16[4,32,256]{2,1,0:T(8,128)(2,1)} %param.13) | copy-start | bytes 196612
  44.1 7.2 %all-to-all-start = ((bf16[4,16,256]{2,1,0:T(8,128)(2,1)}), bf16[4,16,256]{2,1,0:T(8,128)(2,1)S(1)}, u32[]{:S(2)}, u32[]{:S(2)}) async-start(bf16[4,16,256]{2,1,0:T(8,128)(2,1)} %bitcast.10), calls=%async_computation | async-start | bytes 65536 | tf_op jit(solution)/shard_map/all_to_all | solution.py:78
where the time goes:
time: 52.9 us; the launch traced here: 52 us
  starting transfers between devices  22.4 us (42%)
  matrix products  8.67 us (16%)
  blocking collectives  6.44 us (12%)
  other arithmetic  6.36 us (12%)
  local copies, waits for them, and re-layouts  4.48 us (8%)
  waiting for transfers between devices  3.43 us (6%)
    all_gather x1, blocking collectives, local(): window = lax.all_gather(padded, 'sub', axis=0, tiled=True)  6.44 us
    ppermute x1, starting transfers between devices, with_halo(): lax.ppermute(tail, axis, [(i, (i + 1) % count) for i in range(ends)])  6.14 us
    all_to_all x1, starting transfers between devices, local(): lax.all_to_all(send_values, 'leaf', split_axis=0, concat_axis=0, tiled=True)  6 us
    all_to_all x1, starting transfers between devices, local(): lax.all_to_all(send_places, 'leaf', split_axis=0, concat_axis=0, tiled=True)  5.62 us
    all_to_all x1, starting transfers between devices, local(): lax.all_to_all(near_part.astype(jnp.bfloat16), 'sub', split_axis=0, conca...  3.26 us
    dot_general x1, matrix products, near_field(): jnp.einsum('vjkp,jkpq->vjq', taken, blocks, preferred_element_type=jnp.fl...  2.28 us
    all_to_all x1, waiting for transfers between devices, local(): lax.all_to_all(near_part.astype(jnp.bfloat16), 'sub', split_axis=0, conca...  2.17 us
    dot_general x1, matrix products, pack_slots(): send_values = jnp.dot(select.astype(jnp.float32), values, precision=highest)  1.9 us
  transfers between devices with their start and end apart: 5, of which 2 were waited for; matrix products, arithmetic and copies ran while one was open for 35% of the time, Pallas kernels for 0%

commit v1 on v0

v1 whole, which is shorter than its diff:
```python
import functools

import jax
import jax.numpy as jnp
from jax import lax
from jax.experimental import pallas as pl
from jax.experimental.pallas import tpu as pltpu
from jax.sharding import PartitionSpec as P

LANES = 128


def flip(values, axis, bit):
    count = lax.axis_size(axis)
    return lax.ppermute(values, axis, [(i, i ^ bit) for i in range(count)])


def beside(values, axis):
    count = lax.axis_size(axis)
    other = [((i + 1) ^ 1) - 1 for i in range(count)]
    return lax.ppermute(
        values, axis, [(i, j if 0 <= j < count else i) for i, j in enumerate(other)]
    )


def levels_of(subtree):
    sizes = []
    while subtree >= 1:
        sizes.append(subtree)
        subtree = subtree // 2
    starts = [sum(sizes[:number]) for number in range(len(sizes))]
    return sizes, starts


def split_dot(left, right, contract):
    high = left.astype(jnp.bfloat16)
    low = (left - high.astype(jnp.float32)).astype(jnp.bfloat16)
    dims = (contract, ((), ()))
    return lax.dot_general(
        high, right, dims, preferred_element_type=jnp.float32
    ) + lax.dot_general(low, right, dims, preferred_element_type=jnp.float32)


def expand_kernel(
    leaf_count, targets, alive, vectors, basis, transfer, coupling, keep, send, *sums
):
    subtree, rank, leaf_size = basis.shape
    clusters, far_count = coupling.shape[:2]
    nodes = leaf_count * clusters
    sizes, starts = levels_of(subtree)
    rows = vectors.shape[0]
    parity = lax.axis_index("leaf") % 2
    hats = []
    for j in range(subtree):
        hats.append(
            lax.dot_general(
                vectors[:, j * leaf_size : (j + 1) * leaf_size],
                basis[j],
                (((1,), (1,)), ((), ())),
                preferred_element_type=jnp.float32,
            )
        )
    for number in range(len(sizes) - 1):
        for p in range(sizes[number + 1]):
            c = starts[number] + 2 * p
            hats.append(
                split_dot(hats[c], transfer[c], ((1,), (0,)))
                + split_dot(hats[c + 1], transfer[c + 1], ((1,), (0,)))
            )
    shared = len(sums) < clusters
    zero = jnp.zeros((rows, rank), jnp.float32)
    if shared:

        def clear(row, carry):
            sums[0][row] = zero
            return carry

        lax.fori_loop(0, nodes, clear, 0)
    else:
        for number, size in enumerate(sizes):
            for c in range(starts[number], starts[number] + size):
                for tree in range(leaf_count):
                    for j in range(starts[number], starts[number] + size):
                        sums[c][tree * clusters + j] = zero
    lefts = [hat.astype(jnp.bfloat16) for hat in hats]
    for k in range(far_count):
        for c in range(clusters):
            term = jnp.dot(lefts[c], coupling[c, k], preferred_element_type=jnp.float32)
            row = jnp.where(alive[c, k] == 1, targets[c, k], nodes)
            held = sums[0 if shared else c]
            held[row] = held[row] + term
    per = LANES // rank

    def gathered(tree):
        groups = []
        for first in range(0, clusters, per):
            lanes = []
            for place in range(first, first + per):
                if place >= clusters:
                    lanes.append(zero)
                    continue
                number = max(n for n in range(len(sizes)) if starts[n] <= place)
                row = tree * clusters + place
                if shared:
                    lanes.append(sums[0][row])
                else:
                    level = range(starts[number], starts[number] + sizes[number])
                    lanes.append(sum(sums[c][row] for c in level))
            groups.append(jnp.concatenate(lanes, axis=1))
        return groups

    def emit(half, carry):
        for out, tree in ((keep, 2 * half + parity), (send, 2 * half + 1 - parity)):
            for number, group in enumerate(gathered(tree)):
                out[half, number] = group.astype(out.dtype)
        return carry

    if leaf_count <= 8:
        for half in range(leaf_count // 2):
            emit(half, 0)
    else:
        lax.fori_loop(0, leaf_count // 2, emit, 0)


def expand(vectors, basis, transfer, coupling, targets, alive):
    leaf_count = lax.axis_size("leaf")
    clusters, far_count, rank = coupling.shape[:3]
    rows = vectors.shape[0]
    nodes = leaf_count * clusters
    groups = -(-clusters * rank // LANES)
    shape = (leaf_count // 2, groups, rows, LANES)
    copies = clusters if nodes <= 128 else 1
    smem = pl.BlockSpec(memory_space=pltpu.SMEM)
    vmem = pl.BlockSpec(memory_space=pltpu.VMEM)
    return pl.pallas_call(
        functools.partial(expand_kernel, leaf_count),
        out_shape=[
            jax.ShapeDtypeStruct(shape, jnp.float32),
            jax.ShapeDtypeStruct(shape, jnp.bfloat16),
        ],
        in_specs=[smem, smem, vmem, vmem, vmem, vmem],
        out_specs=[vmem, vmem],
        scratch_shapes=[pltpu.VMEM((nodes + 1, rows, rank), jnp.float32)] * copies,
        name="expand",
    )(targets, alive, vectors, basis, transfer, coupling)


def near_kernel(
    sub_count, columns, alive, blocks, *refs
):
    pieces, (own, *outs), window = refs[: len(refs) - sub_count - 1], refs[-sub_count - 1 : -1], refs[-1]
    per_tree = len(pieces) // 3
    rows, points = pieces[0].shape
    count, leaf_size = blocks.shape[1:3]
    subtree = points // leaf_size
    for tree in range(3):
        for part in range(per_tree):
            window[tree, part * rows : (part + 1) * rows, :] = pieces[tree * per_tree + part][...]
    me = lax.axis_index("leaf")
    first = me * subtree
    partner = (me ^ 1) * subtree
    total = None
    for k in range(count):
        column = columns[0, k]
        own_tree = (column >= first) & (column < first + subtree)
        partner_tree = (column >= partner) & (column < partner + subtree)
        tree = jnp.where(own_tree, 0, jnp.where(partner_tree, 1, 2))
        place = lax.rem(column, subtree)
        start = pl.multiple_of(place * leaf_size, leaf_size)
        taken = window[tree, :, pl.ds(start, leaf_size)]
        live = alive[0, k].astype(jnp.float32).astype(jnp.bfloat16)
        product = jnp.dot(taken * live, blocks[0, k], preferred_element_type=jnp.float32)
        total = product if total is None else total + product
    size = total.shape[0] // sub_count
    for number, out in enumerate((own, *outs)):
        out[...] = total[number * size : (number + 1) * size].astype(out.dtype)


def near(pieces, blocks, columns, alive, rows):
    sub_count = lax.axis_size("sub")
    leaf_size = blocks.shape[2]
    smem = pl.BlockSpec(memory_space=pltpu.SMEM)
    vmem = pl.BlockSpec(memory_space=pltpu.VMEM)
    points = pieces[0].shape[1]
    return pl.pallas_call(
        functools.partial(near_kernel, sub_count),
        out_shape=[jax.ShapeDtypeStruct((rows, leaf_size), jnp.float32)]
        + [jax.ShapeDtypeStruct((rows, leaf_size), jnp.bfloat16)] * (sub_count - 1),
        in_specs=[smem, smem] + [vmem] * (1 + len(pieces)),
        out_specs=[vmem] * sub_count,
        scratch_shapes=[pltpu.VMEM((3, rows * sub_count, points), jnp.bfloat16)],
        name="near",
    )(columns, alive, blocks, *pieces)


def finish_kernel(keep, got, transfer, basis, *refs):
    subtree, rank, leaf_size = basis.shape
    nears, out = refs[:-1], refs[-1]
    sizes, starts = levels_of(subtree)
    clusters = sum(sizes)
    per = LANES // rank
    incoming = [keep[0, g] + got[0, g].astype(jnp.float32) for g in range(keep.shape[1])]
    down = [
        incoming[c // per][:, (c % per) * rank : (c % per + 1) * rank] for c in range(clusters)
    ]
    for number in range(len(sizes) - 2, -1, -1):
        for j in range(sizes[number]):
            c = starts[number] + j
            parent = starts[number + 1] + j // 2
            down[c] = down[c] + split_dot(down[parent], transfer[c], ((1,), (1,)))
    me = lax.axis_index("sub")
    for j in range(subtree):
        columns = slice(j * leaf_size, (j + 1) * leaf_size)
        out[:, columns] = jnp.zeros((out.shape[0], leaf_size), out.dtype)
    far = [split_dot(down[j], basis[j], ((1,), (0,))) for j in range(subtree)]
    for j in range(subtree):
        piece = nears[0][...]
        for other in range(1, subtree):
            piece = jnp.where((me ^ other) == j, nears[other][...].astype(jnp.float32), piece)
        out[:, j * leaf_size : (j + 1) * leaf_size] = (piece + far[j]).astype(out.dtype)


def finish(keep, got, transfer, basis, nears):
    rows = nears[0].shape[0]
    subtree, _, leaf_size = basis.shape
    vmem = pl.BlockSpec(memory_space=pltpu.VMEM)
    return pl.pallas_call(
        finish_kernel,
        out_shape=jax.ShapeDtypeStruct((rows, subtree * leaf_size), jnp.bfloat16),
        in_specs=[vmem] * (4 + len(nears)),
        out_specs=vmem,
        name="finish",
    )(keep, got, transfer, basis, *nears)


def local(
    vectors,
    near_blocks,
    near_cols,
    near_mask,
    leaf_basis,
    transfer,
    coupling,
    far_targets,
    far_mask,
):
    leaf_count = lax.axis_size("leaf")
    sub_count = lax.axis_size("sub")
    me = lax.axis_index("leaf")
    rows = vectors.shape[0]
    half = sub_count // 2
    pair = jnp.concatenate([vectors, flip(vectors, "sub", half)], axis=0)
    keep, send = expand(vectors, leaf_basis, transfer, coupling, far_targets, far_mask)
    got = flip(send, "leaf", 1)
    trees = [[pair], [flip(pair, "leaf", 1)], [beside(pair, "leaf")]]
    order = [0, half]
    bit = half // 2
    while bit >= 1:
        trees = [parts + [flip(part, "sub", bit) for part in parts] for parts in trees]
        order = order + [number ^ bit for number in order]
        bit = bit // 2
    pieces = [part for parts in trees for part in parts]
    size = leaf_count // 2
    while size > 1:
        total = (keep + got.astype(keep.dtype)).reshape(2, size // 2, *keep.shape[1:])
        mine = (me // size) % 2
        keep = lax.dynamic_index_in_dim(total, mine, 0, keepdims=False)
        send = lax.dynamic_index_in_dim(total, 1 - mine, 0, keepdims=False)
        got = flip(send.astype(jnp.bfloat16), "leaf", size)
        size = size // 2
    made = near(pieces, near_blocks, near_cols, near_mask, rows)
    nears = [None] * sub_count
    for number, away in zip(order, made):
        nears[number] = away if number == 0 else flip(away, "sub", number)
    return finish(keep, got, transfer, leaf_basis, nears)


def solution(mesh):
    return jax.shard_map(
        local,
        mesh=mesh,
        in_specs=(
            P("sub", "leaf"),
            P(("leaf", "sub"), None, None, None),
            P(("leaf", "sub"), None),
            P(("leaf", "sub"), None),
            P("leaf", None, None),
            P("leaf", None, None),
            P("leaf", None, None, None),
            P("leaf", None),
            P("leaf", None),
        ),
        out_specs=P("sub", "leaf"),
        check_vma=False,
    )
```

time: 52.9 us -> 34.1 us (0.64); the launches traced: 52 us -> 33.8 us
  matrix products: 8.67 us -> 0 us
  Pallas kernels: 0 us -> 7.81 us
  blocking collectives: 6.44 us -> 0 us
  starting transfers between devices: 22.4 us -> 16.7 us
  other arithmetic: 6.36 us -> 0.85 us
  waiting for transfers between devices: 3.43 us -> 5.86 us
  local copies, waits for them, and re-layouts: 4.48 us -> 2.44 us
    all_to_all x3 -> x0, starting transfers between devices: 14.9 us -> none  [the longest x1 6 us: local(): lax.all_to_all(send_values, 'leaf', split_axis=0, concat_axis=0, tiled=True)]
    ppermute x2 -> x12, starting transfers between devices: 7.55 us -> 16.7 us  [the longest x11 16.1 us: flip(): return lax.ppermute(values, axis, [(i, i ^ bit) for i in range(count)])]
    dot_general x10 -> x0, matrix products: 8.67 us -> none  [the longest x1 2.28 us: near_field(): jnp.einsum('vjkp,jkpq->vjq', taken, blocks, preferred_element_type=jnp.fl...]
    pallas_call x0 -> x3, Pallas kernels: none -> 7.81 us  [the longest x1 3.22 us: expand(): pl.pallas_call(functools.partial(expand_kernel, leaf_count), out_shape=[j...]
    all_gather x1 -> x0, blocking collectives: 6.44 us -> none  [local(): window = lax.all_gather(padded, 'sub', axis=0, tiled=True)]
    ppermute x2 -> x12, waiting for transfers between devices: 0.01 us -> 5.86 us  [the longest x11 5.85 us: flip(): return lax.ppermute(values, axis, [(i, i ^ bit) for i in range(count)])]
    all_to_all x3 -> x0, waiting for transfers between devices: 3.42 us -> none  [the longest x1 2.17 us: local(): lax.all_to_all(near_part.astype(jnp.bfloat16), 'sub', split_axis=0, conca...]
    unnamed x10 -> x23, local copies, waits for them, and re-layouts: 0.03 us -> 1.83 us
  transfers between devices with their start and end apart: 5 -> 12, of which waited for: 2 -> 3; matrix products, arithmetic and copies ran while one was open for 35% -> 4% of each run, Pallas kernels for 0% -> 17%
where the time goes in v1:
time: 34.1 us; the launch traced here: 33.8 us
  starting transfers between devices  16.7 us (49%)
  Pallas kernels  7.81 us (23%)
  waiting for transfers between devices  5.86 us (17%)
  local copies, waits for them, and re-layouts  2.44 us (7%)
  other arithmetic  0.85 us (2%)
    ppermute x11, starting transfers between devices, flip(): return lax.ppermute(values, axis, [(i, i ^ bit) for i in range(count)])  16.1 us
    ppermute x11, waiting for transfers between devices, flip(): return lax.ppermute(values, axis, [(i, i ^ bit) for i in range(count)])  5.85 us
    pallas_call x1, Pallas kernels, expand(): pl.pallas_call(functools.partial(expand_kernel, leaf_count), out_shape=[j...  3.22 us
    pallas_call x1, Pallas kernels, near(): pl.pallas_call(functools.partial(near_kernel, sub_count), out_shape=[jax....  2.36 us
    pallas_call x1, Pallas kernels, finish(): pl.pallas_call(finish_kernel, out_shape=jax.ShapeDtypeStruct((rows, subtr...  2.24 us
    unnamed x23, local copies, waits for them, and re-layouts  1.83 us
    add x2, other arithmetic, local(): keep + got.astype(keep.dtype)  0.85 us
  transfers between devices with their start and end apart: 12, of which 3 were waited for; matrix products, arithmetic and copies ran while one was open for 4% of the time, Pallas kernels for 17%

profile of v1, /device:TPU:0, one launch (start us, length us, event | category | flops | bytes accessed | tf_op | source)
XLA Modules:
  0.0 33.8 jit_solution(9540071642738844189)
XLA Ops:
  0.0 3.0 %collective-permute-start.3 = (bf16[16,1024]{1,0:T(8,128)(2,1)}, bf16[16,1024]{1,0:T(8,128)(2,1)S(1)}, u32[]{:S(2)}, u32[]{:S(2)}) collective-permute-start(bf16[16,1024]{1,0:T(8,128)(2,1)} %vectors.1), channel_id=1, source_target_pairs={{0,2},{1,3},{2,0},{3,1},{4,6},{5,7},{6,4},{7,5},{8,10},{9,11},{10,... | collective-permute-start | bytes 98312 | tf_op jit(solution)/shard_map/ppermute | solution.py:15
  3.0 3.2 %expand.1 = (f32[4,2,16,128]{3,2,1,0:T(8,128)}, bf16[4,2,16,128]{3,2,1,0:T(8,128)(2,1)}) custom-call(s32[7,27]{1,0:T(8,128)} %targets.1, s32[7,27]{1,0:T(8,128)} %alive.2, bf16[16,1024]{1,0:T(8,128)(2,1)} %vectors.1, bf16[4,32,256]{2,1,0:T(8,128)(2,1)} %basis.3, bf16[6,32,32]{2,1,0:T(8,128)(2,1)} %transfer.3, bf16[7,27,32,32]{3,2,1,0:T(8,128)(2,1)} %coupling.1), custom_call_target="tpu_custom_call" | custom-call | tf_op jit(solution)/shard_map/expand/pallas_call | solution.py:135
  6.2 1.5 %collective-permute-start = (bf16[4,2,16,128]{3,2,1,0:T(8,128)(2,1)}, bf16[4,2,16,128]{3,2,1,0:T(8,128)(2,1)S(1)}, u32[]{:S(2)}, u32[]{:S(2)}) collective-permute-start(bf16[4,2,16,128]{3,2,1,0:T(8,128)(2,1)} %get-tuple-element.12), channel_id=1, source_target_pairs={{0,4},{4,0},{8,12},{12,8},{16,20},{20,16},{24,28},{28,24},{1,5},{5... | collective-permute-start | bytes 98312 | tf_op jit(solution)/shard_map/ppermute | solution.py:15
  7.7 2.6 %collective-permute-done = bf16[4,2,16,128]{3,2,1,0:T(8,128)(2,1)S(1)} collective-permute-done((bf16[4,2,16,128]{3,2,1,0:T(8,128)(2,1)}, bf16[4,2,16,128]{3,2,1,0:T(8,128)(2,1)S(1)}, u32[]{:S(2)}, u32[]{:S(2)}) %collective-permute-start) | collective-permute-done | bytes 32800 | tf_op jit(solution)/shard_map/ppermute | solution.py:15
  10.3 0.8 %convert_add_fusion = f32[4,2,16,128]{3,2,1,0:T(8,128)S(1)} fusion(f32[4,2,16,128]{3,2,1,0:T(8,128)} %get-tuple-element.11, bf16[4,2,16,128]{3,2,1,0:T(8,128)(2,1)S(1)} %collective-permute-done), kind=kLoop, calls=%fused_computation | loop fusion | flops 32768 | bytes 163840 | tf_op jit(solution)/shard_map/add | solution.py:265
  11.2 2.7 %collective-permute-start.1 = (bf16[2,2,16,128]{3,2,1,0:T(8,128)(2,1)S(1)}, bf16[2,2,16,128]{3,2,1,0:T(8,128)(2,1)S(1)}, u32[]{:S(2)}, u32[]{:S(2)}) collective-permute-start(bf16[2,2,16,128]{3,2,1,0:T(8,128)(2,1)S(1)} %fusion), channel_id=1, source_target_pairs={{0,16},{4,20},{8,24},{12,28},{16,0},{20,4},{24,8},{28,12},{1,17},{... | collective-permute-start | bytes 49160 | tf_op jit(solution)/shard_map/ppermute | solution.py:15
  13.8 0.0 collective-permute-done.3
  13.8 0.7 %collective-permute-start.7 = (bf16[32,1024]{1,0:T(8,128)(2,1)S(1)}, bf16[32,1024]{1,0:T(8,128)(2,1)S(1)}, u32[]{:S(2)}, u32[]{:S(2)}) collective-permute-start(bf16[32,1024]{1,0:T(8,128)(2,1)S(1)} %constant_dynamic-update-slice_fusion.refs_0_), channel_id=1, source_target_pairs={{0,0},{4,8},{8,4},{12,16},{16,12},{20,24},{24,20},{28,28},{1,1},{5... | collective-permute-start | bytes 196616 | tf_op jit(solution)/shard_map/ppermute | solution.py:21
  14.5 4.3 %collective-permute-start.5 = (bf16[32,1024]{1,0:T(8,128)(2,1)S(1)}, bf16[32,1024]{1,0:T(8,128)(2,1)S(1)}, u32[]{:S(2)}, u32[]{:S(2)}) collective-permute-start(bf16[32,1024]{1,0:T(8,128)(2,1)S(1)} %constant_dynamic-update-slice_fusion.refs_0_), channel_id=1, source_target_pairs={{0,4},{4,0},{8,12},{12,8},{16,20},{20,16},{24,28},{28,24},{1,5},{5... | collective-permute-start | bytes 196616 | tf_op jit(solution)/shard_map/ppermute | solution.py:15
  18.9 0.0 collective-permute-start.4
  18.9 0.0 collective-permute-done.1
  18.9 0.0 collective-permute-done.7.refs_4_
  18.9 0.6 %collective-permute-start.8 = (bf16[32,1024]{1,0:T(8,128)(2,1)S(1)}, bf16[32,1024]{1,0:T(8,128)(2,1)S(1)}, u32[]{:S(2)}, u32[]{:S(2)}) collective-permute-start(bf16[32,1024]{1,0:T(8,128)(2,1)S(1)} %collective-permute-done.7.refs_4_), channel_id=1, source_target_pairs={{0,1},{1,0},{2,3},{3,2},{4,5},{5,4},{6,7},{7,6},{8,9},{9,8},{10,11... | collective-permute-start | bytes 196616 | tf_op jit(solution)/shard_map/ppermute | solution.py:15
  19.5 1.6 %collective-permute-done.5.refs_2_ = bf16[32,1024]{1,0:T(8,128)(2,1)S(1)} collective-permute-done((bf16[32,1024]{1,0:T(8,128)(2,1)S(1)}, bf16[32,1024]{1,0:T(8,128)(2,1)S(1)}, u32[]{:S(2)}, u32[]{:S(2)}) %collective-permute-start.5) | collective-permute-done | bytes 65568 | tf_op jit(solution)/shard_map/ppermute | solution.py:15
  21.1 0.0 collective-permute-start.6
  21.1 2.1 %collective-permute-start.2 = (bf16[1,2,16,128]{3,2,1,0:T(8,128)(2,1)S(1)}, bf16[1,2,16,128]{3,2,1,0:T(8,128)(2,1)S(1)}, u32[]{:S(2)}, u32[]{:S(2)}) collective-permute-start(bf16[1,2,16,128]{3,2,1,0:T(8,128)(2,1)S(1)} %dynamic-slice_convert_fusion.1), channel_id=1, source_target_pairs={{0,8},{4,12},{8,0},{12,4},{16,24},{20,28},{24,16},{28,20},{1,9},{5... | collective-permute-start | bytes 24584 | tf_op jit(solution)/shard_map/ppermute | solution.py:15
  23.3 0.0 collective-permute-done.4.refs_1_
  23.3 0.0 collective-permute-done.8.refs_5_
  23.3 0.0 collective-permute-done.6.refs_3_
  23.3 0.6 %copy-done.4 = bf16[32,1024]{1,0:T(8,128)(2,1)} copy-done((bf16[32,1024]{1,0:T(8,128)(2,1)}, bf16[32,1024]{1,0:T(8,128)(2,1)S(1)}, u32[]{:S(2)}) %copy-start.4) | copy-done | bytes 65560
  23.9 0.0 copy-done.5
  23.9 0.6 %copy-done.6 = bf16[32,1024]{1,0:T(8,128)(2,1)} copy-done((bf16[32,1024]{1,0:T(8,128)(2,1)}, bf16[32,1024]{1,0:T(8,128)(2,1)S(1)}, u32[]{:S(2)}) %copy-start.6) | copy-done | bytes 65560
  24.5 2.4 %near.1 = (f32[16,256]{1,0:T(8,128)}, bf16[16,256]{1,0:T(8,128)(2,1)}, bf16[16,256]{1,0:T(8,128)(2,1)}, bf16[16,256]{1,0:T(8,128)(2,1)}) custom-call(s32[1,9]{1,0:T(1,128)} %columns.1, s32[1,9]{1,0:T(1,128)} %alive.3, bf16[1,9,256,256]{3,2,1,0:T(8,128)(2,1)} %blocks.1, bf16[32,1024]{1,0:T(8,128)(2,1)} %copy-done, bf16[32,1024]{1,0:T(8,128)(2,1)} %copy-done.4, ...), custom_call_target="tpu_custom_call" | custom-call | tf_op jit(solution)/shard_map/near/pallas_call | solution.py:185
  26.9 0.2 collective-permute-start.9
  27.1 0.5 %collective-permute-start.10 = (bf16[16,256]{1,0:T(8,128)(2,1)}, bf16[16,256]{1,0:T(8,128)(2,1)S(1)}, u32[]{:S(2)}, u32[]{:S(2)}) collective-permute-start(bf16[16,256]{1,0:T(8,128)(2,1)} %get-tuple-element.15), channel_id=1, source_target_pairs={{0,2},{1,3},{2,0},{3,1},{4,6},{5,7},{6,4},{7,5},{8,10},{9,11},{10,... | collective-permute-start | bytes 24584 | tf_op jit(solution)/shard_map/ppermute | solution.py:15
  27.6 1.2 %collective-permute-start.11 = (bf16[16,256]{1,0:T(8,128)(2,1)}, bf16[16,256]{1,0:T(8,128)(2,1)S(1)}, u32[]{:S(2)}, u32[]{:S(2)}) collective-permute-start(bf16[16,256]{1,0:T(8,128)(2,1)} %get-tuple-element.16), channel_id=1, source_target_pairs={{0,3},{1,2},{2,1},{3,0},{4,7},{5,6},{6,5},{7,4},{8,11},{9,10},{10,... | collective-permute-start | bytes 24584 | tf_op jit(solution)/shard_map/ppermute | solution.py:15
  28.8 0.6 %constant_dynamic-slice_fusion.keep = f32[1,2,16,128]{3,2,1,0:T(8,128)} fusion(f32[2,2,16,128]{3,2,1,0:T(8,128)S(1)} %bitcast_add_fusion, s32[]{:T(128)S(6)} %select_n.38), kind=kLoop, calls=%fused_computation.7 | loop fusion | bytes 32772 | tf_op jit(solution)/shard_map/jit(dynamic_index_in_dim)/squeeze | solution.py:267
  29.4 1.6 %collective-permute-done.10.refs_2_ = bf16[16,256]{1,0:T(8,128)(2,1)S(1)} collective-permute-done((bf16[16,256]{1,0:T(8,128)(2,1)}, bf16[16,256]{1,0:T(8,128)(2,1)S(1)}, u32[]{:S(2)}, u32[]{:S(2)}) %collective-permute-start.10) | collective-permute-done | bytes 8224 | tf_op jit(solution)/shard_map/ppermute | solution.py:15
  31.0 0.0 collective-permute-done.11.refs_3_
  31.0 0.6 %copy-done.9 = bf16[16,256]{1,0:T(8,128)(2,1)} copy-done((bf16[16,256]{1,0:T(8,128)(2,1)}, bf16[16,256]{1,0:T(8,128)(2,1)S(1)}, u32[]{:S(2)}) %copy-start.9) | copy-done | bytes 8216
  31.6 0.0 copy-done.10
  31.6 2.2 %finish.1 = bf16[16,1024]{1,0:T(8,128)(2,1)} custom-call(f32[1,2,16,128]{3,2,1,0:T(8,128)} %constant_dynamic-slice_fusion.keep, bf16[1,2,16,128]{3,2,1,0:T(8,128)(2,1)} %copy-done.7, bf16[6,32,32]{2,1,0:T(8,128)(2,1)} %transfer.3, bf16[4,32,256]{2,1,0:T(8,128)(2,1)} %basis.3, f32[16,256]{1,0:T(8,128)} %get-tuple-element.13.refs_0_, ...), custom_call_target="tpu_custom_call" | custom-call | tf_op jit(solution)/shard_map/finish/pallas_call | solution.py:227
  (24 shorter events, 0.1 us)
Async XLA Ops:
  0.0 7.7 %copy-start.1 = (bf16[16,1024]{1,0:T(8,128)(2,1)S(1)}, bf16[16,1024]{1,0:T(8,128)(2,1)}, u32[]{:S(2)}) copy-start(bf16[16,1024]{1,0:T(8,128)(2,1)} %vectors.1) | copy-start | bytes 98308
  0.0 13.8 %collective-permute-start.3 = (bf16[16,1024]{1,0:T(8,128)(2,1)}, bf16[16,1024]{1,0:T(8,128)(2,1)S(1)}, u32[]{:S(2)}, u32[]{:S(2)}) collective-permute-start(bf16[16,1024]{1,0:T(8,128)(2,1)} %vectors.1), channel_id=1, source_target_pairs={{0,2},{1,3},{2,0},{3,1},{4,6},{5,7},{6,4},{7,5},{8,10},{9,11},{10,... | collective-permute-start | bytes 98312 | tf_op jit(solution)/shard_map/ppermute | solution.py:15
  6.2 4.1 %collective-permute-start = (bf16[4,2,16,128]{3,2,1,0:T(8,128)(2,1)}, bf16[4,2,16,128]{3,2,1,0:T(8,128)(2,1)S(1)}, u32[]{:S(2)}, u32[]{:S(2)}) collective-permute-start(bf16[4,2,16,128]{3,2,1,0:T(8,128)(2,1)} %get-tuple-element.12), channel_id=1, source_target_pairs={{0,4},{4,0},{8,12},{12,8},{16,20},{20,16},{24,28},{28,24},{1,5},{5... | collective-permute-start | bytes 98312 | tf_op jit(solution)/shard_map/ppermute | solution.py:15
  11.2 7.7 %collective-permute-start.1 = (bf16[2,2,16,128]{3,2,1,0:T(8,128)(2,1)S(1)}, bf16[2,2,16,128]{3,2,1,0:T(8,128)(2,1)S(1)}, u32[]{:S(2)}, u32[]{:S(2)}) collective-permute-start(bf16[2,2,16,128]{3,2,1,0:T(8,128)(2,1)S(1)} %fusion), channel_id=1, source_target_pairs={{0,16},{4,20},{8,24},{12,28},{16,0},{20,4},{24,8},{28,12},{1,17},{... | collective-permute-start | bytes 49160 | tf_op jit(solution)/shard_map/ppermute | solution.py:15
  13.8 9.4 %copy-start = (bf16[32,1024]{1,0:T(8,128)(2,1)}, bf16[32,1024]{1,0:T(8,128)(2,1)S(1)}, u32[]{:S(2)}) copy-start(bf16[32,1024]{1,0:T(8,128)(2,1)S(1)} %constant_dynamic-update-slice_fusion.refs_0_) | copy-start | bytes 196612
  13.8 5.0 %collective-permute-start.7 = (bf16[32,1024]{1,0:T(8,128)(2,1)S(1)}, bf16[32,1024]{1,0:T(8,128)(2,1)S(1)}, u32[]{:S(2)}, u32[]{:S(2)}) collective-permute-start(bf16[32,1024]{1,0:T(8,128)(2,1)S(1)} %constant_dynamic-update-slice_fusion.refs_0_), channel_id=1, source_target_pairs={{0,0},{4,8},{8,4},{12,16},{16,12},{20,24},{24,20},{28,28},{1,1},{5... | collective-permute-start | bytes 196616 | tf_op jit(solution)/shard_map/ppermute | solution.py:21
  14.5 6.6 %collective-permute-start.5 = (bf16[32,1024]{1,0:T(8,128)(2,1)S(1)}, bf16[32,1024]{1,0:T(8,128)(2,1)S(1)}, u32[]{:S(2)}, u32[]{:S(2)}) collective-permute-start(bf16[32,1024]{1,0:T(8,128)(2,1)S(1)} %constant_dynamic-update-slice_fusion.refs_0_), channel_id=1, source_target_pairs={{0,4},{4,0},{8,12},{12,8},{16,20},{20,16},{24,28},{28,24},{1,5},{5... | collective-permute-start | bytes 196616 | tf_op jit(solution)/shard_map/ppermute | solution.py:15
  18.9 4.4 %collective-permute-start.4 = (bf16[32,1024]{1,0:T(8,128)(2,1)S(1)}, bf16[32,1024]{1,0:T(8,128)(2,1)S(1)}, u32[]{:S(2)}, u32[]{:S(2)}) collective-permute-start(bf16[32,1024]{1,0:T(8,128)(2,1)S(1)} %constant_dynamic-update-slice_fusion.refs_0_), channel_id=1, source_target_pairs={{0,1},{1,0},{2,3},{3,2},{4,5},{5,4},{6,7},{7,6},{8,9},{9,8},{10,11... | collective-permute-start | bytes 196616 | tf_op jit(solution)/shard_map/ppermute | solution.py:15
  18.9 4.4 %copy-start.2 = (bf16[32,1024]{1,0:T(8,128)(2,1)}, bf16[32,1024]{1,0:T(8,128)(2,1)S(1)}, u32[]{:S(2)}) copy-start(bf16[32,1024]{1,0:T(8,128)(2,1)S(1)} %collective-permute-done.7.refs_4_) | copy-start | bytes 196612
  18.9 4.4 %collective-permute-start.8 = (bf16[32,1024]{1,0:T(8,128)(2,1)S(1)}, bf16[32,1024]{1,0:T(8,128)(2,1)S(1)}, u32[]{:S(2)}, u32[]{:S(2)}) collective-permute-start(bf16[32,1024]{1,0:T(8,128)(2,1)S(1)} %collective-permute-done.7.refs_4_), channel_id=1, source_target_pairs={{0,1},{1,0},{2,3},{3,2},{4,5},{5,4},{6,7},{7,6},{8,9},{9,8},{10,11... | collective-permute-start | bytes 196616 | tf_op jit(solution)/shard_map/ppermute | solution.py:15
  21.1 2.2 %copy-start.3 = (bf16[32,1024]{1,0:T(8,128)(2,1)}, bf16[32,1024]{1,0:T(8,128)(2,1)S(1)}, u32[]{:S(2)}) copy-start(bf16[32,1024]{1,0:T(8,128)(2,1)S(1)} %collective-permute-done.5.refs_2_) | copy-start | bytes 196612
  21.1 2.2 %collective-permute-start.6 = (bf16[32,1024]{1,0:T(8,128)(2,1)S(1)}, bf16[32,1024]{1,0:T(8,128)(2,1)S(1)}, u32[]{:S(2)}, u32[]{:S(2)}) collective-permute-start(bf16[32,1024]{1,0:T(8,128)(2,1)S(1)} %collective-permute-done.5.refs_2_), channel_id=1, source_target_pairs={{0,1},{1,0},{2,3},{3,2},{4,5},{5,4},{6,7},{7,6},{8,9},{9,8},{10,11... | collective-permute-start | bytes 196616 | tf_op jit(solution)/shard_map/ppermute | solution.py:15
  21.1 8.2 %collective-permute-start.2 = (bf16[1,2,16,128]{3,2,1,0:T(8,128)(2,1)S(1)}, bf16[1,2,16,128]{3,2,1,0:T(8,128)(2,1)S(1)}, u32[]{:S(2)}, u32[]{:S(2)}) collective-permute-start(bf16[1,2,16,128]{3,2,1,0:T(8,128)(2,1)S(1)} %dynamic-slice_convert_fusion.1), channel_id=1, source_target_pairs={{0,8},{4,12},{8,0},{12,4},{16,24},{20,28},{24,16},{28,20},{1,9},{5... | collective-permute-start | bytes 24584 | tf_op jit(solution)/shard_map/ppermute | solution.py:15
  23.3 0.6 %copy-start.4 = (bf16[32,1024]{1,0:T(8,128)(2,1)}, bf16[32,1024]{1,0:T(8,128)(2,1)S(1)}, u32[]{:S(2)}) copy-start(bf16[32,1024]{1,0:T(8,128)(2,1)S(1)} %collective-permute-done.4.refs_1_) | copy-start | bytes 196612
  23.3 0.6 %copy-start.5 = (bf16[32,1024]{1,0:T(8,128)(2,1)}, bf16[32,1024]{1,0:T(8,128)(2,1)S(1)}, u32[]{:S(2)}) copy-start(bf16[32,1024]{1,0:T(8,128)(2,1)S(1)} %collective-permute-done.8.refs_5_) | copy-start | bytes 196612
  23.9 0.6 %copy-start.6 = (bf16[32,1024]{1,0:T(8,128)(2,1)}, bf16[32,1024]{1,0:T(8,128)(2,1)S(1)}, u32[]{:S(2)}) copy-start(bf16[32,1024]{1,0:T(8,128)(2,1)S(1)} %collective-permute-done.6.refs_3_) | copy-start | bytes 196612
  26.9 2.5 %collective-permute-start.9 = (bf16[16,256]{1,0:T(8,128)(2,1)}, bf16[16,256]{1,0:T(8,128)(2,1)S(1)}, u32[]{:S(2)}, u32[]{:S(2)}) collective-permute-start(bf16[16,256]{1,0:T(8,128)(2,1)} %get-tuple-element.14), channel_id=1, source_target_pairs={{0,1},{1,0},{2,3},{3,2},{4,5},{5,4},{6,7},{7,6},{8,9},{9,8},{10,11... | collective-permute-start | bytes 24584 | tf_op jit(solution)/shard_map/ppermute | solution.py:15
  27.1 3.9 %collective-permute-start.10 = (bf16[16,256]{1,0:T(8,128)(2,1)}, bf16[16,256]{1,0:T(8,128)(2,1)S(1)}, u32[]{:S(2)}, u32[]{:S(2)}) collective-permute-start(bf16[16,256]{1,0:T(8,128)(2,1)} %get-tuple-element.15), channel_id=1, source_target_pairs={{0,2},{1,3},{2,0},{3,1},{4,6},{5,7},{6,4},{7,5},{8,10},{9,11},{10,... | collective-permute-start | bytes 24584 | tf_op jit(solution)/shard_map/ppermute | solution.py:15
  27.6 3.4 %collective-permute-start.11 = (bf16[16,256]{1,0:T(8,128)(2,1)}, bf16[16,256]{1,0:T(8,128)(2,1)S(1)}, u32[]{:S(2)}, u32[]{:S(2)}) collective-permute-start(bf16[16,256]{1,0:T(8,128)(2,1)} %get-tuple-element.16), channel_id=1, source_target_pairs={{0,3},{1,2},{2,1},{3,0},{4,7},{5,6},{6,5},{7,4},{8,11},{9,10},{10,... | collective-permute-start | bytes 24584 | tf_op jit(solution)/shard_map/ppermute | solution.py:15
  29.4 1.6 %copy-start.7 = (bf16[1,2,16,128]{3,2,1,0:T(8,128)(2,1)}, bf16[1,2,16,128]{3,2,1,0:T(8,128)(2,1)S(1)}, u32[]{:S(2)}) copy-start(bf16[1,2,16,128]{3,2,1,0:T(8,128)(2,1)S(1)} %collective-permute-done.2.got) | copy-start | bytes 24580
  29.4 1.6 %copy-start.8 = (bf16[16,256]{1,0:T(8,128)(2,1)}, bf16[16,256]{1,0:T(8,128)(2,1)S(1)}, u32[]{:S(2)}) copy-start(bf16[16,256]{1,0:T(8,128)(2,1)S(1)} %collective-permute-done.9.refs_1_) | copy-start | bytes 24580
  31.0 0.6 %copy-start.9 = (bf16[16,256]{1,0:T(8,128)(2,1)}, bf16[16,256]{1,0:T(8,128)(2,1)S(1)}, u32[]{:S(2)}) copy-start(bf16[16,256]{1,0:T(8,128)(2,1)S(1)} %collective-permute-done.10.refs_2_) | copy-start | bytes 24580
  31.0 0.6 %copy-start.10 = (bf16[16,256]{1,0:T(8,128)(2,1)}, bf16[16,256]{1,0:T(8,128)(2,1)S(1)}, u32[]{:S(2)}) copy-start(bf16[16,256]{1,0:T(8,128)(2,1)S(1)} %collective-permute-done.11.refs_3_) | copy-start | bytes 24580

commit v2 on v1

--- a/solution.py
+++ b/solution.py
@@ -8,6 +8,7 @@
 from jax.sharding import PartitionSpec as P
 
 LANES = 128
+PARAMS = pltpu.CompilerParams(vmem_limit_bytes=16 * 2**20)
 
 
 def flip(values, axis, bit):
@@ -141,6 +142,7 @@
         in_specs=[smem, smem, vmem, vmem, vmem, vmem],
         out_specs=[vmem, vmem],
         scratch_shapes=[pltpu.VMEM((nodes + 1, rows, rank), jnp.float32)] * copies,
+        compiler_params=PARAMS,
         name="expand",
     )(targets, alive, vectors, basis, transfer, coupling)
 
@@ -189,6 +191,7 @@
         in_specs=[smem, smem] + [vmem] * (1 + len(pieces)),
         out_specs=[vmem] * sub_count,
         scratch_shapes=[pltpu.VMEM((3, rows * sub_count, points), jnp.bfloat16)],
+        compiler_params=PARAMS,
         name="near",
     )(columns, alive, blocks, *pieces)
 
@@ -229,6 +232,7 @@
         out_shape=jax.ShapeDtypeStruct((rows, subtree * leaf_size), jnp.bfloat16),
         in_specs=[vmem] * (4 + len(nears)),
         out_specs=vmem,
+        compiler_params=PARAMS,
         name="finish",
     )(keep, got, transfer, basis, *nears)
 

time: 34.1 us -> 32.6 us (0.956)
  Pallas kernels: 7.81 us -> 3.99 us
  local copies, waits for them, and re-layouts: 2.44 us -> 5.21 us
  other arithmetic: 0.85 us -> 0.01 us
    unnamed x23, local copies, waits for them, and re-layouts: 1.83 us -> 5.19 us
    pallas_call x1, Pallas kernels: 3.22 us -> 1.74 us  [expand(): pl.pallas_call(functools.partial(expand_kernel, leaf_count), out_shape=[j...]
    pallas_call x1, Pallas kernels: 2.36 us -> 0.9 us  [near(): pl.pallas_call(functools.partial(near_kernel, sub_count), out_shape=[jax....]
    pallas_call x1, Pallas kernels: 2.24 us -> 1.35 us  [finish(): pl.pallas_call(finish_kernel, out_shape=jax.ShapeDtypeStruct((rows, subtr...]
    add x2, other arithmetic: 0.85 us -> 0.01 us  [local(): keep + got.astype(keep.dtype)]
    squeeze x1, local copies, waits for them, and re-layouts: 0.6 us -> 0.01 us  [local(): keep = lax.dynamic_index_in_dim(total, mine, 0, keepdims=False)]
  transfers between devices with their start and end apart: 12 -> 12, of which waited for: 3 -> 3; matrix products, arithmetic and copies ran while one was open for 4% -> 0% of each run, Pallas kernels for 17% -> 8%
where the time goes in v2:
time: 32.6 us; the launch traced here: 32.2 us
  starting transfers between devices  16.8 us (52%)
  waiting for transfers between devices  6.05 us (19%)
  local copies, waits for them, and re-layouts  5.21 us (16%)
  Pallas kernels  3.99 us (12%)
    ppermute x11, starting transfers between devices, flip(): return lax.ppermute(values, axis, [(i, i ^ bit) for i in range(count)])  16.2 us
    ppermute x11, waiting for transfers between devices, flip(): return lax.ppermute(values, axis, [(i, i ^ bit) for i in range(count)])  6.05 us
    unnamed x23, local copies, waits for them, and re-layouts  5.19 us
    pallas_call x1, Pallas kernels, expand(): pl.pallas_call(functools.partial(expand_kernel, leaf_count), out_shape=[j...  1.74 us
    pallas_call x1, Pallas kernels, finish(): pl.pallas_call(finish_kernel, out_shape=jax.ShapeDtypeStruct((rows, subtr...  1.35 us
    pallas_call x1, Pallas kernels, near(): pl.pallas_call(functools.partial(near_kernel, sub_count), out_shape=[jax....  0.9 us
    ppermute x1, starting transfers between devices, beside(): lax.ppermute(values, axis, [(i, j if 0 <= j < count else i) for i, j in e...  0.65 us
  transfers between devices with their start and end apart: 12, of which 3 were waited for; matrix products, arithmetic and copies ran while one was open for 0% of the time, Pallas kernels for 8%

profile of v2, /device:TPU:0, one launch (start us, length us, event | category | flops | bytes accessed | tf_op | source)
XLA Modules:
  0.0 32.2 jit_solution(4900760933118405340)
XLA Ops:
  0.0 3.0 %collective-permute-start.3 = (bf16[16,1024]{1,0:T(8,128)(2,1)}, bf16[16,1024]{1,0:T(8,128)(2,1)S(1)}, u32[]{:S(2)}, u32[]{:S(2)}) collective-permute-start(bf16[16,1024]{1,0:T(8,128)(2,1)} %vectors.1), channel_id=1, source_target_pairs={{0,2},{1,3},{2,0},{3,1},{4,6},{5,7},{6,4},{7,5},{8,10},{9,11},{10,... | collective-permute-start | bytes 98312 | tf_op jit(solution)/shard_map/ppermute | solution.py:16
  3.0 1.4 %copy-done = bf16[7,27,32,32]{3,2,1,0:T(8,128)(2,1)S(1)} copy-done((bf16[7,27,32,32]{3,2,1,0:T(8,128)(2,1)S(1)}, bf16[7,27,32,32]{3,2,1,0:T(8,128)(2,1)}, u32[]{:S(2)}) %copy-start) | copy-done | bytes 387096
  4.4 0.8 %copy-done.2 = bf16[4,32,256]{2,1,0:T(8,128)(2,1)S(1)} copy-done((bf16[4,32,256]{2,1,0:T(8,128)(2,1)S(1)}, bf16[4,32,256]{2,1,0:T(8,128)(2,1)}, u32[]{:S(2)}) %copy-start.2) | copy-done | bytes 65560
  5.2 0.8 %copy-done.4 = bf16[6,32,32]{2,1,0:T(8,128)(2,1)S(1)} copy-done((bf16[6,32,32]{2,1,0:T(8,128)(2,1)S(1)}, bf16[6,32,32]{2,1,0:T(8,128)(2,1)}, u32[]{:S(2)}) %copy-start.4) | copy-done | bytes 12312
  6.0 0.8 %copy-done.6 = bf16[16,1024]{1,0:T(8,128)(2,1)S(1)} copy-done((bf16[16,1024]{1,0:T(8,128)(2,1)S(1)}, bf16[16,1024]{1,0:T(8,128)(2,1)}, u32[]{:S(2)}) %copy-start.6) | copy-done | bytes 32792
  6.8 0.7 %copy-done.7 = s32[7,27]{1,0:T(8,128)S(1)} copy-done((s32[7,27]{1,0:T(8,128)S(1)}, s32[7,27]{1,0:T(8,128)}, u32[]{:S(2)}) %copy-start.7) | copy-done | bytes 780
  7.5 0.7 %copy-done.8 = s32[7,27]{1,0:T(8,128)S(1)} copy-done((s32[7,27]{1,0:T(8,128)S(1)}, s32[7,27]{1,0:T(8,128)}, u32[]{:S(2)}) %copy-start.8) | copy-done | bytes 780
  8.2 1.7 %expand.1 = (f32[4,2,16,128]{3,2,1,0:T(8,128)S(1)}, bf16[4,2,16,128]{3,2,1,0:T(8,128)(2,1)S(1)}) custom-call(s32[7,27]{1,0:T(8,128)S(1)} %copy-done.7, s32[7,27]{1,0:T(8,128)S(1)} %copy-done.8, bf16[16,1024]{1,0:T(8,128)(2,1)S(1)} %copy-done.6, bf16[4,32,256]{2,1,0:T(8,128)(2,1)S(1)} %copy-done.2, bf16[6,32,32]{2,1,0:T(8,128)(2,1)S(1)} %copy-done.4, ...), custom_call_target="tpu_custom_call" | custom-call | tf_op jit(solution)/shard_map/expand/pallas_call | solution.py:136
  9.9 1.6 %collective-permute-start = (bf16[4,2,16,128]{3,2,1,0:T(8,128)(2,1)S(1)}, bf16[4,2,16,128]{3,2,1,0:T(8,128)(2,1)S(1)}, u32[]{:S(2)}, u32[]{:S(2)}) collective-permute-start(bf16[4,2,16,128]{3,2,1,0:T(8,128)(2,1)S(1)} %get-tuple-element.12), channel_id=1, source_target_pairs={{0,4},{4,0},{8,12},{12,8},{16,20},{20,16},{24,28},{28,24},{1,5},{5... | collective-permute-start | bytes 98312 | tf_op jit(solution)/shard_map/ppermute | solution.py:16
  11.5 2.4 %collective-permute-done = bf16[4,2,16,128]{3,2,1,0:T(8,128)(2,1)S(1)} collective-permute-done((bf16[4,2,16,128]{3,2,1,0:T(8,128)(2,1)S(1)}, bf16[4,2,16,128]{3,2,1,0:T(8,128)(2,1)S(1)}, u32[]{:S(2)}, u32[]{:S(2)}) %collective-permute-start) | collective-permute-done | bytes 32800 | tf_op jit(solution)/shard_map/ppermute | solution.py:16
  13.9 2.7 %collective-permute-start.1 = (bf16[2,2,16,128]{3,2,1,0:T(8,128)(2,1)S(1)}, bf16[2,2,16,128]{3,2,1,0:T(8,128)(2,1)S(1)}, u32[]{:S(2)}, u32[]{:S(2)}) collective-permute-start(bf16[2,2,16,128]{3,2,1,0:T(8,128)(2,1)S(1)} %fusion), channel_id=1, source_target_pairs={{0,16},{4,20},{8,24},{12,28},{16,0},{20,4},{24,8},{28,12},{1,17},{... | collective-permute-start | bytes 49160 | tf_op jit(solution)/shard_map/ppermute | solution.py:16
  16.6 0.0 collective-permute-done.3
  16.6 0.7 %collective-permute-start.7 = (bf16[32,1024]{1,0:T(8,128)(2,1)S(1)}, bf16[32,1024]{1,0:T(8,128)(2,1)S(1)}, u32[]{:S(2)}, u32[]{:S(2)}) collective-permute-start(bf16[32,1024]{1,0:T(8,128)(2,1)S(1)} %constant_dynamic-update-slice_fusion.refs_0_), channel_id=1, source_target_pairs={{0,0},{4,8},{8,4},{12,16},{16,12},{20,24},{24,20},{28,28},{1,1},{5... | collective-permute-start | bytes 196616 | tf_op jit(solution)/shard_map/ppermute | solution.py:22
  17.3 4.3 %collective-permute-start.5 = (bf16[32,1024]{1,0:T(8,128)(2,1)S(1)}, bf16[32,1024]{1,0:T(8,128)(2,1)S(1)}, u32[]{:S(2)}, u32[]{:S(2)}) collective-permute-start(bf16[32,1024]{1,0:T(8,128)(2,1)S(1)} %constant_dynamic-update-slice_fusion.refs_0_), channel_id=1, source_target_pairs={{0,4},{4,0},{8,12},{12,8},{16,20},{20,16},{24,28},{28,24},{1,5},{5... | collective-permute-start | bytes 196616 | tf_op jit(solution)/shard_map/ppermute | solution.py:16
  21.6 0.0 collective-permute-start.4
  21.6 0.0 collective-permute-done.1
  21.6 0.0 collective-permute-done.7.refs_4_
  21.6 0.6 %collective-permute-start.8 = (bf16[32,1024]{1,0:T(8,128)(2,1)S(1)}, bf16[32,1024]{1,0:T(8,128)(2,1)S(1)}, u32[]{:S(2)}, u32[]{:S(2)}) collective-permute-start(bf16[32,1024]{1,0:T(8,128)(2,1)S(1)} %collective-permute-done.7.refs_4_), channel_id=1, source_target_pairs={{0,1},{1,0},{2,3},{3,2},{4,5},{5,4},{6,7},{7,6},{8,9},{9,8},{10,11... | collective-permute-start | bytes 196616 | tf_op jit(solution)/shard_map/ppermute | solution.py:16
  22.2 1.6 %collective-permute-done.5.refs_2_ = bf16[32,1024]{1,0:T(8,128)(2,1)S(1)} collective-permute-done((bf16[32,1024]{1,0:T(8,128)(2,1)S(1)}, bf16[32,1024]{1,0:T(8,128)(2,1)S(1)}, u32[]{:S(2)}, u32[]{:S(2)}) %collective-permute-start.5) | collective-permute-done | bytes 65568 | tf_op jit(solution)/shard_map/ppermute | solution.py:16
  23.9 2.1 %collective-permute-start.2 = (bf16[1,2,16,128]{3,2,1,0:T(8,128)(2,1)S(1)}, bf16[1,2,16,128]{3,2,1,0:T(8,128)(2,1)S(1)}, u32[]{:S(2)}, u32[]{:S(2)}) collective-permute-start(bf16[1,2,16,128]{3,2,1,0:T(8,128)(2,1)S(1)} %dynamic-slice_convert_fusion.1), channel_id=1, source_target_pairs={{0,8},{4,12},{8,0},{12,4},{16,24},{20,28},{24,16},{28,20},{1,9},{5... | collective-permute-start | bytes 24584 | tf_op jit(solution)/shard_map/ppermute | solution.py:16
  26.0 0.0 collective-permute-done.4.refs_1_
  26.0 0.0 collective-permute-done.8.refs_5_
  26.0 0.0 collective-permute-done.6.refs_3_
  26.0 0.9 %near.1 = (f32[16,256]{1,0:T(8,128)S(1)}, bf16[16,256]{1,0:T(8,128)(2,1)S(1)}, bf16[16,256]{1,0:T(8,128)(2,1)S(1)}, bf16[16,256]{1,0:T(8,128)(2,1)S(1)}) custom-call(s32[1,9]{1,0:T(1,128)S(1)} %copy-done.9, s32[1,9]{1,0:T(1,128)S(1)} %copy-done.10, bf16[1,9,256,256]{3,2,1,0:T(8,128)(2,1)S(1)} %copy-done.1, ...), custom_call_target="tpu_custom_call" | custom-call | tf_op jit(solution)/shard_map/near/pallas_call | solution.py:187
  26.9 0.2 collective-permute-start.9
  27.2 0.5 %collective-permute-start.10 = (bf16[16,256]{1,0:T(8,128)(2,1)S(1)}, bf16[16,256]{1,0:T(8,128)(2,1)S(1)}, u32[]{:S(2)}, u32[]{:S(2)}) collective-permute-start(bf16[16,256]{1,0:T(8,128)(2,1)S(1)} %get-tuple-element.15), channel_id=1, source_target_pairs={{0,2},{1,3},{2,0},{3,1},{4,6},{5,7},{6,4},{7,5},{8,10},{9,11},{10,... | collective-permute-start | bytes 24584 | tf_op jit(solution)/shard_map/ppermute | solution.py:16
  27.7 1.2 %collective-permute-start.11 = (bf16[16,256]{1,0:T(8,128)(2,1)S(1)}, bf16[16,256]{1,0:T(8,128)(2,1)S(1)}, u32[]{:S(2)}, u32[]{:S(2)}) collective-permute-start(bf16[16,256]{1,0:T(8,128)(2,1)S(1)} %get-tuple-element.16), channel_id=1, source_target_pairs={{0,3},{1,2},{2,1},{3,0},{4,7},{5,6},{6,5},{7,4},{8,11},{9,10},{10,... | collective-permute-start | bytes 24584 | tf_op jit(solution)/shard_map/ppermute | solution.py:16
  28.9 0.0 collective-permute-done.2.got
  28.9 0.0 collective-permute-done.9.refs_1_
  28.9 2.0 %collective-permute-done.10.refs_2_ = bf16[16,256]{1,0:T(8,128)(2,1)S(1)} collective-permute-done((bf16[16,256]{1,0:T(8,128)(2,1)S(1)}, bf16[16,256]{1,0:T(8,128)(2,1)S(1)}, u32[]{:S(2)}, u32[]{:S(2)}) %collective-permute-start.10) | collective-permute-done | bytes 8224 | tf_op jit(solution)/shard_map/ppermute | solution.py:16
  30.9 0.0 collective-permute-done.11.refs_3_
  30.9 1.4 %finish.1 = bf16[16,1024]{1,0:T(8,128)(2,1)} custom-call(f32[1,2,16,128]{3,2,1,0:T(8,128)S(1)} %constant_dynamic-slice_fusion.keep, bf16[1,2,16,128]{3,2,1,0:T(8,128)(2,1)S(1)} %collective-permute-done.2.got, bf16[6,32,32]{2,1,0:T(8,128)(2,1)S(1)} %copy-done.5, bf16[4,32,256]{2,1,0:T(8,128)(2,1)S(1)} %copy-done.3, f32[16,256]{1,0:T(8,128)S(1)} %get-tuple-element.13.refs_0_, ...), custom_call_target="tpu_custom_call" | custom-call | tf_op jit(solution)/shard_map/finish/pallas_call | solution.py:230
  (24 shorter events, 0.1 us)
Async XLA Ops:
  0.0 16.6 %collective-permute-start.3 = (bf16[16,1024]{1,0:T(8,128)(2,1)}, bf16[16,1024]{1,0:T(8,128)(2,1)S(1)}, u32[]{:S(2)}, u32[]{:S(2)}) collective-permute-start(bf16[16,1024]{1,0:T(8,128)(2,1)} %vectors.1), channel_id=1, source_target_pairs={{0,2},{1,3},{2,0},{3,1},{4,6},{5,7},{6,4},{7,5},{8,10},{9,11},{10,... | collective-permute-start | bytes 98312 | tf_op jit(solution)/shard_map/ppermute | solution.py:16
  3.0 1.4 %copy-start = (bf16[7,27,32,32]{3,2,1,0:T(8,128)(2,1)S(1)}, bf16[7,27,32,32]{3,2,1,0:T(8,128)(2,1)}, u32[]{:S(2)}) copy-start(bf16[7,27,32,32]{3,2,1,0:T(8,128)(2,1)} %coupling.1) | copy-start | bytes 1161220
  4.4 0.8 %copy-start.2 = (bf16[4,32,256]{2,1,0:T(8,128)(2,1)S(1)}, bf16[4,32,256]{2,1,0:T(8,128)(2,1)}, u32[]{:S(2)}) copy-start(bf16[4,32,256]{2,1,0:T(8,128)(2,1)} %basis.3) | copy-start | bytes 196612
  5.2 0.8 %copy-start.4 = (bf16[6,32,32]{2,1,0:T(8,128)(2,1)S(1)}, bf16[6,32,32]{2,1,0:T(8,128)(2,1)}, u32[]{:S(2)}) copy-start(bf16[6,32,32]{2,1,0:T(8,128)(2,1)} %transfer.3) | copy-start | bytes 36868
  6.0 0.8 %copy-start.6 = (bf16[16,1024]{1,0:T(8,128)(2,1)S(1)}, bf16[16,1024]{1,0:T(8,128)(2,1)}, u32[]{:S(2)}) copy-start(bf16[16,1024]{1,0:T(8,128)(2,1)} %vectors.1) | copy-start | bytes 98308
  6.8 0.7 %copy-start.7 = (s32[7,27]{1,0:T(8,128)S(1)}, s32[7,27]{1,0:T(8,128)}, u32[]{:S(2)}) copy-start(s32[7,27]{1,0:T(8,128)} %targets.1) | copy-start | bytes 2272
  7.5 0.7 %copy-start.8 = (s32[7,27]{1,0:T(8,128)S(1)}, s32[7,27]{1,0:T(8,128)}, u32[]{:S(2)}) copy-start(s32[7,27]{1,0:T(8,128)} %alive.2) | copy-start | bytes 2272
  8.1 17.9 %copy-start.1 = (bf16[1,9,256,256]{3,2,1,0:T(8,128)(2,1)S(1)}, bf16[1,9,256,256]{3,2,1,0:T(8,128)(2,1)}, u32[]{:S(2)}) copy-start(bf16[1,9,256,256]{3,2,1,0:T(8,128)(2,1)} %blocks.1) | copy-start | bytes 3538948
  8.1 17.9 %copy-start.9 = (s32[1,9]{1,0:T(1,128)S(1)}, s32[1,9]{1,0:T(1,128)}, u32[]{:S(2)}) copy-start(s32[1,9]{1,0:T(1,128)} %columns.1) | copy-start | bytes 112
  8.1 17.9 %copy-start.10 = (s32[1,9]{1,0:T(1,128)S(1)}, s32[1,9]{1,0:T(1,128)}, u32[]{:S(2)}) copy-start(s32[1,9]{1,0:T(1,128)} %alive.3) | copy-start | bytes 112
  8.1 22.7 %copy-start.3 = (bf16[4,32,256]{2,1,0:T(8,128)(2,1)S(1)}, bf16[4,32,256]{2,1,0:T(8,128)(2,1)}, u32[]{:S(2)}) copy-start(bf16[4,32,256]{2,1,0:T(8,128)(2,1)} %basis.3) | copy-start | bytes 196612
  8.2 22.7 %copy-start.5 = (bf16[6,32,32]{2,1,0:T(8,128)(2,1)S(1)}, bf16[6,32,32]{2,1,0:T(8,128)(2,1)}, u32[]{:S(2)}) copy-start(bf16[6,32,32]{2,1,0:T(8,128)(2,1)} %transfer.3) | copy-start | bytes 36868
  9.9 4.0 %collective-permute-start = (bf16[4,2,16,128]{3,2,1,0:T(8,128)(2,1)S(1)}, bf16[4,2,16,128]{3,2,1,0:T(8,128)(2,1)S(1)}, u32[]{:S(2)}, u32[]{:S(2)}) collective-permute-start(bf16[4,2,16,128]{3,2,1,0:T(8,128)(2,1)S(1)} %get-tuple-element.12), channel_id=1, source_target_pairs={{0,4},{4,0},{8,12},{12,8},{16,20},{20,16},{24,28},{28,24},{1,5},{5... | collective-permute-start | bytes 98312 | tf_op jit(solution)/shard_map/ppermute | solution.py:16
  13.9 7.7 %collective-permute-start.1 = (bf16[2,2,16,128]{3,2,1,0:T(8,128)(2,1)S(1)}, bf16[2,2,16,128]{3,2,1,0:T(8,128)(2,1)S(1)}, u32[]{:S(2)}, u32[]{:S(2)}) collective-permute-start(bf16[2,2,16,128]{3,2,1,0:T(8,128)(2,1)S(1)} %fusion), channel_id=1, source_target_pairs={{0,16},{4,20},{8,24},{12,28},{16,0},{20,4},{24,8},{28,12},{1,17},{... | collective-permute-start | bytes 49160 | tf_op jit(solution)/shard_map/ppermute | solution.py:16
  16.6 5.0 %collective-permute-start.7 = (bf16[32,1024]{1,0:T(8,128)(2,1)S(1)}, bf16[32,1024]{1,0:T(8,128)(2,1)S(1)}, u32[]{:S(2)}, u32[]{:S(2)}) collective-permute-start(bf16[32,1024]{1,0:T(8,128)(2,1)S(1)} %constant_dynamic-update-slice_fusion.refs_0_), channel_id=1, source_target_pairs={{0,0},{4,8},{8,4},{12,16},{16,12},{20,24},{24,20},{28,28},{1,1},{5... | collective-permute-start | bytes 196616 | tf_op jit(solution)/shard_map/ppermute | solution.py:22
  17.3 6.6 %collective-permute-start.5 = (bf16[32,1024]{1,0:T(8,128)(2,1)S(1)}, bf16[32,1024]{1,0:T(8,128)(2,1)S(1)}, u32[]{:S(2)}, u32[]{:S(2)}) collective-permute-start(bf16[32,1024]{1,0:T(8,128)(2,1)S(1)} %constant_dynamic-update-slice_fusion.refs_0_), channel_id=1, source_target_pairs={{0,4},{4,0},{8,12},{12,8},{16,20},{20,16},{24,28},{28,24},{1,5},{5... | collective-permute-start | bytes 196616 | tf_op jit(solution)/shard_map/ppermute | solution.py:16
  21.6 4.4 %collective-permute-start.4 = (bf16[32,1024]{1,0:T(8,128)(2,1)S(1)}, bf16[32,1024]{1,0:T(8,128)(2,1)S(1)}, u32[]{:S(2)}, u32[]{:S(2)}) collective-permute-start(bf16[32,1024]{1,0:T(8,128)(2,1)S(1)} %constant_dynamic-update-slice_fusion.refs_0_), channel_id=1, source_target_pairs={{0,1},{1,0},{2,3},{3,2},{4,5},{5,4},{6,7},{7,6},{8,9},{9,8},{10,11... | collective-permute-start | bytes 196616 | tf_op jit(solution)/shard_map/ppermute | solution.py:16
  21.6 4.4 %collective-permute-start.8 = (bf16[32,1024]{1,0:T(8,128)(2,1)S(1)}, bf16[32,1024]{1,0:T(8,128)(2,1)S(1)}, u32[]{:S(2)}, u32[]{:S(2)}) collective-permute-start(bf16[32,1024]{1,0:T(8,128)(2,1)S(1)} %collective-permute-done.7.refs_4_), channel_id=1, source_target_pairs={{0,1},{1,0},{2,3},{3,2},{4,5},{5,4},{6,7},{7,6},{8,9},{9,8},{10,11... | collective-permute-start | bytes 196616 | tf_op jit(solution)/shard_map/ppermute | solution.py:16
  23.8 2.1 %collective-permute-start.6 = (bf16[32,1024]{1,0:T(8,128)(2,1)S(1)}, bf16[32,1024]{1,0:T(8,128)(2,1)S(1)}, u32[]{:S(2)}, u32[]{:S(2)}) collective-permute-start(bf16[32,1024]{1,0:T(8,128)(2,1)S(1)} %collective-permute-done.5.refs_2_), channel_id=1, source_target_pairs={{0,1},{1,0},{2,3},{3,2},{4,5},{5,4},{6,7},{7,6},{8,9},{9,8},{10,11... | collective-permute-start | bytes 196616 | tf_op jit(solution)/shard_map/ppermute | solution.py:16
  23.9 5.0 %collective-permute-start.2 = (bf16[1,2,16,128]{3,2,1,0:T(8,128)(2,1)S(1)}, bf16[1,2,16,128]{3,2,1,0:T(8,128)(2,1)S(1)}, u32[]{:S(2)}, u32[]{:S(2)}) collective-permute-start(bf16[1,2,16,128]{3,2,1,0:T(8,128)(2,1)S(1)} %dynamic-slice_convert_fusion.1), channel_id=1, source_target_pairs={{0,8},{4,12},{8,0},{12,4},{16,24},{20,28},{24,16},{28,20},{1,9},{5... | collective-permute-start | bytes 24584 | tf_op jit(solution)/shard_map/ppermute | solution.py:16
  26.9 1.9 %collective-permute-start.9 = (bf16[16,256]{1,0:T(8,128)(2,1)S(1)}, bf16[16,256]{1,0:T(8,128)(2,1)S(1)}, u32[]{:S(2)}, u32[]{:S(2)}) collective-permute-start(bf16[16,256]{1,0:T(8,128)(2,1)S(1)} %get-tuple-element.14), channel_id=1, source_target_pairs={{0,1},{1,0},{2,3},{3,2},{4,5},{5,4},{6,7},{7,6},{8,9},{9,8},{10,11... | collective-permute-start | bytes 24584 | tf_op jit(solution)/shard_map/ppermute | solution.py:16
  27.2 3.7 %collective-permute-start.10 = (bf16[16,256]{1,0:T(8,128)(2,1)S(1)}, bf16[16,256]{1,0:T(8,128)(2,1)S(1)}, u32[]{:S(2)}, u32[]{:S(2)}) collective-permute-start(bf16[16,256]{1,0:T(8,128)(2,1)S(1)} %get-tuple-element.15), channel_id=1, source_target_pairs={{0,2},{1,3},{2,0},{3,1},{4,6},{5,7},{6,4},{7,5},{8,10},{9,11},{10,... | collective-permute-start | bytes 24584 | tf_op jit(solution)/shard_map/ppermute | solution.py:16
  27.7 3.2 %collective-permute-start.11 = (bf16[16,256]{1,0:T(8,128)(2,1)S(1)}, bf16[16,256]{1,0:T(8,128)(2,1)S(1)}, u32[]{:S(2)}, u32[]{:S(2)}) collective-permute-start(bf16[16,256]{1,0:T(8,128)(2,1)S(1)} %get-tuple-element.16), channel_id=1, source_target_pairs={{0,3},{1,2},{2,1},{3,0},{4,7},{5,6},{6,5},{7,4},{8,11},{9,10},{10,... | collective-permute-start | bytes 24584 | tf_op jit(solution)/shard_map/ppermute | solution.py:16

commit v3 on v2

v3 whole, which is shorter than its diff:
```python
import functools

import jax
import jax.numpy as jnp
from jax import lax
from jax.experimental import pallas as pl
from jax.experimental.pallas import tpu as pltpu
from jax.sharding import PartitionSpec as P


LANES = 128
PARAMS = pltpu.CompilerParams(vmem_limit_bytes=16 * 2**20)
SMEM = pl.BlockSpec(memory_space=pltpu.SMEM)
VMEM = pl.BlockSpec(memory_space=pltpu.VMEM)
HBM = pl.BlockSpec(memory_space=pltpu.HBM)


def flip(values, axis, bit):
    count = lax.axis_size(axis)
    return lax.ppermute(values, axis, [(i, i ^ bit) for i in range(count)])


def beside(values, axis):
    count = lax.axis_size(axis)
    other = [((i + 1) ^ 1) - 1 for i in range(count)]
    pairs = [(i, j if 0 <= j < count else i) for i, j in enumerate(other)]
    return lax.ppermute(values, axis, pairs)


def bits_of(count):
    bits = []
    while count > 1:
        count = count // 2
        bits.append(count)
    return bits


def levels_of(subtree):
    sizes = []
    while subtree >= 1:
        sizes.append(subtree)
        subtree = subtree // 2
    starts = [sum(sizes[:number]) for number in range(len(sizes))]
    return sizes, starts


def halves(values):
    high = values.astype(jnp.bfloat16)
    return high, (values - high.astype(jnp.float32)).astype(jnp.bfloat16)


def dot(left, right, contract=((1,), (0,))):
    return lax.dot_general(left, right, (contract, ((), ())), preferred_element_type=jnp.float32)


def expand_kernel(
    leaf_count, targets_in, alive_in, vectors_in, basis_in, transfer_in, coupling_in, keep, send, *scratch
):
    targets, alive, vectors, basis, transfer, coupling, done, *sums = scratch
    subtree, rank, leaf_size = basis.shape
    clusters, far_count = coupling.shape[:2]
    nodes = leaf_count * clusters
    sizes, starts = levels_of(subtree)
    rows = vectors.shape[0]
    parity = lax.axis_index("leaf") % 2
    copies = [
        pltpu.make_async_copy(source, target, done.at[number])
        for number, (source, target) in enumerate(
            (
                (vectors_in, vectors),
                (basis_in, basis),
                (coupling_in.at[:subtree], coupling.at[:subtree]),
                (transfer_in, transfer),
                (targets_in, targets),
                (alive_in, alive),
                (coupling_in.at[subtree:], coupling.at[subtree:]),
            )
        )
    ]
    for copy in copies:
        copy.start()
    zero = jnp.zeros((rows, rank), jnp.float32)
    shared = len(sums) < clusters
    if shared:

        def clear(row, carry):
            sums[0][row] = zero
            return carry

        lax.fori_loop(0, nodes, clear, 0)
    else:
        for number, size in enumerate(sizes):
            for c in range(starts[number], starts[number] + size):
                for tree in range(leaf_count):
                    for j in range(starts[number], starts[number] + size):
                        sums[c][tree * clusters + j] = zero
    copies[0].wait()
    copies[1].wait()
    hats = [
        dot(vectors[:, j * leaf_size : (j + 1) * leaf_size], basis[j], ((1,), (1,)))
        for j in range(subtree)
    ]
    copies[3].wait()
    for number in range(len(sizes) - 1):
        for p in range(sizes[number + 1]):
            total = None
            for c in (starts[number] + 2 * p, starts[number] + 2 * p + 1):
                high, low = halves(hats[c])
                part = dot(high, transfer[c]) + dot(low, transfer[c])
                total = part if total is None else total + part
            hats.append(total)
    lefts = [hat.astype(jnp.bfloat16) for hat in hats]
    copies[4].wait()
    copies[5].wait()
    for wait, members in ((2, range(subtree)), (6, range(subtree, clusters))):
        copies[wait].wait()
        for k in range(far_count):
            for c in members:
                term = dot(lefts[c], coupling[c, k])
                row = jnp.where(alive[c, k] == 1, targets[c, k], nodes)
                held = sums[0 if shared else c]
                held[row] = held[row] + term
    per = LANES // rank

    def gathered(tree):
        groups = []
        for first in range(0, clusters, per):
            lanes = []
            for place in range(first, first + per):
                if place >= clusters:
                    lanes.append(zero)
                    continue
                number = max(n for n in range(len(sizes)) if starts[n] <= place)
                row = tree * clusters + place
                if shared:
                    lanes.append(sums[0][row])
                else:
                    level = range(starts[number], starts[number] + sizes[number])
                    lanes.append(sum(sums[c][row] for c in level))
            groups.append(jnp.concatenate(lanes, axis=1))
        return groups

    def emit(half, carry):
        for out, tree in ((keep, 2 * half + parity), (send, 2 * half + 1 - parity)):
            for number, group in enumerate(gathered(tree)):
                out[half, number] = group.astype(out.dtype)
        return carry

    if leaf_count <= 8:
        for half in range(leaf_count // 2):
            emit(half, 0)
    else:
        lax.fori_loop(0, leaf_count // 2, emit, 0)


def expand(vectors, basis, transfer, coupling, targets, alive):
    leaf_count = lax.axis_size("leaf")
    clusters, _, rank = coupling.shape[:3]
    rows = vectors.shape[0]
    nodes = leaf_count * clusters
    groups = -(-clusters * rank // LANES)
    shape = (leaf_count // 2, groups, rows, LANES)
    copies = clusters if nodes <= 128 else 1
    return pl.pallas_call(
        functools.partial(expand_kernel, leaf_count),
        out_shape=[
            jax.ShapeDtypeStruct(shape, jnp.float32),
            jax.ShapeDtypeStruct(shape, jnp.bfloat16),
        ],
        in_specs=[HBM] * 6,
        out_specs=[VMEM, VMEM],
        scratch_shapes=[
            pltpu.SMEM(targets.shape, targets.dtype),
            pltpu.SMEM(alive.shape, alive.dtype),
            pltpu.VMEM(vectors.shape, vectors.dtype),
            pltpu.VMEM(basis.shape, basis.dtype),
            pltpu.VMEM(transfer.shape, transfer.dtype),
            pltpu.VMEM(coupling.shape, coupling.dtype),
            pltpu.SemaphoreType.DMA((7,)),
        ]
        + [pltpu.VMEM((nodes + 1, rows, rank), jnp.float32)] * copies,
        compiler_params=PARAMS,
        name="expand",
    )(
        *(
            pltpu.with_memory_space_constraint(value, pltpu.HBM)
            for value in (targets, alive, vectors, basis, transfer, coupling)
        )
    )


def operator_kernel(transfer, basis, high_out, low_out):
    subtree, rank, leaf_size = basis.shape
    sizes, starts = levels_of(subtree)
    high_out[...] = jnp.zeros(high_out.shape, high_out.dtype)
    low_out[...] = jnp.zeros(low_out.shape, low_out.dtype)
    for j in range(subtree):
        columns = slice(j * leaf_size, (j + 1) * leaf_size)
        parts = (basis[j],)
        c = j
        for number in range(len(sizes)):
            at = slice(c * rank, (c + 1) * rank)
            high_out[at, columns] = parts[0]
            if len(parts) > 1:
                low_out[at, columns] = parts[1]
            if number + 1 < len(sizes):
                total = sum(dot(transfer[c], part, ((0,), (0,))) for part in parts)
                parts = halves(total)
                c = starts[number + 1] + (c - starts[number]) // 2


def operator(transfer, basis, depth):
    subtree, _, leaf_size = basis.shape
    shape = jax.ShapeDtypeStruct((depth, subtree * leaf_size), jnp.bfloat16)
    return pl.pallas_call(
        operator_kernel,
        out_shape=[shape, shape],
        in_specs=[VMEM, VMEM],
        out_specs=[VMEM, VMEM],
        compiler_params=PARAMS,
        name="operator",
    )(transfer, basis)


def near_kernel(places, sub_count, columns, alive, blocks, *refs):
    window, outs, pieces = refs[-1], refs[-1 - len(places) : -1], refs[: -1 - len(places)]
    per_tree = len(pieces) // 3
    rows, points = pieces[0].shape
    count, leaf_size = blocks.shape[1:3]
    subtree = points // leaf_size
    for tree in range(3):
        for part in range(per_tree):
            window[tree, part * rows : (part + 1) * rows, :] = pieces[tree * per_tree + part][...]
    me = lax.axis_index("leaf")
    first = me * subtree
    partner = (me ^ 1) * subtree
    total = None
    for k in range(count):
        column = columns[0, k]
        own_tree = (column >= first) & (column < first + subtree)
        partner_tree = (column >= partner) & (column < partner + subtree)
        tree = jnp.where(own_tree, 0, jnp.where(partner_tree, 1, 2))
        place = lax.rem(column, subtree)
        start = pl.multiple_of(place * leaf_size, leaf_size)
        taken = window[tree, :, pl.ds(start, leaf_size)]
        live = alive[0, k].astype(jnp.float32).astype(jnp.bfloat16)
        product = dot(taken * live, blocks[0, k])
        total = product if total is None else total + product
    size = total.shape[0] // sub_count
    for out, groups in zip(outs, places):
        for number, group in enumerate(groups):
            out[number] = total[group * size : (group + 1) * size].astype(out.dtype)


def near(pieces, blocks, columns, alive, rows, places):
    sub_count = lax.axis_size("sub")
    leaf_size = blocks.shape[2]
    points = pieces[0].shape[1]
    return pl.pallas_call(
        functools.partial(near_kernel, places, sub_count),
        out_shape=[
            jax.ShapeDtypeStruct(
                (len(groups), rows, leaf_size), jnp.bfloat16 if number else jnp.float32
            )
            for number, groups in enumerate(places)
        ],
        in_specs=[SMEM, SMEM] + [VMEM] * (1 + len(pieces)),
        out_specs=[VMEM] * len(places),
        scratch_shapes=[pltpu.VMEM((3, rows * sub_count, points), jnp.bfloat16)],
        compiler_params=PARAMS,
        name="near",
    )(columns, alive, blocks, *pieces)


def finish_kernel(sources, keep, got, high_in, low_in, *refs):
    nears, out = refs[:-1], refs[-1]
    incoming = jnp.concatenate(
        [keep[0, g] + got[0, g].astype(jnp.float32) for g in range(keep.shape[1])], axis=1
    )
    high, low = halves(incoming)
    far = dot(high, high_in[...]) + dot(low, high_in[...]) + dot(high, low_in[...])
    me = lax.axis_index("sub")
    leaf_size = nears[0].shape[2]
    pieces = [(source, nears[at][row].astype(jnp.float32)) for source, at, row in sources]
    for j in range(len(sources)):
        piece = pieces[0][1]
        for source, values in pieces[1:]:
            piece = jnp.where((me ^ source) == j, values, piece)
        columns = slice(j * leaf_size, (j + 1) * leaf_size)
        out[:, columns] = (piece + far[:, columns]).astype(out.dtype)


def finish(keep, got, high, low, nears, sources):
    rows = nears[0].shape[1]
    return pl.pallas_call(
        functools.partial(finish_kernel, sources),
        out_shape=jax.ShapeDtypeStruct((rows, high.shape[1]), jnp.bfloat16),
        in_specs=[VMEM] * (4 + len(nears)),
        out_specs=VMEM,
        compiler_params=PARAMS,
        name="finish",
    )(keep, got, high, low, *nears)


def local(
    vectors,
    near_blocks,
    near_cols,
    near_mask,
    leaf_basis,
    transfer,
    coupling,
    far_targets,
    far_mask,
):
    leaf_count = lax.axis_size("leaf")
    sub_count = lax.axis_size("sub")
    me = lax.axis_index("leaf")
    rows = vectors.shape[0]
    bits = bits_of(sub_count)
    pair = jnp.concatenate([vectors, flip(vectors, "sub", bits[0])], axis=0)
    keep, send = expand(vectors, leaf_basis, transfer, coupling, far_targets, far_mask)
    trees = [[pair], [flip(pair, "leaf", 1)], [beside(pair, "leaf")]]
    got = flip(send, "leaf", 1)
    order = [0, bits[0]]
    for bit in bits[1:]:
        trees = [parts + [flip(part, "sub", bit) for part in parts] for parts in trees]
        order = order + [number ^ bit for number in order]
    pieces = [part for parts in trees for part in parts]
    high, low = operator(transfer, leaf_basis, keep.shape[1] * LANES)
    for size in bits_of(leaf_count)[:-1]:
        total = (keep + got.astype(keep.dtype)).reshape(2, size // 2, *keep.shape[1:])
        mine = (me & size) // size
        keep = lax.dynamic_index_in_dim(total, mine, 0, keepdims=False)
        send = lax.dynamic_index_in_dim(total, 1 - mine, 0, keepdims=False)
        got = flip(send.astype(jnp.bfloat16), "leaf", size)
    places = [[order.index(0)]] + [
        [order.index(home) for home in range(bit, 2 * bit)] for bit in bits
    ]
    made = near(pieces, near_blocks, near_cols, near_mask, rows, places)
    arrays = list(made)
    pool = {0: [(0, 0, 0)]}
    for number, bit in enumerate(bits):
        for row in range(bit):
            pool[bit + row] = [(0, number + 1, row)]
    for bit in bits:
        sent = [(home, item) for home in range(bit, 2 * bit) for item in pool[home]]
        if len(sent) == arrays[sent[0][1][1]].shape[0]:
            stack = arrays[sent[0][1][1]]
        else:
            stack = jnp.concatenate([arrays[at][row : row + 1] for _, (_, at, row) in sent], axis=0)
        arrays.append(flip(stack, "sub", bit))
        for row, (home, (source, _, _)) in enumerate(sent):
            pool[home ^ bit].append((source ^ bit, len(arrays) - 1, row))
    used = sorted({at for _, at, _ in pool[0]})
    sources = [(source, used.index(at), row) for source, at, row in pool[0]]
    return finish(keep, got, high, low, [arrays[at] for at in used], sources)


def solution(mesh):
    return jax.shard_map(
        local,
        mesh=mesh,
        in_specs=(
            P("sub", "leaf"),
            P(("leaf", "sub"), None, None, None),
            P(("leaf", "sub"), None),
            P(("leaf", "sub"), None),
            P("leaf", None, None),
            P("leaf", None, None),
            P("leaf", None, None, None),
            P("leaf", None),
            P("leaf", None),
        ),
        out_specs=P("sub", "leaf"),
        check_vma=False,
    )
```

time: 32.6 us -> 24.1 us (0.74)
  local copies, waits for them, and re-layouts: 5.21 us -> 0.06 us
  waiting for transfers between devices: 6.05 us -> 4.03 us
  starting transfers between devices: 16.8 us -> 15 us
  Pallas kernels: 3.99 us -> 4.61 us
    unnamed x23 -> x13, local copies, waits for them, and re-layouts: 5.19 us -> 0.03 us
    ppermute x11 -> x10, waiting for transfers between devices: 6.05 us -> 4.03 us  [flip(): return lax.ppermute(values, axis, [(i, i ^ bit) for i in range(count)])]
    ppermute x11 -> x10, starting transfers between devices: 16.2 us -> 14.4 us  [flip(): return lax.ppermute(values, axis, [(i, i ^ bit) for i in range(count)])]
    pallas_call x1, Pallas kernels: 1.74 us -> 2.31 us  [expand(): pl.pallas_call(functools.partial(expand_kernel, leaf_count), out_shape=[j...]
    pallas_call x2 -> x3, Pallas kernels: 2.25 us -> 2.3 us  [the longest x1 0.94 us: finish(): pl.pallas_call(functools.partial(finish_kernel, sources), out_shape=jax.S...]
  transfers between devices with their start and end apart: 12 -> 11, of which waited for: 3 -> 5; matrix products, arithmetic and copies ran while one was open for 0% -> 0% of each run, Pallas kernels for 8% -> 12%
where the time goes in v3:
time: 24.1 us; the launch traced here: 23.9 us
  starting transfers between devices  15 us (62%)
  Pallas kernels  4.61 us (19%)
  waiting for transfers between devices  4.03 us (17%)
    ppermute x10, starting transfers between devices, flip(): return lax.ppermute(values, axis, [(i, i ^ bit) for i in range(count)])  14.4 us
    ppermute x10, waiting for transfers between devices, flip(): return lax.ppermute(values, axis, [(i, i ^ bit) for i in range(count)])  4.03 us
    pallas_call x1, Pallas kernels, expand(): pl.pallas_call(functools.partial(expand_kernel, leaf_count), out_shape=[j...  2.31 us
    pallas_call x1, Pallas kernels, finish(): pl.pallas_call(functools.partial(finish_kernel, sources), out_shape=jax.S...  0.94 us
    pallas_call x1, Pallas kernels, near(): pl.pallas_call(functools.partial(near_kernel, places, sub_count), out_sha...  0.89 us
    ppermute x1, starting transfers between devices, beside(): return lax.ppermute(values, axis, pairs)  0.66 us
  transfers between devices with their start and end apart: 11, of which 5 were waited for; matrix products, arithmetic and copies ran while one was open for 0% of the time, Pallas kernels for 12%

profile of v3, /device:TPU:0, one launch (start us, length us, event | category | flops | bytes accessed | tf_op | source)
XLA Modules:
  0.0 23.9 jit_solution(15845831692882308398)
XLA Ops:
  0.0 0.0 copy-start
  0.0 3.0 %collective-permute-start.3 = (bf16[16,1024]{1,0:T(8,128)(2,1)}, bf16[16,1024]{1,0:T(8,128)(2,1)S(1)}, u32[]{:S(2)}, u32[]{:S(2)}) collective-permute-start(bf16[16,1024]{1,0:T(8,128)(2,1)} %vectors_in.1), channel_id=1, source_target_pairs={{0,2},{1,3},{2,0},{3,1},{4,6},{5,7},{6,4},{7,5},{8,10},{9,11},{10,... | collective-permute-start | bytes 98312 | tf_op jit(solution)/shard_map/ppermute | solution.py:20
  3.1 2.3 %expand.1 = (f32[4,2,16,128]{3,2,1,0:T(8,128)S(1)}, bf16[4,2,16,128]{3,2,1,0:T(8,128)(2,1)S(1)}) custom-call(s32[7,27]{1,0:T(8,128)} %targets_in.1, s32[7,27]{1,0:T(8,128)} %alive_in.1, bf16[16,1024]{1,0:T(8,128)(2,1)} %vectors_in.1, bf16[4,32,256]{2,1,0:T(8,128)(2,1)} %basis.1, bf16[6,32,32]{2,1,0:T(8,128)(2,1)} %transfer.1, bf16[7,27,32,32]{3,2,1,0:T(8,128)(2,1)} %coupling_in.1), custom_call_target="tpu_custom_call" | custom-call | tf_op jit(solution)/shard_map/expand/pallas_call | solution.py:164
  5.4 1.6 %collective-permute-start = (bf16[4,2,16,128]{3,2,1,0:T(8,128)(2,1)S(1)}, bf16[4,2,16,128]{3,2,1,0:T(8,128)(2,1)S(1)}, u32[]{:S(2)}, u32[]{:S(2)}) collective-permute-start(bf16[4,2,16,128]{3,2,1,0:T(8,128)(2,1)S(1)} %get-tuple-element.13), channel_id=1, source_target_pairs={{0,4},{4,0},{8,12},{12,8},{16,20},{20,16},{24,28},{28,24},{1,5},{5... | collective-permute-start | bytes 98312 | tf_op jit(solution)/shard_map/ppermute | solution.py:20
  7.0 0.0 copy-done.5
  7.0 0.0 collective-permute-done.3
  7.0 0.7 %collective-permute-start.7 = (bf16[32,1024]{1,0:T(8,128)(2,1)S(1)}, bf16[32,1024]{1,0:T(8,128)(2,1)S(1)}, u32[]{:S(2)}, u32[]{:S(2)}) collective-permute-start(bf16[32,1024]{1,0:T(8,128)(2,1)S(1)} %constant_dynamic-update-slice_fusion.refs_0_), channel_id=1, source_target_pairs={{0,0},{4,8},{8,4},{12,16},{16,12},{20,24},{24,20},{28,28},{1,1},{5... | collective-permute-start | bytes 196616 | tf_op jit(solution)/shard_map/ppermute | solution.py:27
  7.7 4.3 %collective-permute-start.5 = (bf16[32,1024]{1,0:T(8,128)(2,1)S(1)}, bf16[32,1024]{1,0:T(8,128)(2,1)S(1)}, u32[]{:S(2)}, u32[]{:S(2)}) collective-permute-start(bf16[32,1024]{1,0:T(8,128)(2,1)S(1)} %constant_dynamic-update-slice_fusion.refs_0_), channel_id=1, source_target_pairs={{0,4},{4,0},{8,12},{12,8},{16,20},{20,16},{24,28},{28,24},{1,5},{5... | collective-permute-start | bytes 196616 | tf_op jit(solution)/shard_map/ppermute | solution.py:20
  12.0 0.0 collective-permute-done
  12.0 2.7 %collective-permute-start.1 = (bf16[2,2,16,128]{3,2,1,0:T(8,128)(2,1)S(1)}, bf16[2,2,16,128]{3,2,1,0:T(8,128)(2,1)S(1)}, u32[]{:S(2)}, u32[]{:S(2)}) collective-permute-start(bf16[2,2,16,128]{3,2,1,0:T(8,128)(2,1)S(1)} %fusion), channel_id=1, source_target_pairs={{0,16},{4,20},{8,24},{12,28},{16,0},{20,4},{24,8},{28,12},{1,17},{... | collective-permute-start | bytes 49160 | tf_op jit(solution)/shard_map/ppermute | solution.py:20
  14.7 0.0 copy-done.2
  14.7 0.0 copy-done.1
  14.7 0.5 %operator.1 = (bf16[256,1024]{1,0:T(8,128)(2,1)S(1)}, bf16[256,1024]{1,0:T(8,128)(2,1)S(1)}) custom-call(bf16[6,32,32]{2,1,0:T(8,128)(2,1)S(1)} %copy-done.2, bf16[4,32,256]{2,1,0:T(8,128)(2,1)S(1)} %copy-done.1), custom_call_target="tpu_custom_call" | custom-call | tf_op jit(solution)/shard_map/operator/pallas_call | solution.py:215
  15.2 0.1 collective-permute-start.4
  15.3 0.0 collective-permute-done.7.refs_4_
  15.3 0.5 %collective-permute-start.8 = (bf16[32,1024]{1,0:T(8,128)(2,1)S(1)}, bf16[32,1024]{1,0:T(8,128)(2,1)S(1)}, u32[]{:S(2)}, u32[]{:S(2)}) collective-permute-start(bf16[32,1024]{1,0:T(8,128)(2,1)S(1)} %collective-permute-done.7.refs_4_), channel_id=1, source_target_pairs={{0,1},{1,0},{2,3},{3,2},{4,5},{5,4},{6,7},{7,6},{8,9},{9,8},{10,11... | collective-permute-start | bytes 196616 | tf_op jit(solution)/shard_map/ppermute | solution.py:20
  15.8 0.0 collective-permute-done.5.refs_2_
  15.8 0.1 collective-permute-start.6
  15.9 0.9 %collective-permute-done.1 = bf16[2,2,16,128]{3,2,1,0:T(8,128)(2,1)S(1)} collective-permute-done((bf16[2,2,16,128]{3,2,1,0:T(8,128)(2,1)S(1)}, bf16[2,2,16,128]{3,2,1,0:T(8,128)(2,1)S(1)}, u32[]{:S(2)}, u32[]{:S(2)}) %collective-permute-start.1) | collective-permute-done | bytes 16416 | tf_op jit(solution)/shard_map/ppermute | solution.py:20
  16.8 0.0 collective-permute-done.4.refs_1_
  16.8 0.0 collective-permute-done.8.refs_5_
  16.8 0.3 %collective-permute-done.6.refs_3_ = bf16[32,1024]{1,0:T(8,128)(2,1)S(1)} collective-permute-done((bf16[32,1024]{1,0:T(8,128)(2,1)S(1)}, bf16[32,1024]{1,0:T(8,128)(2,1)S(1)}, u32[]{:S(2)}, u32[]{:S(2)}) %collective-permute-start.6) | collective-permute-done | bytes 65568 | tf_op jit(solution)/shard_map/ppermute | solution.py:20
  17.1 0.0 copy-done.4
  17.1 0.0 copy-done
  17.1 0.9 %near.1 = (f32[1,16,256]{2,1,0:T(8,128)S(1)}, bf16[2,16,256]{2,1,0:T(8,128)(2,1)S(1)}, bf16[1,16,256]{2,1,0:T(8,128)(2,1)S(1)}) custom-call(s32[1,9]{1,0:T(1,128)S(1)} %copy-done.3, s32[1,9]{1,0:T(1,128)S(1)} %copy-done.4, bf16[1,9,256,256]{3,2,1,0:T(8,128)(2,1)S(1)} %copy-done, bf16[32,1024]{1,0:T(8,128)(2,1)S(1)} %constant_dynamic-update-slice_fusion.refs_0_, ...), custom_call_target="tpu_custom_call" | custom-call | tf_op jit(solution)/shard_map/near/pallas_call | solution.py:259
  18.0 0.8 %collective-permute-start.9 = (bf16[2,16,256]{2,1,0:T(8,128)(2,1)S(1)}, bf16[2,16,256]{2,1,0:T(8,128)(2,1)S(1)}, u32[]{:S(2)}, u32[]{:S(2)}) collective-permute-start(bf16[2,16,256]{2,1,0:T(8,128)(2,1)S(1)} %get-tuple-element.17), channel_id=1, source_target_pairs={{0,2},{1,3},{2,0},{3,1},{4,6},{5,7},{6,4},{7,5},{8,10},{9,11},{10,... | collective-permute-start | bytes 49160 | tf_op jit(solution)/shard_map/ppermute | solution.py:20
  18.7 1.3 %collective-permute-start.2 = (bf16[1,2,16,128]{3,2,1,0:T(8,128)(2,1)S(1)}, bf16[1,2,16,128]{3,2,1,0:T(8,128)(2,1)S(1)}, u32[]{:S(2)}, u32[]{:S(2)}) collective-permute-start(bf16[1,2,16,128]{3,2,1,0:T(8,128)(2,1)S(1)} %dynamic-slice_convert_fusion.1), channel_id=1, source_target_pairs={{0,8},{4,12},{8,0},{12,4},{16,24},{20,28},{24,16},{28,20},{1,9},{5... | collective-permute-start | bytes 24584 | tf_op jit(solution)/shard_map/ppermute | solution.py:20
  20.1 1.7 %collective-permute-done.9.refs_1_ = bf16[2,16,256]{2,1,0:T(8,128)(2,1)S(1)} collective-permute-done((bf16[2,16,256]{2,1,0:T(8,128)(2,1)S(1)}, bf16[2,16,256]{2,1,0:T(8,128)(2,1)S(1)}, u32[]{:S(2)}, u32[]{:S(2)}) %collective-permute-start.9) | collective-permute-done | bytes 16416 | tf_op jit(solution)/shard_map/ppermute | solution.py:20
  21.8 0.0 collective-permute-start.10
  21.8 0.6 %collective-permute-done.2.got = bf16[1,2,16,128]{3,2,1,0:T(8,128)(2,1)S(1)} collective-permute-done((bf16[1,2,16,128]{3,2,1,0:T(8,128)(2,1)S(1)}, bf16[1,2,16,128]{3,2,1,0:T(8,128)(2,1)S(1)}, u32[]{:S(2)}, u32[]{:S(2)}) %collective-permute-start.2) | collective-permute-done | bytes 8224 | tf_op jit(solution)/shard_map/ppermute | solution.py:20
  22.4 0.6 %collective-permute-done.10.refs_2_ = bf16[2,16,256]{2,1,0:T(8,128)(2,1)S(1)} collective-permute-done((bf16[2,16,256]{2,1,0:T(8,128)(2,1)S(1)}, bf16[2,16,256]{2,1,0:T(8,128)(2,1)S(1)}, u32[]{:S(2)}, u32[]{:S(2)}) %collective-permute-start.10) | collective-permute-done | bytes 16416 | tf_op jit(solution)/shard_map/ppermute | solution.py:20
  23.0 0.9 %finish.1 = bf16[16,1024]{1,0:T(8,128)(2,1)} custom-call(f32[1,2,16,128]{3,2,1,0:T(8,128)S(1)} %constant_dynamic-slice_fusion.keep, bf16[1,2,16,128]{3,2,1,0:T(8,128)(2,1)S(1)} %collective-permute-done.2.got, bf16[256,1024]{1,0:T(8,128)(2,1)S(1)} %get-tuple-element.14.high_in, bf16[256,1024]{1,0:T(8,128)(2,1)S(1)} %get-tuple-element.15.low_in, ...), custom_call_target="tpu_custom_call" | custom-call | tf_op jit(solution)/shard_map/finish/pallas_call | solution.py:295
  (15 shorter events, 0.1 us)
Async XLA Ops:
  0.0 7.0 %copy-start.5 = (bf16[16,1024]{1,0:T(8,128)(2,1)S(1)}, bf16[16,1024]{1,0:T(8,128)(2,1)}, u32[]{:S(2)}) copy-start(bf16[16,1024]{1,0:T(8,128)(2,1)} %vectors_in.1) | copy-start | bytes 98308
  0.0 14.7 %copy-start.2 = (bf16[6,32,32]{2,1,0:T(8,128)(2,1)S(1)}, bf16[6,32,32]{2,1,0:T(8,128)(2,1)}, u32[]{:S(2)}) copy-start(bf16[6,32,32]{2,1,0:T(8,128)(2,1)} %transfer.1) | copy-start | bytes 36868
  0.0 14.7 %copy-start.1 = (bf16[4,32,256]{2,1,0:T(8,128)(2,1)S(1)}, bf16[4,32,256]{2,1,0:T(8,128)(2,1)}, u32[]{:S(2)}) copy-start(bf16[4,32,256]{2,1,0:T(8,128)(2,1)} %basis.1) | copy-start | bytes 196612
  0.0 17.1 %copy-start.4 = (s32[1,9]{1,0:T(1,128)S(1)}, s32[1,9]{1,0:T(1,128)}, u32[]{:S(2)}) copy-start(s32[1,9]{1,0:T(1,128)} %alive.1) | copy-start | bytes 112
  0.0 17.1 %copy-start.3 = (s32[1,9]{1,0:T(1,128)S(1)}, s32[1,9]{1,0:T(1,128)}, u32[]{:S(2)}) copy-start(s32[1,9]{1,0:T(1,128)} %columns.1) | copy-start | bytes 112
  0.0 17.1 %copy-start = (bf16[1,9,256,256]{3,2,1,0:T(8,128)(2,1)S(1)}, bf16[1,9,256,256]{3,2,1,0:T(8,128)(2,1)}, u32[]{:S(2)}) copy-start(bf16[1,9,256,256]{3,2,1,0:T(8,128)(2,1)} %blocks.1) | copy-start | bytes 3538948
  0.0 7.0 %collective-permute-start.3 = (bf16[16,1024]{1,0:T(8,128)(2,1)}, bf16[16,1024]{1,0:T(8,128)(2,1)S(1)}, u32[]{:S(2)}, u32[]{:S(2)}) collective-permute-start(bf16[16,1024]{1,0:T(8,128)(2,1)} %vectors_in.1), channel_id=1, source_target_pairs={{0,2},{1,3},{2,0},{3,1},{4,6},{5,7},{6,4},{7,5},{8,10},{9,11},{10,... | collective-permute-start | bytes 98312 | tf_op jit(solution)/shard_map/ppermute | solution.py:20
  5.4 6.6 %collective-permute-start = (bf16[4,2,16,128]{3,2,1,0:T(8,128)(2,1)S(1)}, bf16[4,2,16,128]{3,2,1,0:T(8,128)(2,1)S(1)}, u32[]{:S(2)}, u32[]{:S(2)}) collective-permute-start(bf16[4,2,16,128]{3,2,1,0:T(8,128)(2,1)S(1)} %get-tuple-element.13), channel_id=1, source_target_pairs={{0,4},{4,0},{8,12},{12,8},{16,20},{20,16},{24,28},{28,24},{1,5},{5... | collective-permute-start | bytes 98312 | tf_op jit(solution)/shard_map/ppermute | solution.py:20
  7.0 8.3 %collective-permute-start.7 = (bf16[32,1024]{1,0:T(8,128)(2,1)S(1)}, bf16[32,1024]{1,0:T(8,128)(2,1)S(1)}, u32[]{:S(2)}, u32[]{:S(2)}) collective-permute-start(bf16[32,1024]{1,0:T(8,128)(2,1)S(1)} %constant_dynamic-update-slice_fusion.refs_0_), channel_id=1, source_target_pairs={{0,0},{4,8},{8,4},{12,16},{16,12},{20,24},{24,20},{28,28},{1,1},{5... | collective-permute-start | bytes 196616 | tf_op jit(solution)/shard_map/ppermute | solution.py:27
  7.7 8.1 %collective-permute-start.5 = (bf16[32,1024]{1,0:T(8,128)(2,1)S(1)}, bf16[32,1024]{1,0:T(8,128)(2,1)S(1)}, u32[]{:S(2)}, u32[]{:S(2)}) collective-permute-start(bf16[32,1024]{1,0:T(8,128)(2,1)S(1)} %constant_dynamic-update-slice_fusion.refs_0_), channel_id=1, source_target_pairs={{0,4},{4,0},{8,12},{12,8},{16,20},{20,16},{24,28},{28,24},{1,5},{5... | collective-permute-start | bytes 196616 | tf_op jit(solution)/shard_map/ppermute | solution.py:20
  12.0 4.7 %collective-permute-start.1 = (bf16[2,2,16,128]{3,2,1,0:T(8,128)(2,1)S(1)}, bf16[2,2,16,128]{3,2,1,0:T(8,128)(2,1)S(1)}, u32[]{:S(2)}, u32[]{:S(2)}) collective-permute-start(bf16[2,2,16,128]{3,2,1,0:T(8,128)(2,1)S(1)} %fusion), channel_id=1, source_target_pairs={{0,16},{4,20},{8,24},{12,28},{16,0},{20,4},{24,8},{28,12},{1,17},{... | collective-permute-start | bytes 49160 | tf_op jit(solution)/shard_map/ppermute | solution.py:20
  15.2 1.5 %collective-permute-start.4 = (bf16[32,1024]{1,0:T(8,128)(2,1)S(1)}, bf16[32,1024]{1,0:T(8,128)(2,1)S(1)}, u32[]{:S(2)}, u32[]{:S(2)}) collective-permute-start(bf16[32,1024]{1,0:T(8,128)(2,1)S(1)} %constant_dynamic-update-slice_fusion.refs_0_), channel_id=1, source_target_pairs={{0,1},{1,0},{2,3},{3,2},{4,5},{5,4},{6,7},{7,6},{8,9},{9,8},{10,11... | collective-permute-start | bytes 196616 | tf_op jit(solution)/shard_map/ppermute | solution.py:20
  15.3 1.5 %collective-permute-start.8 = (bf16[32,1024]{1,0:T(8,128)(2,1)S(1)}, bf16[32,1024]{1,0:T(8,128)(2,1)S(1)}, u32[]{:S(2)}, u32[]{:S(2)}) collective-permute-start(bf16[32,1024]{1,0:T(8,128)(2,1)S(1)} %collective-permute-done.7.refs_4_), channel_id=1, source_target_pairs={{0,1},{1,0},{2,3},{3,2},{4,5},{5,4},{6,7},{7,6},{8,9},{9,8},{10,11... | collective-permute-start | bytes 196616 | tf_op jit(solution)/shard_map/ppermute | solution.py:20
  15.8 1.3 %collective-permute-start.6 = (bf16[32,1024]{1,0:T(8,128)(2,1)S(1)}, bf16[32,1024]{1,0:T(8,128)(2,1)S(1)}, u32[]{:S(2)}, u32[]{:S(2)}) collective-permute-start(bf16[32,1024]{1,0:T(8,128)(2,1)S(1)} %collective-permute-done.5.refs_2_), channel_id=1, source_target_pairs={{0,1},{1,0},{2,3},{3,2},{4,5},{5,4},{6,7},{7,6},{8,9},{9,8},{10,11... | collective-permute-start | bytes 196616 | tf_op jit(solution)/shard_map/ppermute | solution.py:20
  18.0 3.8 %collective-permute-start.9 = (bf16[2,16,256]{2,1,0:T(8,128)(2,1)S(1)}, bf16[2,16,256]{2,1,0:T(8,128)(2,1)S(1)}, u32[]{:S(2)}, u32[]{:S(2)}) collective-permute-start(bf16[2,16,256]{2,1,0:T(8,128)(2,1)S(1)} %get-tuple-element.17), channel_id=1, source_target_pairs={{0,2},{1,3},{2,0},{3,1},{4,6},{5,7},{6,4},{7,5},{8,10},{9,11},{10,... | collective-permute-start | bytes 49160 | tf_op jit(solution)/shard_map/ppermute | solution.py:20
  18.7 3.7 %collective-permute-start.2 = (bf16[1,2,16,128]{3,2,1,0:T(8,128)(2,1)S(1)}, bf16[1,2,16,128]{3,2,1,0:T(8,128)(2,1)S(1)}, u32[]{:S(2)}, u32[]{:S(2)}) collective-permute-start(bf16[1,2,16,128]{3,2,1,0:T(8,128)(2,1)S(1)} %dynamic-slice_convert_fusion.1), channel_id=1, source_target_pairs={{0,8},{4,12},{8,0},{12,4},{16,24},{20,28},{24,16},{28,20},{1,9},{5... | collective-permute-start | bytes 24584 | tf_op jit(solution)/shard_map/ppermute | solution.py:20
  21.8 1.2 %collective-permute-start.10 = (bf16[2,16,256]{2,1,0:T(8,128)(2,1)S(1)}, bf16[2,16,256]{2,1,0:T(8,128)(2,1)S(1)}, u32[]{:S(2)}, u32[]{:S(2)}) collective-permute-start(bf16[2,16,256]{2,1,0:T(8,128)(2,1)S(1)} %pad_maximum_fusion), channel_id=1, source_target_pairs={{0,1},{1,0},{2,3},{3,2},{4,5},{5,4},{6,7},{7,6},{8,9},{9,8},{10,11... | collective-permute-start | bytes 49160 | tf_op jit(solution)/shard_map/ppermute | solution.py:20

commit v4 on v3

--- a/solution.py
+++ b/solution.py
@@ -20,11 +20,18 @@
     return lax.ppermute(values, axis, [(i, i ^ bit) for i in range(count)])
 
 
-def beside(values, axis):
-    count = lax.axis_size(axis)
-    other = [((i + 1) ^ 1) - 1 for i in range(count)]
-    pairs = [(i, j if 0 <= j < count else i) for i, j in enumerate(other)]
-    return lax.ppermute(values, axis, pairs)
+def beside(values):
+    leaf_count, sub_count = lax.axis_size("leaf"), lax.axis_size("sub")
+    pairs = []
+    for leaf in range(leaf_count):
+        other = ((leaf + 1) ^ 1) - 1
+        for sub in range(sub_count):
+            here = leaf * sub_count + sub
+            if 0 <= other < leaf_count:
+                pairs.append((here, other * sub_count + sub))
+            else:
+                pairs.append((here, leaf * sub_count + (sub ^ 1)))
+    return lax.ppermute(values, ("leaf", "sub"), pairs)
 
 
 def bits_of(count):
@@ -54,7 +61,7 @@
 
 
 def expand_kernel(
-    leaf_count, targets_in, alive_in, vectors_in, basis_in, transfer_in, coupling_in, keep, send, *scratch
+    leaf_count, targets_in, alive_in, vectors_in, basis_in, transfer_in, coupling_in, keep, send, own, *scratch
 ):
     targets, alive, vectors, basis, transfer, coupling, done, *sums = scratch
     subtree, rank, leaf_size = basis.shape
@@ -95,6 +102,7 @@
                     for j in range(starts[number], starts[number] + size):
                         sums[c][tree * clusters + j] = zero
     copies[0].wait()
+    own[...] = vectors[...]
     copies[1].wait()
     hats = [
         dot(vectors[:, j * leaf_size : (j + 1) * leaf_size], basis[j], ((1,), (1,)))
@@ -166,9 +174,10 @@
         out_shape=[
             jax.ShapeDtypeStruct(shape, jnp.float32),
             jax.ShapeDtypeStruct(shape, jnp.bfloat16),
+            jax.ShapeDtypeStruct(vectors.shape, vectors.dtype),
         ],
         in_specs=[HBM] * 6,
-        out_specs=[VMEM, VMEM],
+        out_specs=[VMEM] * 3,
         scratch_shapes=[
             pltpu.SMEM(targets.shape, targets.dtype),
             pltpu.SMEM(alive.shape, alive.dtype),
@@ -318,9 +327,9 @@
     me = lax.axis_index("leaf")
     rows = vectors.shape[0]
     bits = bits_of(sub_count)
-    pair = jnp.concatenate([vectors, flip(vectors, "sub", bits[0])], axis=0)
-    keep, send = expand(vectors, leaf_basis, transfer, coupling, far_targets, far_mask)
-    trees = [[pair], [flip(pair, "leaf", 1)], [beside(pair, "leaf")]]
+    keep, send, own = expand(vectors, leaf_basis, transfer, coupling, far_targets, far_mask)
+    pair = jnp.concatenate([own, flip(vectors, "sub", bits[0])], axis=0)
+    trees = [[pair], [flip(pair, "leaf", 1)], [beside(pair)]]
     got = flip(send, "leaf", 1)
     order = [0, bits[0]]
     for bit in bits[1:]:

time: 24.1 us -> 22.1 us (0.917)
  starting transfers between devices: 15 us -> 13.1 us
    ppermute x10, starting transfers between devices: 14.4 us -> 13.1 us  [flip(): return lax.ppermute(values, axis, [(i, i ^ bit) for i in range(count)])]
    ppermute x1, starting transfers between devices: 0.66 us -> 0.07 us  [beside(): return lax.ppermute(values, ('leaf', 'sub'), pairs)]
  transfers between devices with their start and end apart: 11 -> 11, of which waited for: 5 -> 5; matrix products, arithmetic and copies ran while one was open for 0% -> 0% of each run, Pallas kernels for 12% -> 13%
where the time goes in v4:
time: 22.1 us; the launch traced here: 22 us
  starting transfers between devices  13.1 us (59%)
  Pallas kernels  4.61 us (21%)
  waiting for transfers between devices  4.02 us (18%)
    ppermute x10, starting transfers between devices, flip(): return lax.ppermute(values, axis, [(i, i ^ bit) for i in range(count)])  13.1 us
    ppermute x10, waiting for transfers between devices, flip(): return lax.ppermute(values, axis, [(i, i ^ bit) for i in range(count)])  4.02 us
    pallas_call x1, Pallas kernels, expand(): pl.pallas_call(functools.partial(expand_kernel, leaf_count), out_shape=[j...  2.31 us
    pallas_call x1, Pallas kernels, finish(): pl.pallas_call(functools.partial(finish_kernel, sources), out_shape=jax.S...  0.94 us
    pallas_call x1, Pallas kernels, near(): pl.pallas_call(functools.partial(near_kernel, places, sub_count), out_sha...  0.89 us
    pallas_call x1, Pallas kernels, operator(): pl.pallas_call(operator_kernel, out_shape=[shape, shape], in_specs=[VMEM,...  0.47 us
  transfers between devices with their start and end apart: 11, of which 5 were waited for; matrix products, arithmetic and copies ran while one was open for 0% of the time, Pallas kernels for 13%

profile of v4, /device:TPU:0, one launch (start us, length us, event | category | flops | bytes accessed | tf_op | source)
XLA Modules:
  0.0 22.0 jit_solution(10109408774124974127)
XLA Ops:
  0.0 0.0 copy-start.2
  0.0 3.0 %collective-permute-start.3 = (bf16[16,1024]{1,0:T(8,128)(2,1)}, bf16[16,1024]{1,0:T(8,128)(2,1)S(1)}, u32[]{:S(2)}, u32[]{:S(2)}) collective-permute-start(bf16[16,1024]{1,0:T(8,128)(2,1)} %vectors_in.1), channel_id=1, source_target_pairs={{0,2},{1,3},{2,0},{3,1},{4,6},{5,7},{6,4},{7,5},{8,10},{9,11},{10,... | collective-permute-start | bytes 98312 | tf_op jit(solution)/shard_map/ppermute | solution.py:20
  3.1 2.3 %expand.1 = (f32[4,2,16,128]{3,2,1,0:T(8,128)S(1)}, bf16[4,2,16,128]{3,2,1,0:T(8,128)(2,1)S(1)}, bf16[16,1024]{1,0:T(8,128)(2,1)S(1)}) custom-call(s32[7,27]{1,0:T(8,128)} %targets_in.1, s32[7,27]{1,0:T(8,128)} %alive_in.1, bf16[16,1024]{1,0:T(8,128)(2,1)} %vectors_in.1, bf16[4,32,256]{2,1,0:T(8,128)(2,1)} %basis.1, bf16[6,32,32]{2,1,0:T(8,128)(2,1)} %transfer.1, ...), custom_call_target="tpu_custom_call" | custom-call | tf_op jit(solution)/shard_map/expand/pallas_call | solution.py:172
  5.4 1.6 %collective-permute-start = (bf16[4,2,16,128]{3,2,1,0:T(8,128)(2,1)S(1)}, bf16[4,2,16,128]{3,2,1,0:T(8,128)(2,1)S(1)}, u32[]{:S(2)}, u32[]{:S(2)}) collective-permute-start(bf16[4,2,16,128]{3,2,1,0:T(8,128)(2,1)S(1)} %get-tuple-element.14), channel_id=1, source_target_pairs={{0,4},{4,0},{8,12},{12,8},{16,20},{20,16},{24,28},{28,24},{1,5},{5... | collective-permute-start | bytes 98312 | tf_op jit(solution)/shard_map/ppermute | solution.py:20
  7.0 0.0 collective-permute-done.3
  7.0 0.1 collective-permute-start.7
  7.0 3.0 %collective-permute-start.5 = (bf16[32,1024]{1,0:T(8,128)(2,1)S(1)}, bf16[32,1024]{1,0:T(8,128)(2,1)S(1)}, u32[]{:S(2)}, u32[]{:S(2)}) collective-permute-start(bf16[32,1024]{1,0:T(8,128)(2,1)S(1)} %constant_dynamic-update-slice_fusion.refs_0_), channel_id=1, source_target_pairs={{0,4},{4,0},{8,12},{12,8},{16,20},{20,16},{24,28},{28,24},{1,5},{5... | collective-permute-start | bytes 196616 | tf_op jit(solution)/shard_map/ppermute | solution.py:20
  10.1 0.0 collective-permute-done
  10.1 2.7 %collective-permute-start.1 = (bf16[2,2,16,128]{3,2,1,0:T(8,128)(2,1)S(1)}, bf16[2,2,16,128]{3,2,1,0:T(8,128)(2,1)S(1)}, u32[]{:S(2)}, u32[]{:S(2)}) collective-permute-start(bf16[2,2,16,128]{3,2,1,0:T(8,128)(2,1)S(1)} %fusion), channel_id=1, source_target_pairs={{0,16},{4,20},{8,24},{12,28},{16,0},{20,4},{24,8},{28,12},{1,17},{... | collective-permute-start | bytes 49160 | tf_op jit(solution)/shard_map/ppermute | solution.py:20
  12.8 0.0 copy-done.2
  12.8 0.0 copy-done.1
  12.8 0.5 %operator.1 = (bf16[256,1024]{1,0:T(8,128)(2,1)S(1)}, bf16[256,1024]{1,0:T(8,128)(2,1)S(1)}) custom-call(bf16[6,32,32]{2,1,0:T(8,128)(2,1)S(1)} %copy-done.2, bf16[4,32,256]{2,1,0:T(8,128)(2,1)S(1)} %copy-done.1), custom_call_target="tpu_custom_call" | custom-call | tf_op jit(solution)/shard_map/operator/pallas_call | solution.py:224
  13.3 0.1 collective-permute-start.4
  13.4 0.0 collective-permute-done.7.refs_4_
  13.4 0.5 %collective-permute-start.8 = (bf16[32,1024]{1,0:T(8,128)(2,1)S(1)}, bf16[32,1024]{1,0:T(8,128)(2,1)S(1)}, u32[]{:S(2)}, u32[]{:S(2)}) collective-permute-start(bf16[32,1024]{1,0:T(8,128)(2,1)S(1)} %collective-permute-done.7.refs_4_), channel_id=1, source_target_pairs={{0,1},{1,0},{2,3},{3,2},{4,5},{5,4},{6,7},{7,6},{8,9},{9,8},{10,11... | collective-permute-start | bytes 196616 | tf_op jit(solution)/shard_map/ppermute | solution.py:20
  13.9 0.0 collective-permute-done.5.refs_2_
  13.9 0.1 collective-permute-start.6
  13.9 0.9 %collective-permute-done.1 = bf16[2,2,16,128]{3,2,1,0:T(8,128)(2,1)S(1)} collective-permute-done((bf16[2,2,16,128]{3,2,1,0:T(8,128)(2,1)S(1)}, bf16[2,2,16,128]{3,2,1,0:T(8,128)(2,1)S(1)}, u32[]{:S(2)}, u32[]{:S(2)}) %collective-permute-start.1) | collective-permute-done | bytes 16416 | tf_op jit(solution)/shard_map/ppermute | solution.py:20
  14.8 0.0 collective-permute-done.4.refs_1_
  14.8 0.0 collective-permute-done.8.refs_5_
  14.8 0.3 %collective-permute-done.6.refs_3_ = bf16[32,1024]{1,0:T(8,128)(2,1)S(1)} collective-permute-done((bf16[32,1024]{1,0:T(8,128)(2,1)S(1)}, bf16[32,1024]{1,0:T(8,128)(2,1)S(1)}, u32[]{:S(2)}, u32[]{:S(2)}) %collective-permute-start.6) | collective-permute-done | bytes 65568 | tf_op jit(solution)/shard_map/ppermute | solution.py:20
  15.1 0.0 copy-done.4
  15.1 0.0 copy-done.3
  15.1 0.0 copy-done
  15.1 0.9 %near.1 = (f32[1,16,256]{2,1,0:T(8,128)S(1)}, bf16[2,16,256]{2,1,0:T(8,128)(2,1)S(1)}, bf16[1,16,256]{2,1,0:T(8,128)(2,1)S(1)}) custom-call(s32[1,9]{1,0:T(1,128)S(1)} %copy-done.3, s32[1,9]{1,0:T(1,128)S(1)} %copy-done.4, bf16[1,9,256,256]{3,2,1,0:T(8,128)(2,1)S(1)} %copy-done, bf16[32,1024]{1,0:T(8,128)(2,1)S(1)} %constant_dynamic-update-slice_fusion.refs_0_, ...), custom_call_target="tpu_custom_call" | custom-call | tf_op jit(solution)/shard_map/near/pallas_call | solution.py:268
  16.0 0.7 %collective-permute-start.9 = (bf16[2,16,256]{2,1,0:T(8,128)(2,1)S(1)}, bf16[2,16,256]{2,1,0:T(8,128)(2,1)S(1)}, u32[]{:S(2)}, u32[]{:S(2)}) collective-permute-start(bf16[2,16,256]{2,1,0:T(8,128)(2,1)S(1)} %get-tuple-element.19), channel_id=1, source_target_pairs={{0,2},{1,3},{2,0},{3,1},{4,6},{5,7},{6,4},{7,5},{8,10},{9,11},{10,... | collective-permute-start | bytes 49160 | tf_op jit(solution)/shard_map/ppermute | solution.py:20
  16.8 1.3 %collective-permute-start.2 = (bf16[1,2,16,128]{3,2,1,0:T(8,128)(2,1)S(1)}, bf16[1,2,16,128]{3,2,1,0:T(8,128)(2,1)S(1)}, u32[]{:S(2)}, u32[]{:S(2)}) collective-permute-start(bf16[1,2,16,128]{3,2,1,0:T(8,128)(2,1)S(1)} %dynamic-slice_convert_fusion.1), channel_id=1, source_target_pairs={{0,8},{4,12},{8,0},{12,4},{16,24},{20,28},{24,16},{28,20},{1,9},{5... | collective-permute-start | bytes 24584 | tf_op jit(solution)/shard_map/ppermute | solution.py:20
  18.1 1.7 %collective-permute-done.9.refs_1_ = bf16[2,16,256]{2,1,0:T(8,128)(2,1)S(1)} collective-permute-done((bf16[2,16,256]{2,1,0:T(8,128)(2,1)S(1)}, bf16[2,16,256]{2,1,0:T(8,128)(2,1)S(1)}, u32[]{:S(2)}, u32[]{:S(2)}) %collective-permute-start.9) | collective-permute-done | bytes 16416 | tf_op jit(solution)/shard_map/ppermute | solution.py:20
  19.8 0.0 collective-permute-start.10
  19.9 0.6 %collective-permute-done.2.got = bf16[1,2,16,128]{3,2,1,0:T(8,128)(2,1)S(1)} collective-permute-done((bf16[1,2,16,128]{3,2,1,0:T(8,128)(2,1)S(1)}, bf16[1,2,16,128]{3,2,1,0:T(8,128)(2,1)S(1)}, u32[]{:S(2)}, u32[]{:S(2)}) %collective-permute-start.2) | collective-permute-done | bytes 8224 | tf_op jit(solution)/shard_map/ppermute | solution.py:20
  20.4 0.6 %collective-permute-done.10.refs_2_ = bf16[2,16,256]{2,1,0:T(8,128)(2,1)S(1)} collective-permute-done((bf16[2,16,256]{2,1,0:T(8,128)(2,1)S(1)}, bf16[2,16,256]{2,1,0:T(8,128)(2,1)S(1)}, u32[]{:S(2)}, u32[]{:S(2)}) %collective-permute-start.10) | collective-permute-done | bytes 16416 | tf_op jit(solution)/shard_map/ppermute | solution.py:20
  21.0 0.9 %finish.1 = bf16[16,1024]{1,0:T(8,128)(2,1)} custom-call(f32[1,2,16,128]{3,2,1,0:T(8,128)S(1)} %constant_dynamic-slice_fusion.keep, bf16[1,2,16,128]{3,2,1,0:T(8,128)(2,1)S(1)} %collective-permute-done.2.got, bf16[256,1024]{1,0:T(8,128)(2,1)S(1)} %get-tuple-element.15.high_in, bf16[256,1024]{1,0:T(8,128)(2,1)S(1)} %get-tuple-element.16.low_in, ...), custom_call_target="tpu_custom_call" | custom-call | tf_op jit(solution)/shard_map/finish/pallas_call | solution.py:304
  (13 shorter events, 0.1 us)
Async XLA Ops:
  0.0 12.8 %copy-start.2 = (bf16[6,32,32]{2,1,0:T(8,128)(2,1)S(1)}, bf16[6,32,32]{2,1,0:T(8,128)(2,1)}, u32[]{:S(2)}) copy-start(bf16[6,32,32]{2,1,0:T(8,128)(2,1)} %transfer.1) | copy-start | bytes 36868
  0.0 12.8 %copy-start.1 = (bf16[4,32,256]{2,1,0:T(8,128)(2,1)S(1)}, bf16[4,32,256]{2,1,0:T(8,128)(2,1)}, u32[]{:S(2)}) copy-start(bf16[4,32,256]{2,1,0:T(8,128)(2,1)} %basis.1) | copy-start | bytes 196612
  0.0 15.1 %copy-start.4 = (s32[1,9]{1,0:T(1,128)S(1)}, s32[1,9]{1,0:T(1,128)}, u32[]{:S(2)}) copy-start(s32[1,9]{1,0:T(1,128)} %alive.1) | copy-start | bytes 112
  0.0 15.1 %copy-start.3 = (s32[1,9]{1,0:T(1,128)S(1)}, s32[1,9]{1,0:T(1,128)}, u32[]{:S(2)}) copy-start(s32[1,9]{1,0:T(1,128)} %columns.1) | copy-start | bytes 112
  0.0 15.1 %copy-start = (bf16[1,9,256,256]{3,2,1,0:T(8,128)(2,1)S(1)}, bf16[1,9,256,256]{3,2,1,0:T(8,128)(2,1)}, u32[]{:S(2)}) copy-start(bf16[1,9,256,256]{3,2,1,0:T(8,128)(2,1)} %blocks.1) | copy-start | bytes 3538948
  0.0 6.9 %collective-permute-start.3 = (bf16[16,1024]{1,0:T(8,128)(2,1)}, bf16[16,1024]{1,0:T(8,128)(2,1)S(1)}, u32[]{:S(2)}, u32[]{:S(2)}) collective-permute-start(bf16[16,1024]{1,0:T(8,128)(2,1)} %vectors_in.1), channel_id=1, source_target_pairs={{0,2},{1,3},{2,0},{3,1},{4,6},{5,7},{6,4},{7,5},{8,10},{9,11},{10,... | collective-permute-start | bytes 98312 | tf_op jit(solution)/shard_map/ppermute | solution.py:20
  5.4 4.7 %collective-permute-start = (bf16[4,2,16,128]{3,2,1,0:T(8,128)(2,1)S(1)}, bf16[4,2,16,128]{3,2,1,0:T(8,128)(2,1)S(1)}, u32[]{:S(2)}, u32[]{:S(2)}) collective-permute-start(bf16[4,2,16,128]{3,2,1,0:T(8,128)(2,1)S(1)} %get-tuple-element.14), channel_id=1, source_target_pairs={{0,4},{4,0},{8,12},{12,8},{16,20},{20,16},{24,28},{28,24},{1,5},{5... | collective-permute-start | bytes 98312 | tf_op jit(solution)/shard_map/ppermute | solution.py:20
  7.0 6.4 %collective-permute-start.7 = (bf16[32,1024]{1,0:T(8,128)(2,1)S(1)}, bf16[32,1024]{1,0:T(8,128)(2,1)S(1)}, u32[]{:S(2)}, u32[]{:S(2)}) collective-permute-start(bf16[32,1024]{1,0:T(8,128)(2,1)S(1)} %constant_dynamic-update-slice_fusion.refs_0_), channel_id=1, source_target_pairs={{0,1},{1,0},{2,3},{3,2},{4,8},{5,9},{6,10},{7,11},{8,4},{9,5},{10,... | collective-permute-start | bytes 196616 | tf_op jit(solution)/shard_map/ppermute | solution.py:34
  7.0 6.8 %collective-permute-start.5 = (bf16[32,1024]{1,0:T(8,128)(2,1)S(1)}, bf16[32,1024]{1,0:T(8,128)(2,1)S(1)}, u32[]{:S(2)}, u32[]{:S(2)}) collective-permute-start(bf16[32,1024]{1,0:T(8,128)(2,1)S(1)} %constant_dynamic-update-slice_fusion.refs_0_), channel_id=1, source_target_pairs={{0,4},{4,0},{8,12},{12,8},{16,20},{20,16},{24,28},{28,24},{1,5},{5... | collective-permute-start | bytes 196616 | tf_op jit(solution)/shard_map/ppermute | solution.py:20
  10.1 4.7 %collective-permute-start.1 = (bf16[2,2,16,128]{3,2,1,0:T(8,128)(2,1)S(1)}, bf16[2,2,16,128]{3,2,1,0:T(8,128)(2,1)S(1)}, u32[]{:S(2)}, u32[]{:S(2)}) collective-permute-start(bf16[2,2,16,128]{3,2,1,0:T(8,128)(2,1)S(1)} %fusion), channel_id=1, source_target_pairs={{0,16},{4,20},{8,24},{12,28},{16,0},{20,4},{24,8},{28,12},{1,17},{... | collective-permute-start | bytes 49160 | tf_op jit(solution)/shard_map/ppermute | solution.py:20
  13.3 1.5 %collective-permute-start.4 = (bf16[32,1024]{1,0:T(8,128)(2,1)S(1)}, bf16[32,1024]{1,0:T(8,128)(2,1)S(1)}, u32[]{:S(2)}, u32[]{:S(2)}) collective-permute-start(bf16[32,1024]{1,0:T(8,128)(2,1)S(1)} %constant_dynamic-update-slice_fusion.refs_0_), channel_id=1, source_target_pairs={{0,1},{1,0},{2,3},{3,2},{4,5},{5,4},{6,7},{7,6},{8,9},{9,8},{10,11... | collective-permute-start | bytes 196616 | tf_op jit(solution)/shard_map/ppermute | solution.py:20
  13.4 1.5 %collective-permute-start.8 = (bf16[32,1024]{1,0:T(8,128)(2,1)S(1)}, bf16[32,1024]{1,0:T(8,128)(2,1)S(1)}, u32[]{:S(2)}, u32[]{:S(2)}) collective-permute-start(bf16[32,1024]{1,0:T(8,128)(2,1)S(1)} %collective-permute-done.7.refs_4_), channel_id=1, source_target_pairs={{0,1},{1,0},{2,3},{3,2},{4,5},{5,4},{6,7},{7,6},{8,9},{9,8},{10,11... | collective-permute-start | bytes 196616 | tf_op jit(solution)/shard_map/ppermute | solution.py:20
  13.9 1.3 %collective-permute-start.6 = (bf16[32,1024]{1,0:T(8,128)(2,1)S(1)}, bf16[32,1024]{1,0:T(8,128)(2,1)S(1)}, u32[]{:S(2)}, u32[]{:S(2)}) collective-permute-start(bf16[32,1024]{1,0:T(8,128)(2,1)S(1)} %collective-permute-done.5.refs_2_), channel_id=1, source_target_pairs={{0,1},{1,0},{2,3},{3,2},{4,5},{5,4},{6,7},{7,6},{8,9},{9,8},{10,11... | collective-permute-start | bytes 196616 | tf_op jit(solution)/shard_map/ppermute | solution.py:20
  16.0 3.8 %collective-permute-start.9 = (bf16[2,16,256]{2,1,0:T(8,128)(2,1)S(1)}, bf16[2,16,256]{2,1,0:T(8,128)(2,1)S(1)}, u32[]{:S(2)}, u32[]{:S(2)}) collective-permute-start(bf16[2,16,256]{2,1,0:T(8,128)(2,1)S(1)} %get-tuple-element.19), channel_id=1, source_target_pairs={{0,2},{1,3},{2,0},{3,1},{4,6},{5,7},{6,4},{7,5},{8,10},{9,11},{10,... | collective-permute-start | bytes 49160 | tf_op jit(solution)/shard_map/ppermute | solution.py:20
  16.8 3.7 %collective-permute-start.2 = (bf16[1,2,16,128]{3,2,1,0:T(8,128)(2,1)S(1)}, bf16[1,2,16,128]{3,2,1,0:T(8,128)(2,1)S(1)}, u32[]{:S(2)}, u32[]{:S(2)}) collective-permute-start(bf16[1,2,16,128]{3,2,1,0:T(8,128)(2,1)S(1)} %dynamic-slice_convert_fusion.1), channel_id=1, source_target_pairs={{0,8},{4,12},{8,0},{12,4},{16,24},{20,28},{24,16},{28,20},{1,9},{5... | collective-permute-start | bytes 24584 | tf_op jit(solution)/shard_map/ppermute | solution.py:20
  19.8 1.2 %collective-permute-start.10 = (bf16[2,16,256]{2,1,0:T(8,128)(2,1)S(1)}, bf16[2,16,256]{2,1,0:T(8,128)(2,1)S(1)}, u32[]{:S(2)}, u32[]{:S(2)}) collective-permute-start(bf16[2,16,256]{2,1,0:T(8,128)(2,1)S(1)} %pad_maximum_fusion), channel_id=1, source_target_pairs={{0,1},{1,0},{2,3},{3,2},{4,5},{5,4},{6,7},{7,6},{8,9},{9,8},{10,11... | collective-permute-start | bytes 49160 | tf_op jit(solution)/shard_map/ppermute | solution.py:20

commit v5 on v4

--- a/solution.py
+++ b/solution.py
@@ -231,40 +231,61 @@
     )(transfer, basis)
 
 
-def near_kernel(places, sub_count, columns, alive, blocks, *refs):
-    window, outs, pieces = refs[-1], refs[-1 - len(places) : -1], refs[: -1 - len(places)]
-    per_tree = len(pieces) // 3
-    rows, points = pieces[0].shape
+def arrange_kernel(columns, alive, blocks, out):
     count, leaf_size = blocks.shape[1:3]
-    subtree = points // leaf_size
-    for tree in range(3):
-        for part in range(per_tree):
-            window[tree, part * rows : (part + 1) * rows, :] = pieces[tree * per_tree + part][...]
+    subtree = (out.shape[0] - 1) // 3
     me = lax.axis_index("leaf")
     first = me * subtree
     partner = (me ^ 1) * subtree
-    total = None
+    zero = jnp.zeros((leaf_size, blocks.shape[3]), out.dtype)
+    for place in range(3 * subtree):
+        out[place] = zero
     for k in range(count):
         column = columns[0, k]
         own_tree = (column >= first) & (column < first + subtree)
         partner_tree = (column >= partner) & (column < partner + subtree)
         tree = jnp.where(own_tree, 0, jnp.where(partner_tree, 1, 2))
-        place = lax.rem(column, subtree)
-        start = pl.multiple_of(place * leaf_size, leaf_size)
-        taken = window[tree, :, pl.ds(start, leaf_size)]
-        live = alive[0, k].astype(jnp.float32).astype(jnp.bfloat16)
-        product = dot(taken * live, blocks[0, k])
-        total = product if total is None else total + product
+        place = tree * subtree + lax.rem(column, subtree)
+        out[jnp.where(alive[0, k] == 1, place, 3 * subtree)] = blocks[0, k]
+
+
+def arrange(blocks, columns, alive, subtree):
+    return pl.pallas_call(
+        arrange_kernel,
+        out_shape=jax.ShapeDtypeStruct((3 * subtree + 1, *blocks.shape[2:]), blocks.dtype),
+        in_specs=[SMEM, SMEM, VMEM],
+        out_specs=VMEM,
+        compiler_params=PARAMS,
+        name="arrange",
+    )(columns, alive, blocks)
+
+
+def near_kernel(places, sub_count, blocks, *refs):
+    outs, pieces = refs[-len(places) :], refs[: -len(places)]
+    middles, outers = pieces[0::2], pieces[1::2]
+    rows, points = middles[0].shape
+    leaf_size = blocks.shape[1]
+    subtree = points // leaf_size
+    total = None
+    for tree in range(3):
+        for j in range(subtree):
+            columns = slice(j * leaf_size, (j + 1) * leaf_size)
+            if tree == 0:
+                taken = [ref[:, columns] for ref in middles]
+            else:
+                taken = [ref[(tree - 1) * rows : tree * rows, columns] for ref in outers]
+            product = dot(jnp.concatenate(taken, axis=0), blocks[tree * subtree + j])
+            total = product if total is None else total + product
     size = total.shape[0] // sub_count
     for out, groups in zip(outs, places):
         for number, group in enumerate(groups):
             out[number] = total[group * size : (group + 1) * size].astype(out.dtype)
 
 
-def near(pieces, blocks, columns, alive, rows, places):
+def near(pieces, blocks, rows, places):
     sub_count = lax.axis_size("sub")
-    leaf_size = blocks.shape[2]
-    points = pieces[0].shape[1]
+    leaf_size = blocks.shape[1]
+    flat = [array for pair in pieces for array in pair]
     return pl.pallas_call(
         functools.partial(near_kernel, places, sub_count),
         out_shape=[
@@ -273,21 +294,36 @@
             )
             for number, groups in enumerate(places)
         ],
-        in_specs=[SMEM, SMEM] + [VMEM] * (1 + len(pieces)),
+        in_specs=[VMEM] * (1 + len(flat)),
         out_specs=[VMEM] * len(places),
-        scratch_shapes=[pltpu.VMEM((3, rows * sub_count, points), jnp.bfloat16)],
         compiler_params=PARAMS,
         name="near",
-    )(columns, alive, blocks, *pieces)
-
-
-def finish_kernel(sources, keep, got, high_in, low_in, *refs):
-    nears, out = refs[:-1], refs[-1]
+    )(blocks, *flat)
+
+
+def far_kernel(keep, got, high_in, low_in, out):
     incoming = jnp.concatenate(
         [keep[0, g] + got[0, g].astype(jnp.float32) for g in range(keep.shape[1])], axis=1
     )
     high, low = halves(incoming)
-    far = dot(high, high_in[...]) + dot(low, high_in[...]) + dot(high, low_in[...])
+    rows = high.shape[0]
+    both = dot(jnp.concatenate([high, low], axis=0), high_in[...])
+    out[...] = both[:rows] + both[rows:] + dot(high, low_in[...])
+
+
+def far(keep, got, high, low):
+    return pl.pallas_call(
+        far_kernel,
+        out_shape=jax.ShapeDtypeStruct((keep.shape[2], high.shape[1]), jnp.float32),
+        in_specs=[VMEM] * 4,
+        out_specs=VMEM,
+        compiler_params=PARAMS,
+        name="far",
+    )(keep, got, high, low)
+
+
+def finish_kernel(sources, far_in, *refs):
+    nears, out = refs[:-1], refs[-1]
     me = lax.axis_index("sub")
     leaf_size = nears[0].shape[2]
     pieces = [(source, nears[at][row].astype(jnp.float32)) for source, at, row in sources]
@@ -296,19 +332,18 @@
         for source, values in pieces[1:]:
             piece = jnp.where((me ^ source) == j, values, piece)
         columns = slice(j * leaf_size, (j + 1) * leaf_size)
-        out[:, columns] = (piece + far[:, columns]).astype(out.dtype)
-
-
-def finish(keep, got, high, low, nears, sources):
-    rows = nears[0].shape[1]
+        out[:, columns] = (piece + far_in[:, columns]).astype(out.dtype)
+
+
+def finish(far_part, nears, sources):
     return pl.pallas_call(
         functools.partial(finish_kernel, sources),
-        out_shape=jax.ShapeDtypeStruct((rows, high.shape[1]), jnp.bfloat16),
-        in_specs=[VMEM] * (4 + len(nears)),
+        out_shape=jax.ShapeDtypeStruct(far_part.shape, jnp.bfloat16),
+        in_specs=[VMEM] * (1 + len(nears)),
         out_specs=VMEM,
         compiler_params=PARAMS,
         name="finish",
-    )(keep, got, high, low, *nears)
+    )(far_part, *nears)
 
 
 def local(
@@ -329,13 +364,16 @@
     bits = bits_of(sub_count)
     keep, send, own = expand(vectors, leaf_basis, transfer, coupling, far_targets, far_mask)
     pair = jnp.concatenate([own, flip(vectors, "sub", bits[0])], axis=0)
-    trees = [[pair], [flip(pair, "leaf", 1)], [beside(pair)]]
+    sides = jnp.concatenate([flip(pair, "leaf", 1), beside(pair)], axis=0)
     got = flip(send, "leaf", 1)
     order = [0, bits[0]]
+    pieces = [(pair, sides)]
     for bit in bits[1:]:
-        trees = [parts + [flip(part, "sub", bit) for part in parts] for parts in trees]
+        pieces = pieces + [
+            (flip(middle, "sub", bit), flip(outer, "sub", bit))
+            for middle, outer in pieces
+        ]
         order = order + [number ^ bit for number in order]
-    pieces = [part for parts in trees for part in parts]
     high, low = operator(transfer, leaf_basis, keep.shape[1] * LANES)
     for size in bits_of(leaf_count)[:-1]:
         total = (keep + got.astype(keep.dtype)).reshape(2, size // 2, *keep.shape[1:])
@@ -346,7 +384,8 @@
     places = [[order.index(0)]] + [
         [order.index(home) for home in range(bit, 2 * bit)] for bit in bits
     ]
-    made = near(pieces, near_blocks, near_cols, near_mask, rows, places)
+    blocks = arrange(near_blocks, near_cols, near_mask, leaf_basis.shape[0])
+    made = near(pieces, blocks, rows, places)
     arrays = list(made)
     pool = {0: [(0, 0, 0)]}
     for number, bit in enumerate(bits):
@@ -363,7 +402,8 @@
             pool[home ^ bit].append((source ^ bit, len(arrays) - 1, row))
     used = sorted({at for _, at, _ in pool[0]})
     sources = [(source, used.index(at), row) for source, at, row in pool[0]]
-    return finish(keep, got, high, low, [arrays[at] for at in used], sources)
+    far_part = far(keep, got, high, low)
+    return finish(far_part, [arrays[at] for at in used], sources)
 
 
 def solution(mesh):

time: 22.1 us -> 22.5 us (1.018)
    pallas_call x0 -> x2, Pallas kernels: none -> 0.98 us  [the longest x1 0.72 us: arrange(): pl.pallas_call(arrange_kernel, out_shape=jax.ShapeDtypeStruct((3 * subtre...]
    pallas_call x1, Pallas kernels: 0.89 us -> 0.39 us  [near(): pl.pallas_call(functools.partial(near_kernel, places, sub_count), out_sha...]
    ppermute x10 -> x9, starting transfers between devices: 13.1 us -> 12.6 us  [flip(): return lax.ppermute(values, axis, [(i, i ^ bit) for i in range(count)])]
    ppermute x1, starting transfers between devices: 0.07 us -> 0.5 us  [beside(): return lax.ppermute(values, ('leaf', 'sub'), pairs)]
    pallas_call x1, Pallas kernels: 0.94 us -> 0.63 us  [finish(): pl.pallas_call(functools.partial(finish_kernel, sources), out_shape=jax.S...]
    ppermute x10 -> x9, waiting for transfers between devices: 4.02 us -> 4.15 us  [flip(): return lax.ppermute(values, axis, [(i, i ^ bit) for i in range(count)])]
  transfers between devices with their start and end apart: 11 -> 10, of which waited for: 5 -> 4; matrix products, arithmetic and copies ran while one was open for 0% -> 0% of each run, Pallas kernels for 13% -> 17%
where the time goes in v5:
time: 22.5 us; the launch traced here: 22.3 us
  starting transfers between devices  13.1 us (58%)
  Pallas kernels  4.79 us (21%)
  waiting for transfers between devices  4.16 us (18%)
    ppermute x9, starting transfers between devices, flip(): return lax.ppermute(values, axis, [(i, i ^ bit) for i in range(count)])  12.6 us
    ppermute x9, waiting for transfers between devices, flip(): return lax.ppermute(values, axis, [(i, i ^ bit) for i in range(count)])  4.15 us
    pallas_call x1, Pallas kernels, expand(): pl.pallas_call(functools.partial(expand_kernel, leaf_count), out_shape=[j...  2.31 us
    pallas_call x1, Pallas kernels, arrange(): pl.pallas_call(arrange_kernel, out_shape=jax.ShapeDtypeStruct((3 * subtre...  0.72 us
    pallas_call x1, Pallas kernels, finish(): pl.pallas_call(functools.partial(finish_kernel, sources), out_shape=jax.S...  0.63 us
    ppermute x1, starting transfers between devices, beside(): return lax.ppermute(values, ('leaf', 'sub'), pairs)  0.5 us
    pallas_call x1, Pallas kernels, operator(): pl.pallas_call(operator_kernel, out_shape=[shape, shape], in_specs=[VMEM,...  0.47 us
  transfers between devices with their start and end apart: 10, of which 4 were waited for; matrix products, arithmetic and copies ran while one was open for 0% of the time, Pallas kernels for 17%

profile of v5, /device:TPU:0, one launch (start us, length us, event | category | flops | bytes accessed | tf_op | source)
XLA Modules:
  0.0 22.3 jit_solution(8657791727159674950)
XLA Ops:
  0.0 0.0 copy-start.2
  0.0 3.0 %collective-permute-start.3 = (bf16[16,1024]{1,0:T(8,128)(2,1)}, bf16[16,1024]{1,0:T(8,128)(2,1)S(1)}, u32[]{:S(2)}, u32[]{:S(2)}) collective-permute-start(bf16[16,1024]{1,0:T(8,128)(2,1)} %vectors_in.1), channel_id=1, source_target_pairs={{0,2},{1,3},{2,0},{3,1},{4,6},{5,7},{6,4},{7,5},{8,10},{9,11},{10,... | collective-permute-start | bytes 98312 | tf_op jit(solution)/shard_map/ppermute | solution.py:20
  3.1 2.3 %expand.1 = (f32[4,2,16,128]{3,2,1,0:T(8,128)S(1)}, bf16[4,2,16,128]{3,2,1,0:T(8,128)(2,1)S(1)}, bf16[16,1024]{1,0:T(8,128)(2,1)S(1)}) custom-call(s32[7,27]{1,0:T(8,128)} %targets_in.1, s32[7,27]{1,0:T(8,128)} %alive_in.1, bf16[16,1024]{1,0:T(8,128)(2,1)} %vectors_in.1, bf16[4,32,256]{2,1,0:T(8,128)(2,1)} %basis.1, bf16[6,32,32]{2,1,0:T(8,128)(2,1)} %transfer.1, ...), custom_call_target="tpu_custom_call" | custom-call | tf_op jit(solution)/shard_map/expand/pallas_call | solution.py:172
  5.4 1.6 %collective-permute-start = (bf16[4,2,16,128]{3,2,1,0:T(8,128)(2,1)S(1)}, bf16[4,2,16,128]{3,2,1,0:T(8,128)(2,1)S(1)}, u32[]{:S(2)}, u32[]{:S(2)}) collective-permute-start(bf16[4,2,16,128]{3,2,1,0:T(8,128)(2,1)S(1)} %get-tuple-element.14), channel_id=1, source_target_pairs={{0,4},{4,0},{8,12},{12,8},{16,20},{20,16},{24,28},{28,24},{1,5},{5... | collective-permute-start | bytes 98312 | tf_op jit(solution)/shard_map/ppermute | solution.py:20
  7.0 0.0 copy-done.2
  7.0 0.0 copy-done.1
  7.0 0.5 %operator.1 = (bf16[256,1024]{1,0:T(8,128)(2,1)S(1)}, bf16[256,1024]{1,0:T(8,128)(2,1)S(1)}) custom-call(bf16[6,32,32]{2,1,0:T(8,128)(2,1)S(1)} %copy-done.2, bf16[4,32,256]{2,1,0:T(8,128)(2,1)S(1)} %copy-done.1), custom_call_target="tpu_custom_call" | custom-call | tf_op jit(solution)/shard_map/operator/pallas_call | solution.py:224
  7.5 0.0 copy-done.4
  7.5 0.0 copy-done.3
  7.5 0.0 copy-done
  7.5 0.7 %arrange.1.blocks = bf16[13,256,256]{2,1,0:T(8,128)(2,1)S(1)} custom-call(s32[1,9]{1,0:T(1,128)S(1)} %copy-done.3, s32[1,9]{1,0:T(1,128)S(1)} %copy-done.4, bf16[1,9,256,256]{3,2,1,0:T(8,128)(2,1)S(1)} %copy-done), custom_call_target="tpu_custom_call" | custom-call | tf_op jit(solution)/shard_map/arrange/pallas_call | solution.py:253
  8.2 0.0 collective-permute-done.3
  8.3 0.1 collective-permute-start.6
  8.3 0.5 %collective-permute-start.5 = (bf16[32,1024]{1,0:T(8,128)(2,1)S(1)}, bf16[32,1024]{1,0:T(8,128)(2,1)S(1)}, u32[]{:S(2)}, u32[]{:S(2)}) collective-permute-start(bf16[32,1024]{1,0:T(8,128)(2,1)S(1)} %constant_dynamic-update-slice_fusion.refs_0_), channel_id=1, source_target_pairs={{0,1},{1,0},{2,3},{3,2},{4,8},{5,9},{6,10},{7,11},{8,4},{9,5},{10,... | collective-permute-start | bytes 196616 | tf_op jit(solution)/shard_map/ppermute | solution.py:34
  8.8 2.6 %collective-permute-start.4 = (bf16[32,1024]{1,0:T(8,128)(2,1)S(1)}, bf16[32,1024]{1,0:T(8,128)(2,1)S(1)}, u32[]{:S(2)}, u32[]{:S(2)}) collective-permute-start(bf16[32,1024]{1,0:T(8,128)(2,1)S(1)} %constant_dynamic-update-slice_fusion.refs_0_), channel_id=1, source_target_pairs={{0,4},{4,0},{8,12},{12,8},{16,20},{20,16},{24,28},{28,24},{1,5},{5... | collective-permute-start | bytes 196616 | tf_op jit(solution)/shard_map/ppermute | solution.py:20
  11.4 0.0 collective-permute-done
  11.5 2.7 %collective-permute-start.1 = (bf16[2,2,16,128]{3,2,1,0:T(8,128)(2,1)S(1)}, bf16[2,2,16,128]{3,2,1,0:T(8,128)(2,1)S(1)}, u32[]{:S(2)}, u32[]{:S(2)}) collective-permute-start(bf16[2,2,16,128]{3,2,1,0:T(8,128)(2,1)S(1)} %fusion), channel_id=1, source_target_pairs={{0,16},{4,20},{8,24},{12,28},{16,0},{20,4},{24,8},{28,12},{1,17},{... | collective-permute-start | bytes 49160 | tf_op jit(solution)/shard_map/ppermute | solution.py:20
  14.1 0.0 collective-permute-done.4
  14.2 0.0 collective-permute-done.5
  14.2 0.1 collective-permute-start.7
  14.3 2.0 %collective-permute-done.1 = bf16[2,2,16,128]{3,2,1,0:T(8,128)(2,1)S(1)} collective-permute-done((bf16[2,2,16,128]{3,2,1,0:T(8,128)(2,1)S(1)}, bf16[2,2,16,128]{3,2,1,0:T(8,128)(2,1)S(1)}, u32[]{:S(2)}, u32[]{:S(2)}) %collective-permute-start.1) | collective-permute-done | bytes 16416 | tf_op jit(solution)/shard_map/ppermute | solution.py:20
  16.3 0.0 collective-permute-done.6.refs_2_
  16.3 0.0 collective-permute-done.7.refs_3_
  16.3 0.4 %near.1 = (f32[1,16,256]{2,1,0:T(8,128)S(1)}, bf16[2,16,256]{2,1,0:T(8,128)(2,1)S(1)}, bf16[1,16,256]{2,1,0:T(8,128)(2,1)S(1)}) custom-call(bf16[13,256,256]{2,1,0:T(8,128)(2,1)S(1)} %arrange.1.blocks, bf16[32,1024]{1,0:T(8,128)(2,1)S(1)} %constant_dynamic-update-slice_fusion.refs_0_, bf16[64,1024]{1,0:T(8,128)(2,1)S(1)} %constant_dynamic-update-slice_fusion.2.refs_1_, ...), custom_call_target="tpu_custom_call" | custom-call | tf_op jit(solution)/shard_map/near/pallas_call | solution.py:289
  16.7 0.7 %collective-permute-start.8 = (bf16[2,16,256]{2,1,0:T(8,128)(2,1)S(1)}, bf16[2,16,256]{2,1,0:T(8,128)(2,1)S(1)}, u32[]{:S(2)}, u32[]{:S(2)}) collective-permute-start(bf16[2,16,256]{2,1,0:T(8,128)(2,1)S(1)} %get-tuple-element.19), channel_id=1, source_target_pairs={{0,2},{1,3},{2,0},{3,1},{4,6},{5,7},{6,4},{7,5},{8,10},{9,11},{10,... | collective-permute-start | bytes 49160 | tf_op jit(solution)/shard_map/ppermute | solution.py:20
  17.5 1.8 %collective-permute-start.2 = (bf16[1,2,16,128]{3,2,1,0:T(8,128)(2,1)S(1)}, bf16[1,2,16,128]{3,2,1,0:T(8,128)(2,1)S(1)}, u32[]{:S(2)}, u32[]{:S(2)}) collective-permute-start(bf16[1,2,16,128]{3,2,1,0:T(8,128)(2,1)S(1)} %dynamic-slice_convert_fusion.1), channel_id=1, source_target_pairs={{0,8},{4,12},{8,0},{12,4},{16,24},{20,28},{24,16},{28,20},{1,9},{5... | collective-permute-start | bytes 24584 | tf_op jit(solution)/shard_map/ppermute | solution.py:20
  19.3 1.2 %collective-permute-done.8.refs_1_ = bf16[2,16,256]{2,1,0:T(8,128)(2,1)S(1)} collective-permute-done((bf16[2,16,256]{2,1,0:T(8,128)(2,1)S(1)}, bf16[2,16,256]{2,1,0:T(8,128)(2,1)S(1)}, u32[]{:S(2)}, u32[]{:S(2)}) %collective-permute-start.8) | collective-permute-done | bytes 16416 | tf_op jit(solution)/shard_map/ppermute | solution.py:20
  20.5 0.0 collective-permute-start.9
  20.5 0.6 %collective-permute-done.2.got = bf16[1,2,16,128]{3,2,1,0:T(8,128)(2,1)S(1)} collective-permute-done((bf16[1,2,16,128]{3,2,1,0:T(8,128)(2,1)S(1)}, bf16[1,2,16,128]{3,2,1,0:T(8,128)(2,1)S(1)}, u32[]{:S(2)}, u32[]{:S(2)}) %collective-permute-start.2) | collective-permute-done | bytes 8224 | tf_op jit(solution)/shard_map/ppermute | solution.py:20
  21.1 0.3 %far.1.far_in = f32[16,1024]{1,0:T(8,128)S(1)} custom-call(f32[1,2,16,128]{3,2,1,0:T(8,128)S(1)} %constant_dynamic-slice_fusion.keep, bf16[1,2,16,128]{3,2,1,0:T(8,128)(2,1)S(1)} %collective-permute-done.2.got, bf16[256,1024]{1,0:T(8,128)(2,1)S(1)} %get-tuple-element.15.high_in, bf16[256,1024]{1,0:T(8,128)(2,1)S(1)} %get-tuple-element.16.low_in), custom_call_target="tpu_custom_call" | custom-call | tf_op jit(solution)/shard_map/far/pallas_call | solution.py:315
  21.4 0.3 %collective-permute-done.9.refs_2_ = bf16[2,16,256]{2,1,0:T(8,128)(2,1)S(1)} collective-permute-done((bf16[2,16,256]{2,1,0:T(8,128)(2,1)S(1)}, bf16[2,16,256]{2,1,0:T(8,128)(2,1)S(1)}, u32[]{:S(2)}, u32[]{:S(2)}) %collective-permute-start.9) | collective-permute-done | bytes 16416 | tf_op jit(solution)/shard_map/ppermute | solution.py:20
  21.7 0.6 %finish.1 = bf16[16,1024]{1,0:T(8,128)(2,1)} custom-call(f32[16,1024]{1,0:T(8,128)S(1)} %far.1.far_in, f32[1,16,256]{2,1,0:T(8,128)S(1)} %get-tuple-element.18.refs_0_, bf16[2,16,256]{2,1,0:T(8,128)(2,1)S(1)} %collective-permute-done.8.refs_1_, bf16[2,16,256]{2,1,0:T(8,128)(2,1)S(1)} %collective-permute-done.9.refs_2_), custom_call_target="tpu_custom_call" | custom-call | tf_op jit(solution)/shard_map/finish/pallas_call | solution.py:339
  (15 shorter events, 0.1 us)
Async XLA Ops:
  0.0 7.0 %copy-start.2 = (bf16[6,32,32]{2,1,0:T(8,128)(2,1)S(1)}, bf16[6,32,32]{2,1,0:T(8,128)(2,1)}, u32[]{:S(2)}) copy-start(bf16[6,32,32]{2,1,0:T(8,128)(2,1)} %transfer.1) | copy-start | bytes 36868
  0.0 7.0 %copy-start.1 = (bf16[4,32,256]{2,1,0:T(8,128)(2,1)S(1)}, bf16[4,32,256]{2,1,0:T(8,128)(2,1)}, u32[]{:S(2)}) copy-start(bf16[4,32,256]{2,1,0:T(8,128)(2,1)} %basis.1) | copy-start | bytes 196612
  0.0 7.5 %copy-start.4 = (s32[1,9]{1,0:T(1,128)S(1)}, s32[1,9]{1,0:T(1,128)}, u32[]{:S(2)}) copy-start(s32[1,9]{1,0:T(1,128)} %alive.1) | copy-start | bytes 112
  0.0 7.5 %copy-start.3 = (s32[1,9]{1,0:T(1,128)S(1)}, s32[1,9]{1,0:T(1,128)}, u32[]{:S(2)}) copy-start(s32[1,9]{1,0:T(1,128)} %columns.1) | copy-start | bytes 112
  0.0 7.5 %copy-start = (bf16[1,9,256,256]{3,2,1,0:T(8,128)(2,1)S(1)}, bf16[1,9,256,256]{3,2,1,0:T(8,128)(2,1)}, u32[]{:S(2)}) copy-start(bf16[1,9,256,256]{3,2,1,0:T(8,128)(2,1)} %blocks.1) | copy-start | bytes 3538948
  0.0 8.2 %collective-permute-start.3 = (bf16[16,1024]{1,0:T(8,128)(2,1)}, bf16[16,1024]{1,0:T(8,128)(2,1)S(1)}, u32[]{:S(2)}, u32[]{:S(2)}) collective-permute-start(bf16[16,1024]{1,0:T(8,128)(2,1)} %vectors_in.1), channel_id=1, source_target_pairs={{0,2},{1,3},{2,0},{3,1},{4,6},{5,7},{6,4},{7,5},{8,10},{9,11},{10,... | collective-permute-start | bytes 98312 | tf_op jit(solution)/shard_map/ppermute | solution.py:20
  5.4 6.1 %collective-permute-start = (bf16[4,2,16,128]{3,2,1,0:T(8,128)(2,1)S(1)}, bf16[4,2,16,128]{3,2,1,0:T(8,128)(2,1)S(1)}, u32[]{:S(2)}, u32[]{:S(2)}) collective-permute-start(bf16[4,2,16,128]{3,2,1,0:T(8,128)(2,1)S(1)} %get-tuple-element.14), channel_id=1, source_target_pairs={{0,4},{4,0},{8,12},{12,8},{16,20},{20,16},{24,28},{28,24},{1,5},{5... | collective-permute-start | bytes 98312 | tf_op jit(solution)/shard_map/ppermute | solution.py:20
  8.3 8.0 %collective-permute-start.6 = (bf16[32,1024]{1,0:T(8,128)(2,1)S(1)}, bf16[32,1024]{1,0:T(8,128)(2,1)S(1)}, u32[]{:S(2)}, u32[]{:S(2)}) collective-permute-start(bf16[32,1024]{1,0:T(8,128)(2,1)S(1)} %constant_dynamic-update-slice_fusion.refs_0_), channel_id=1, source_target_pairs={{0,1},{1,0},{2,3},{3,2},{4,5},{5,4},{6,7},{7,6},{8,9},{9,8},{10,11... | collective-permute-start | bytes 196616 | tf_op jit(solution)/shard_map/ppermute | solution.py:20
  8.3 5.8 %collective-permute-start.5 = (bf16[32,1024]{1,0:T(8,128)(2,1)S(1)}, bf16[32,1024]{1,0:T(8,128)(2,1)S(1)}, u32[]{:S(2)}, u32[]{:S(2)}) collective-permute-start(bf16[32,1024]{1,0:T(8,128)(2,1)S(1)} %constant_dynamic-update-slice_fusion.refs_0_), channel_id=1, source_target_pairs={{0,1},{1,0},{2,3},{3,2},{4,8},{5,9},{6,10},{7,11},{8,4},{9,5},{10,... | collective-permute-start | bytes 196616 | tf_op jit(solution)/shard_map/ppermute | solution.py:34
  8.8 5.3 %collective-permute-start.4 = (bf16[32,1024]{1,0:T(8,128)(2,1)S(1)}, bf16[32,1024]{1,0:T(8,128)(2,1)S(1)}, u32[]{:S(2)}, u32[]{:S(2)}) collective-permute-start(bf16[32,1024]{1,0:T(8,128)(2,1)S(1)} %constant_dynamic-update-slice_fusion.refs_0_), channel_id=1, source_target_pairs={{0,4},{4,0},{8,12},{12,8},{16,20},{20,16},{24,28},{28,24},{1,5},{5... | collective-permute-start | bytes 196616 | tf_op jit(solution)/shard_map/ppermute | solution.py:20
  11.5 4.8 %collective-permute-start.1 = (bf16[2,2,16,128]{3,2,1,0:T(8,128)(2,1)S(1)}, bf16[2,2,16,128]{3,2,1,0:T(8,128)(2,1)S(1)}, u32[]{:S(2)}, u32[]{:S(2)}) collective-permute-start(bf16[2,2,16,128]{3,2,1,0:T(8,128)(2,1)S(1)} %fusion), channel_id=1, source_target_pairs={{0,16},{4,20},{8,24},{12,28},{16,0},{20,4},{24,8},{28,12},{1,17},{... | collective-permute-start | bytes 49160 | tf_op jit(solution)/shard_map/ppermute | solution.py:20
  14.2 2.1 %collective-permute-start.7 = (bf16[64,1024]{1,0:T(8,128)(2,1)S(1)}, bf16[64,1024]{1,0:T(8,128)(2,1)S(1)}, u32[]{:S(2)}, u32[]{:S(2)}) collective-permute-start(bf16[64,1024]{1,0:T(8,128)(2,1)S(1)} %constant_dynamic-update-slice_fusion.2.refs_1_), channel_id=1, source_target_pairs={{0,1},{1,0},{2,3},{3,2},{4,5},{5,4},{6,7},{7,6},{8,9},{9,8},{10,11... | collective-permute-start | bytes 393224 | tf_op jit(solution)/shard_map/ppermute | solution.py:20
  16.7 3.8 %collective-permute-start.8 = (bf16[2,16,256]{2,1,0:T(8,128)(2,1)S(1)}, bf16[2,16,256]{2,1,0:T(8,128)(2,1)S(1)}, u32[]{:S(2)}, u32[]{:S(2)}) collective-permute-start(bf16[2,16,256]{2,1,0:T(8,128)(2,1)S(1)} %get-tuple-element.19), channel_id=1, source_target_pairs={{0,2},{1,3},{2,0},{3,1},{4,6},{5,7},{6,4},{7,5},{8,10},{9,11},{10,... | collective-permute-start | bytes 49160 | tf_op jit(solution)/shard_map/ppermute | solution.py:20
  17.5 3.7 %collective-permute-start.2 = (bf16[1,2,16,128]{3,2,1,0:T(8,128)(2,1)S(1)}, bf16[1,2,16,128]{3,2,1,0:T(8,128)(2,1)S(1)}, u32[]{:S(2)}, u32[]{:S(2)}) collective-permute-start(bf16[1,2,16,128]{3,2,1,0:T(8,128)(2,1)S(1)} %dynamic-slice_convert_fusion.1), channel_id=1, source_target_pairs={{0,8},{4,12},{8,0},{12,4},{16,24},{20,28},{24,16},{28,20},{1,9},{5... | collective-permute-start | bytes 24584 | tf_op jit(solution)/shard_map/ppermute | solution.py:20
  20.5 1.2 %collective-permute-start.9 = (bf16[2,16,256]{2,1,0:T(8,128)(2,1)S(1)}, bf16[2,16,256]{2,1,0:T(8,128)(2,1)S(1)}, u32[]{:S(2)}, u32[]{:S(2)}) collective-permute-start(bf16[2,16,256]{2,1,0:T(8,128)(2,1)S(1)} %pad_maximum_fusion), channel_id=1, source_target_pairs={{0,1},{1,0},{2,3},{3,2},{4,5},{5,4},{6,7},{7,6},{8,9},{9,8},{10,11... | collective-permute-start | bytes 49160 | tf_op jit(solution)/shard_map/ppermute | solution.py:20

commit v6 on v5

--- a/solution.py
+++ b/solution.py
@@ -42,6 +42,11 @@
     return bits
 
 
+def stages_of(leaf_count):
+    bits = bits_of(leaf_count)[::-1]
+    return bits[1:] + bits[:1]
+
+
 def levels_of(subtree):
     sizes = []
     while subtree >= 1:
@@ -69,7 +74,8 @@
     nodes = leaf_count * clusters
     sizes, starts = levels_of(subtree)
     rows = vectors.shape[0]
-    parity = lax.axis_index("leaf") % 2
+    bit = stages_of(leaf_count)[0]
+    mine = (lax.axis_index("leaf") & bit) // bit
     copies = [
         pltpu.make_async_copy(source, target, done.at[number])
         for number, (source, target) in enumerate(
@@ -149,7 +155,8 @@
         return groups
 
     def emit(half, carry):
-        for out, tree in ((keep, 2 * half + parity), (send, 2 * half + 1 - parity)):
+        first = (half // bit) * 2 * bit + half % bit
+        for out, tree in ((keep, first + mine * bit), (send, first + (1 - mine) * bit)):
             for number, group in enumerate(gathered(tree)):
                 out[half, number] = group.astype(out.dtype)
         return carry
@@ -365,7 +372,8 @@
     keep, send, own = expand(vectors, leaf_basis, transfer, coupling, far_targets, far_mask)
     pair = jnp.concatenate([own, flip(vectors, "sub", bits[0])], axis=0)
     sides = jnp.concatenate([flip(pair, "leaf", 1), beside(pair)], axis=0)
-    got = flip(send, "leaf", 1)
+    stages = stages_of(leaf_count)
+    got = flip(send, "leaf", stages[0])
     order = [0, bits[0]]
     pieces = [(pair, sides)]
     for bit in bits[1:]:
@@ -375,12 +383,12 @@
         ]
         order = order + [number ^ bit for number in order]
     high, low = operator(transfer, leaf_basis, keep.shape[1] * LANES)
-    for size in bits_of(leaf_count)[:-1]:
-        total = (keep + got.astype(keep.dtype)).reshape(2, size // 2, *keep.shape[1:])
-        mine = (me & size) // size
+    for bit in sorted(stages[1:], reverse=True):
+        total = (keep + got.astype(keep.dtype)).reshape(2, -1, *keep.shape[1:])
+        mine = (me & bit) // bit
         keep = lax.dynamic_index_in_dim(total, mine, 0, keepdims=False)
         send = lax.dynamic_index_in_dim(total, 1 - mine, 0, keepdims=False)
-        got = flip(send.astype(jnp.bfloat16), "leaf", size)
+        got = flip(send.astype(jnp.bfloat16), "leaf", bit)
     places = [[order.index(0)]] + [
         [order.index(home) for home in range(bit, 2 * bit)] for bit in bits
     ]

time: 22.5 us -> 21.3 us (0.947)
  starting transfers between devices: 13.1 us -> 12.3 us
  waiting for transfers between devices: 4.16 us -> 3.8 us
    ppermute x9, starting transfers between devices: 12.6 us -> 11.8 us  [flip(): return lax.ppermute(values, axis, [(i, i ^ bit) for i in range(count)])]
    ppermute x9, waiting for transfers between devices: 4.15 us -> 3.79 us  [flip(): return lax.ppermute(values, axis, [(i, i ^ bit) for i in range(count)])]
  transfers between devices with their start and end apart: 10 -> 10, of which waited for: 4 -> 5; matrix products, arithmetic and copies ran while one was open for 0% -> 0% of each run, Pallas kernels for 17% -> 18%
where the time goes in v6:
time: 21.3 us; the launch traced here: 21.2 us
  starting transfers between devices  12.3 us (58%)
  Pallas kernels  4.8 us (23%)
  waiting for transfers between devices  3.8 us (18%)
    ppermute x9, starting transfers between devices, flip(): return lax.ppermute(values, axis, [(i, i ^ bit) for i in range(count)])  11.8 us
    ppermute x9, waiting for transfers between devices, flip(): return lax.ppermute(values, axis, [(i, i ^ bit) for i in range(count)])  3.79 us
    pallas_call x1, Pallas kernels, expand(): pl.pallas_call(functools.partial(expand_kernel, leaf_count), out_shape=[j...  2.32 us
    pallas_call x1, Pallas kernels, arrange(): pl.pallas_call(arrange_kernel, out_shape=jax.ShapeDtypeStruct((3 * subtre...  0.72 us
    pallas_call x1, Pallas kernels, finish(): pl.pallas_call(functools.partial(finish_kernel, sources), out_shape=jax.S...  0.63 us
    ppermute x1, starting transfers between devices, beside(): return lax.ppermute(values, ('leaf', 'sub'), pairs)  0.5 us
    pallas_call x1, Pallas kernels, operator(): pl.pallas_call(operator_kernel, out_shape=[shape, shape], in_specs=[VMEM,...  0.47 us
  transfers between devices with their start and end apart: 10, of which 5 were waited for; matrix products, arithmetic and copies ran while one was open for 0% of the time, Pallas kernels for 18%

profile of v6, /device:TPU:0, one launch (start us, length us, event | category | flops | bytes accessed | tf_op | source)
XLA Modules:
  0.0 21.2 jit_solution(5428164693005965935)
XLA Ops:
  0.0 0.0 copy-start.2
  0.0 3.0 %collective-permute-start.3 = (bf16[16,1024]{1,0:T(8,128)(2,1)}, bf16[16,1024]{1,0:T(8,128)(2,1)S(1)}, u32[]{:S(2)}, u32[]{:S(2)}) collective-permute-start(bf16[16,1024]{1,0:T(8,128)(2,1)} %vectors_in.1), channel_id=1, source_target_pairs={{0,2},{1,3},{2,0},{3,1},{4,6},{5,7},{6,4},{7,5},{8,10},{9,11},{10,... | collective-permute-start | bytes 98312 | tf_op jit(solution)/shard_map/ppermute | solution.py:20
  3.1 2.3 %expand.1 = (f32[4,2,16,128]{3,2,1,0:T(8,128)S(1)}, bf16[4,2,16,128]{3,2,1,0:T(8,128)(2,1)S(1)}, bf16[16,1024]{1,0:T(8,128)(2,1)S(1)}) custom-call(s32[7,27]{1,0:T(8,128)} %targets_in.1, s32[7,27]{1,0:T(8,128)} %alive_in.1, bf16[16,1024]{1,0:T(8,128)(2,1)} %vectors_in.1, bf16[4,32,256]{2,1,0:T(8,128)(2,1)} %basis.1, bf16[6,32,32]{2,1,0:T(8,128)(2,1)} %transfer.1, ...), custom_call_target="tpu_custom_call" | custom-call | tf_op jit(solution)/shard_map/expand/pallas_call | solution.py:179
  5.4 1.6 %collective-permute-start = (bf16[4,2,16,128]{3,2,1,0:T(8,128)(2,1)S(1)}, bf16[4,2,16,128]{3,2,1,0:T(8,128)(2,1)S(1)}, u32[]{:S(2)}, u32[]{:S(2)}) collective-permute-start(bf16[4,2,16,128]{3,2,1,0:T(8,128)(2,1)S(1)} %get-tuple-element.14), channel_id=1, source_target_pairs={{0,8},{4,12},{8,0},{12,4},{16,24},{20,28},{24,16},{28,20},{1,9},{5... | collective-permute-start | bytes 98312 | tf_op jit(solution)/shard_map/ppermute | solution.py:20
  7.0 0.0 copy-done.2
  7.0 0.0 copy-done.1
  7.1 0.5 %operator.1 = (bf16[256,1024]{1,0:T(8,128)(2,1)S(1)}, bf16[256,1024]{1,0:T(8,128)(2,1)S(1)}) custom-call(bf16[6,32,32]{2,1,0:T(8,128)(2,1)S(1)} %copy-done.2, bf16[4,32,256]{2,1,0:T(8,128)(2,1)S(1)} %copy-done.1), custom_call_target="tpu_custom_call" | custom-call | tf_op jit(solution)/shard_map/operator/pallas_call | solution.py:231
  7.5 0.0 copy-done.4
  7.6 0.0 copy-done.3
  7.6 0.0 copy-done
  7.6 0.7 %arrange.1.blocks = bf16[13,256,256]{2,1,0:T(8,128)(2,1)S(1)} custom-call(s32[1,9]{1,0:T(1,128)S(1)} %copy-done.3, s32[1,9]{1,0:T(1,128)S(1)} %copy-done.4, bf16[1,9,256,256]{3,2,1,0:T(8,128)(2,1)S(1)} %copy-done), custom_call_target="tpu_custom_call" | custom-call | tf_op jit(solution)/shard_map/arrange/pallas_call | solution.py:260
  8.3 0.0 collective-permute-done.3
  8.3 0.1 collective-permute-start.6
  8.4 0.5 %collective-permute-start.5 = (bf16[32,1024]{1,0:T(8,128)(2,1)S(1)}, bf16[32,1024]{1,0:T(8,128)(2,1)S(1)}, u32[]{:S(2)}, u32[]{:S(2)}) collective-permute-start(bf16[32,1024]{1,0:T(8,128)(2,1)S(1)} %constant_dynamic-update-slice_fusion.refs_0_), channel_id=1, source_target_pairs={{0,1},{1,0},{2,3},{3,2},{4,8},{5,9},{6,10},{7,11},{8,4},{9,5},{10,... | collective-permute-start | bytes 196616 | tf_op jit(solution)/shard_map/ppermute | solution.py:34
  8.9 1.5 %collective-permute-start.4 = (bf16[32,1024]{1,0:T(8,128)(2,1)S(1)}, bf16[32,1024]{1,0:T(8,128)(2,1)S(1)}, u32[]{:S(2)}, u32[]{:S(2)}) collective-permute-start(bf16[32,1024]{1,0:T(8,128)(2,1)S(1)} %constant_dynamic-update-slice_fusion.refs_0_), channel_id=1, source_target_pairs={{0,4},{4,0},{8,12},{12,8},{16,20},{20,16},{24,28},{28,24},{1,5},{5... | collective-permute-start | bytes 196616 | tf_op jit(solution)/shard_map/ppermute | solution.py:20
  10.4 0.0 collective-permute-done
  10.4 2.7 %collective-permute-start.1 = (bf16[2,2,16,128]{3,2,1,0:T(8,128)(2,1)S(1)}, bf16[2,2,16,128]{3,2,1,0:T(8,128)(2,1)S(1)}, u32[]{:S(2)}, u32[]{:S(2)}) collective-permute-start(bf16[2,2,16,128]{3,2,1,0:T(8,128)(2,1)S(1)} %fusion), channel_id=1, source_target_pairs={{0,16},{4,20},{8,24},{12,28},{16,0},{20,4},{24,8},{28,12},{1,17},{... | collective-permute-start | bytes 49160 | tf_op jit(solution)/shard_map/ppermute | solution.py:20
  13.1 0.5 %collective-permute-done.4 = bf16[32,1024]{1,0:T(8,128)(2,1)S(1)} collective-permute-done((bf16[32,1024]{1,0:T(8,128)(2,1)S(1)}, bf16[32,1024]{1,0:T(8,128)(2,1)S(1)}, u32[]{:S(2)}, u32[]{:S(2)}) %collective-permute-start.4) | collective-permute-done | bytes 65568 | tf_op jit(solution)/shard_map/ppermute | solution.py:20
  13.6 0.0 collective-permute-done.5
  13.6 0.1 collective-permute-start.7
  13.7 1.5 %collective-permute-done.1 = bf16[2,2,16,128]{3,2,1,0:T(8,128)(2,1)S(1)} collective-permute-done((bf16[2,2,16,128]{3,2,1,0:T(8,128)(2,1)S(1)}, bf16[2,2,16,128]{3,2,1,0:T(8,128)(2,1)S(1)}, u32[]{:S(2)}, u32[]{:S(2)}) %collective-permute-start.1) | collective-permute-done | bytes 16416 | tf_op jit(solution)/shard_map/ppermute | solution.py:20
  15.1 0.0 collective-permute-done.6.refs_2_
  15.1 0.0 collective-permute-done.7.refs_3_
  15.1 0.4 %near.1 = (f32[1,16,256]{2,1,0:T(8,128)S(1)}, bf16[2,16,256]{2,1,0:T(8,128)(2,1)S(1)}, bf16[1,16,256]{2,1,0:T(8,128)(2,1)S(1)}) custom-call(bf16[13,256,256]{2,1,0:T(8,128)(2,1)S(1)} %arrange.1.blocks, bf16[32,1024]{1,0:T(8,128)(2,1)S(1)} %constant_dynamic-update-slice_fusion.refs_0_, bf16[64,1024]{1,0:T(8,128)(2,1)S(1)} %constant_dynamic-update-slice_fusion.2.refs_1_, ...), custom_call_target="tpu_custom_call" | custom-call | tf_op jit(solution)/shard_map/near/pallas_call | solution.py:296
  15.5 0.4 %collective-permute-start.8 = (bf16[2,16,256]{2,1,0:T(8,128)(2,1)S(1)}, bf16[2,16,256]{2,1,0:T(8,128)(2,1)S(1)}, u32[]{:S(2)}, u32[]{:S(2)}) collective-permute-start(bf16[2,16,256]{2,1,0:T(8,128)(2,1)S(1)} %get-tuple-element.19), channel_id=1, source_target_pairs={{0,2},{1,3},{2,0},{3,1},{4,6},{5,7},{6,4},{7,5},{8,10},{9,11},{10,... | collective-permute-start | bytes 49160 | tf_op jit(solution)/shard_map/ppermute | solution.py:20
  16.0 2.4 %collective-permute-start.2 = (bf16[1,2,16,128]{3,2,1,0:T(8,128)(2,1)S(1)}, bf16[1,2,16,128]{3,2,1,0:T(8,128)(2,1)S(1)}, u32[]{:S(2)}, u32[]{:S(2)}) collective-permute-start(bf16[1,2,16,128]{3,2,1,0:T(8,128)(2,1)S(1)} %dynamic-slice_convert_fusion.1), channel_id=1, source_target_pairs={{0,4},{4,0},{8,12},{12,8},{16,20},{20,16},{24,28},{28,24},{1,5},{5... | collective-permute-start | bytes 24584 | tf_op jit(solution)/shard_map/ppermute | solution.py:20
  18.4 0.9 %collective-permute-done.8.refs_1_ = bf16[2,16,256]{2,1,0:T(8,128)(2,1)S(1)} collective-permute-done((bf16[2,16,256]{2,1,0:T(8,128)(2,1)S(1)}, bf16[2,16,256]{2,1,0:T(8,128)(2,1)S(1)}, u32[]{:S(2)}, u32[]{:S(2)}) %collective-permute-start.8) | collective-permute-done | bytes 16416 | tf_op jit(solution)/shard_map/ppermute | solution.py:20
  19.4 0.0 collective-permute-start.9
  19.4 0.7 %collective-permute-done.2.got = bf16[1,2,16,128]{3,2,1,0:T(8,128)(2,1)S(1)} collective-permute-done((bf16[1,2,16,128]{3,2,1,0:T(8,128)(2,1)S(1)}, bf16[1,2,16,128]{3,2,1,0:T(8,128)(2,1)S(1)}, u32[]{:S(2)}, u32[]{:S(2)}) %collective-permute-start.2) | collective-permute-done | bytes 8224 | tf_op jit(solution)/shard_map/ppermute | solution.py:20
  20.0 0.3 %far.1.far_in = f32[16,1024]{1,0:T(8,128)S(1)} custom-call(f32[1,2,16,128]{3,2,1,0:T(8,128)S(1)} %constant_dynamic-slice_fusion.keep, bf16[1,2,16,128]{3,2,1,0:T(8,128)(2,1)S(1)} %collective-permute-done.2.got, bf16[256,1024]{1,0:T(8,128)(2,1)S(1)} %get-tuple-element.15.high_in, bf16[256,1024]{1,0:T(8,128)(2,1)S(1)} %get-tuple-element.16.low_in), custom_call_target="tpu_custom_call" | custom-call | tf_op jit(solution)/shard_map/far/pallas_call | solution.py:322
  20.3 0.2 %collective-permute-done.9.refs_2_ = bf16[2,16,256]{2,1,0:T(8,128)(2,1)S(1)} collective-permute-done((bf16[2,16,256]{2,1,0:T(8,128)(2,1)S(1)}, bf16[2,16,256]{2,1,0:T(8,128)(2,1)S(1)}, u32[]{:S(2)}, u32[]{:S(2)}) %collective-permute-start.9) | collective-permute-done | bytes 16416 | tf_op jit(solution)/shard_map/ppermute | solution.py:20
  20.5 0.6 %finish.1 = bf16[16,1024]{1,0:T(8,128)(2,1)} custom-call(f32[16,1024]{1,0:T(8,128)S(1)} %far.1.far_in, f32[1,16,256]{2,1,0:T(8,128)S(1)} %get-tuple-element.18.refs_0_, bf16[2,16,256]{2,1,0:T(8,128)(2,1)S(1)} %collective-permute-done.8.refs_1_, bf16[2,16,256]{2,1,0:T(8,128)(2,1)S(1)} %collective-permute-done.9.refs_2_), custom_call_target="tpu_custom_call" | custom-call | tf_op jit(solution)/shard_map/finish/pallas_call | solution.py:346
  (15 shorter events, 0.1 us)
Async XLA Ops:
  0.0 7.0 %copy-start.2 = (bf16[6,32,32]{2,1,0:T(8,128)(2,1)S(1)}, bf16[6,32,32]{2,1,0:T(8,128)(2,1)}, u32[]{:S(2)}) copy-start(bf16[6,32,32]{2,1,0:T(8,128)(2,1)} %transfer.1) | copy-start | bytes 36868
  0.0 7.0 %copy-start.1 = (bf16[4,32,256]{2,1,0:T(8,128)(2,1)S(1)}, bf16[4,32,256]{2,1,0:T(8,128)(2,1)}, u32[]{:S(2)}) copy-start(bf16[4,32,256]{2,1,0:T(8,128)(2,1)} %basis.1) | copy-start | bytes 196612
  0.0 7.5 %copy-start.4 = (s32[1,9]{1,0:T(1,128)S(1)}, s32[1,9]{1,0:T(1,128)}, u32[]{:S(2)}) copy-start(s32[1,9]{1,0:T(1,128)} %alive.1) | copy-start | bytes 112
  0.0 7.6 %copy-start.3 = (s32[1,9]{1,0:T(1,128)S(1)}, s32[1,9]{1,0:T(1,128)}, u32[]{:S(2)}) copy-start(s32[1,9]{1,0:T(1,128)} %columns.1) | copy-start | bytes 112
  0.0 7.6 %copy-start = (bf16[1,9,256,256]{3,2,1,0:T(8,128)(2,1)S(1)}, bf16[1,9,256,256]{3,2,1,0:T(8,128)(2,1)}, u32[]{:S(2)}) copy-start(bf16[1,9,256,256]{3,2,1,0:T(8,128)(2,1)} %blocks.1) | copy-start | bytes 3538948
  0.0 8.3 %collective-permute-start.3 = (bf16[16,1024]{1,0:T(8,128)(2,1)}, bf16[16,1024]{1,0:T(8,128)(2,1)S(1)}, u32[]{:S(2)}, u32[]{:S(2)}) collective-permute-start(bf16[16,1024]{1,0:T(8,128)(2,1)} %vectors_in.1), channel_id=1, source_target_pairs={{0,2},{1,3},{2,0},{3,1},{4,6},{5,7},{6,4},{7,5},{8,10},{9,11},{10,... | collective-permute-start | bytes 98312 | tf_op jit(solution)/shard_map/ppermute | solution.py:20
  5.4 5.0 %collective-permute-start = (bf16[4,2,16,128]{3,2,1,0:T(8,128)(2,1)S(1)}, bf16[4,2,16,128]{3,2,1,0:T(8,128)(2,1)S(1)}, u32[]{:S(2)}, u32[]{:S(2)}) collective-permute-start(bf16[4,2,16,128]{3,2,1,0:T(8,128)(2,1)S(1)} %get-tuple-element.14), channel_id=1, source_target_pairs={{0,8},{4,12},{8,0},{12,4},{16,24},{20,28},{24,16},{28,20},{1,9},{5... | collective-permute-start | bytes 98312 | tf_op jit(solution)/shard_map/ppermute | solution.py:20
  8.3 6.8 %collective-permute-start.6 = (bf16[32,1024]{1,0:T(8,128)(2,1)S(1)}, bf16[32,1024]{1,0:T(8,128)(2,1)S(1)}, u32[]{:S(2)}, u32[]{:S(2)}) collective-permute-start(bf16[32,1024]{1,0:T(8,128)(2,1)S(1)} %constant_dynamic-update-slice_fusion.refs_0_), channel_id=1, source_target_pairs={{0,1},{1,0},{2,3},{3,2},{4,5},{5,4},{6,7},{7,6},{8,9},{9,8},{10,11... | collective-permute-start | bytes 196616 | tf_op jit(solution)/shard_map/ppermute | solution.py:20
  8.4 5.2 %collective-permute-start.5 = (bf16[32,1024]{1,0:T(8,128)(2,1)S(1)}, bf16[32,1024]{1,0:T(8,128)(2,1)S(1)}, u32[]{:S(2)}, u32[]{:S(2)}) collective-permute-start(bf16[32,1024]{1,0:T(8,128)(2,1)S(1)} %constant_dynamic-update-slice_fusion.refs_0_), channel_id=1, source_target_pairs={{0,1},{1,0},{2,3},{3,2},{4,8},{5,9},{6,10},{7,11},{8,4},{9,5},{10,... | collective-permute-start | bytes 196616 | tf_op jit(solution)/shard_map/ppermute | solution.py:34
  8.9 4.7 %collective-permute-start.4 = (bf16[32,1024]{1,0:T(8,128)(2,1)S(1)}, bf16[32,1024]{1,0:T(8,128)(2,1)S(1)}, u32[]{:S(2)}, u32[]{:S(2)}) collective-permute-start(bf16[32,1024]{1,0:T(8,128)(2,1)S(1)} %constant_dynamic-update-slice_fusion.refs_0_), channel_id=1, source_target_pairs={{0,4},{4,0},{8,12},{12,8},{16,20},{20,16},{24,28},{28,24},{1,5},{5... | collective-permute-start | bytes 196616 | tf_op jit(solution)/shard_map/ppermute | solution.py:20
  10.4 4.7 %collective-permute-start.1 = (bf16[2,2,16,128]{3,2,1,0:T(8,128)(2,1)S(1)}, bf16[2,2,16,128]{3,2,1,0:T(8,128)(2,1)S(1)}, u32[]{:S(2)}, u32[]{:S(2)}) collective-permute-start(bf16[2,2,16,128]{3,2,1,0:T(8,128)(2,1)S(1)} %fusion), channel_id=1, source_target_pairs={{0,16},{4,20},{8,24},{12,28},{16,0},{20,4},{24,8},{28,12},{1,17},{... | collective-permute-start | bytes 49160 | tf_op jit(solution)/shard_map/ppermute | solution.py:20
  13.6 1.5 %collective-permute-start.7 = (bf16[64,1024]{1,0:T(8,128)(2,1)S(1)}, bf16[64,1024]{1,0:T(8,128)(2,1)S(1)}, u32[]{:S(2)}, u32[]{:S(2)}) collective-permute-start(bf16[64,1024]{1,0:T(8,128)(2,1)S(1)} %constant_dynamic-update-slice_fusion.2.refs_1_), channel_id=1, source_target_pairs={{0,1},{1,0},{2,3},{3,2},{4,5},{5,4},{6,7},{7,6},{8,9},{9,8},{10,11... | collective-permute-start | bytes 393224 | tf_op jit(solution)/shard_map/ppermute | solution.py:20
  15.5 3.8 %collective-permute-start.8 = (bf16[2,16,256]{2,1,0:T(8,128)(2,1)S(1)}, bf16[2,16,256]{2,1,0:T(8,128)(2,1)S(1)}, u32[]{:S(2)}, u32[]{:S(2)}) collective-permute-start(bf16[2,16,256]{2,1,0:T(8,128)(2,1)S(1)} %get-tuple-element.19), channel_id=1, source_target_pairs={{0,2},{1,3},{2,0},{3,1},{4,6},{5,7},{6,4},{7,5},{8,10},{9,11},{10,... | collective-permute-start | bytes 49160 | tf_op jit(solution)/shard_map/ppermute | solution.py:20
  16.0 4.1 %collective-permute-start.2 = (bf16[1,2,16,128]{3,2,1,0:T(8,128)(2,1)S(1)}, bf16[1,2,16,128]{3,2,1,0:T(8,128)(2,1)S(1)}, u32[]{:S(2)}, u32[]{:S(2)}) collective-permute-start(bf16[1,2,16,128]{3,2,1,0:T(8,128)(2,1)S(1)} %dynamic-slice_convert_fusion.1), channel_id=1, source_target_pairs={{0,4},{4,0},{8,12},{12,8},{16,20},{20,16},{24,28},{28,24},{1,5},{5... | collective-permute-start | bytes 24584 | tf_op jit(solution)/shard_map/ppermute | solution.py:20
  19.4 1.2 %collective-permute-start.9 = (bf16[2,16,256]{2,1,0:T(8,128)(2,1)S(1)}, bf16[2,16,256]{2,1,0:T(8,128)(2,1)S(1)}, u32[]{:S(2)}, u32[]{:S(2)}) collective-permute-start(bf16[2,16,256]{2,1,0:T(8,128)(2,1)S(1)} %pad_maximum_fusion), channel_id=1, source_target_pairs={{0,1},{1,0},{2,3},{3,2},{4,5},{5,4},{6,7},{7,6},{8,9},{9,8},{10,11... | collective-permute-start | bytes 49160 | tf_op jit(solution)/shard_map/ppermute | solution.py:20

commit v7 on v6

--- a/solution.py
+++ b/solution.py
@@ -20,18 +20,26 @@
     return lax.ppermute(values, axis, [(i, i ^ bit) for i in range(count)])
 
 
-def beside(values):
+def across(values, partner, turn):
     leaf_count, sub_count = lax.axis_size("leaf"), lax.axis_size("sub")
     pairs = []
     for leaf in range(leaf_count):
-        other = ((leaf + 1) ^ 1) - 1
+        other = partner(leaf)
+        inside = 0 <= other < leaf_count
         for sub in range(sub_count):
             here = leaf * sub_count + sub
-            if 0 <= other < leaf_count:
-                pairs.append((here, other * sub_count + sub))
+            if inside:
+                pairs.append((here, other * sub_count + (sub ^ turn)))
             else:
                 pairs.append((here, leaf * sub_count + (sub ^ 1)))
     return lax.ppermute(values, ("leaf", "sub"), pairs)
+
+
+def span_of(steps):
+    numbers = [0]
+    for step in steps:
+        numbers = numbers + [number ^ step for number in numbers]
+    return numbers
 
 
 def bits_of(count):
@@ -368,20 +376,27 @@
     sub_count = lax.axis_size("sub")
     me = lax.axis_index("leaf")
     rows = vectors.shape[0]
-    bits = bits_of(sub_count)
+    steps = [bit | 1 for bit in bits_of(sub_count)]
+    turn = 0
     keep, send, own = expand(vectors, leaf_basis, transfer, coupling, far_targets, far_mask)
-    pair = jnp.concatenate([own, flip(vectors, "sub", bits[0])], axis=0)
-    sides = jnp.concatenate([flip(pair, "leaf", 1), beside(pair)], axis=0)
+    pair = jnp.concatenate([own, flip(vectors, "sub", steps[0])], axis=0)
+    near_side = across(pair, lambda leaf: leaf ^ 1, turn)
+    far_side = across(pair, lambda leaf: ((leaf + 1) ^ 1) - 1, turn)
+    sides = jnp.concatenate([near_side, far_side], axis=0)
     stages = stages_of(leaf_count)
     got = flip(send, "leaf", stages[0])
-    order = [0, bits[0]]
     pieces = [(pair, sides)]
-    for bit in bits[1:]:
+    for step in steps[1:]:
         pieces = pieces + [
-            (flip(middle, "sub", bit), flip(outer, "sub", bit))
+            (flip(middle, "sub", step), flip(outer, "sub", step))
             for middle, outer in pieces
         ]
-        order = order + [number ^ bit for number in order]
+    order = span_of(steps)
+    middles = [middle for middle, _ in pieces]
+    outers = [outer for _, outer in pieces]
+    if turn:
+        outers = outers[len(outers) // 2 :] + outers[: len(outers) // 2]
+    pieces = list(zip(middles, outers))
     high, low = operator(transfer, leaf_basis, keep.shape[1] * LANES)
     for bit in sorted(stages[1:], reverse=True):
         total = (keep + got.astype(keep.dtype)).reshape(2, -1, *keep.shape[1:])
@@ -389,18 +404,17 @@
         keep = lax.dynamic_index_in_dim(total, mine, 0, keepdims=False)
         send = lax.dynamic_index_in_dim(total, 1 - mine, 0, keepdims=False)
         got = flip(send.astype(jnp.bfloat16), "leaf", bit)
-    places = [[order.index(0)]] + [
-        [order.index(home) for home in range(bit, 2 * bit)] for bit in bits
-    ]
+    homes = [[step ^ rest for rest in span_of(steps[n + 1 :])] for n, step in enumerate(steps)]
+    places = [[order.index(0)]] + [[order.index(home) for home in group] for group in homes]
     blocks = arrange(near_blocks, near_cols, near_mask, leaf_basis.shape[0])
     made = near(pieces, blocks, rows, places)
     arrays = list(made)
     pool = {0: [(0, 0, 0)]}
-    for number, bit in enumerate(bits):
-        for row in range(bit):
-            pool[bit + row] = [(0, number + 1, row)]
-    for bit in bits:
-        sent = [(home, item) for home in range(bit, 2 * bit) for item in pool[home]]
+    for number, group in enumerate(homes):
+        for row, home in enumerate(group):
+            pool[home] = [(0, number + 1, row)]
+    for step, bit in enumerate(steps):
+        sent = [(home, item) for home in homes[step] for item in pool[home]]
         if len(sent) == arrays[sent[0][1][1]].shape[0]:
             stack = arrays[sent[0][1][1]]
         else:

time: 21.3 us -> 20.5 us (0.962)
  starting transfers between devices: 12.3 us -> 11.8 us
    ppermute x9 -> x8, starting transfers between devices: 11.8 us -> 9.85 us  [flip(): return lax.ppermute(values, axis, [(i, i ^ bit) for i in range(count)])]
    ppermute x1 -> x2, starting transfers between devices: 0.5 us -> 1.91 us  [across(): return lax.ppermute(values, ('leaf', 'sub'), pairs)]
    ppermute x9 -> x8, waiting for transfers between devices: 3.79 us -> 3.42 us  [flip(): return lax.ppermute(values, axis, [(i, i ^ bit) for i in range(count)])]
  transfers between devices with their start and end apart: 10 -> 10, of which waited for: 5 -> 4; matrix products, arithmetic and copies ran while one was open for 0% -> 0% of each run, Pallas kernels for 18% -> 18%
where the time goes in v7:
time: 20.5 us; the launch traced here: 20.4 us
  starting transfers between devices  11.8 us (58%)
  Pallas kernels  4.79 us (23%)
  waiting for transfers between devices  3.59 us (18%)
    ppermute x8, starting transfers between devices, flip(): return lax.ppermute(values, axis, [(i, i ^ bit) for i in range(count)])  9.85 us
    ppermute x8, waiting for transfers between devices, flip(): return lax.ppermute(values, axis, [(i, i ^ bit) for i in range(count)])  3.42 us
    pallas_call x1, Pallas kernels, expand(): pl.pallas_call(functools.partial(expand_kernel, leaf_count), out_shape=[j...  2.32 us
    ppermute x2, starting transfers between devices, across(): return lax.ppermute(values, ('leaf', 'sub'), pairs)  1.91 us
    pallas_call x1, Pallas kernels, arrange(): pl.pallas_call(arrange_kernel, out_shape=jax.ShapeDtypeStruct((3 * subtre...  0.72 us
    pallas_call x1, Pallas kernels, finish(): pl.pallas_call(functools.partial(finish_kernel, sources), out_shape=jax.S...  0.63 us
    pallas_call x1, Pallas kernels, operator(): pl.pallas_call(operator_kernel, out_shape=[shape, shape], in_specs=[VMEM,...  0.47 us
  transfers between devices with their start and end apart: 10, of which 4 were waited for; matrix products, arithmetic and copies ran while one was open for 0% of the time, Pallas kernels for 18%

profile of v7, /device:TPU:0, one launch (start us, length us, event | category | flops | bytes accessed | tf_op | source)
XLA Modules:
  0.0 20.4 jit_solution(18210680370068887681)
XLA Ops:
  0.0 0.0 copy-start.2
  0.0 2.5 %collective-permute-start.3 = (bf16[16,1024]{1,0:T(8,128)(2,1)}, bf16[16,1024]{1,0:T(8,128)(2,1)S(1)}, u32[]{:S(2)}, u32[]{:S(2)}) collective-permute-start(bf16[16,1024]{1,0:T(8,128)(2,1)} %vectors_in.1), channel_id=1, source_target_pairs={{0,3},{1,2},{2,1},{3,0},{4,7},{5,6},{6,5},{7,4},{8,11},{9,10},{10,... | collective-permute-start | bytes 98312 | tf_op jit(solution)/shard_map/ppermute | solution.py:20
  2.5 2.3 %expand.1 = (f32[4,2,16,128]{3,2,1,0:T(8,128)S(1)}, bf16[4,2,16,128]{3,2,1,0:T(8,128)(2,1)S(1)}, bf16[16,1024]{1,0:T(8,128)(2,1)S(1)}) custom-call(s32[7,27]{1,0:T(8,128)} %targets_in.1, s32[7,27]{1,0:T(8,128)} %alive_in.1, bf16[16,1024]{1,0:T(8,128)(2,1)} %vectors_in.1, bf16[4,32,256]{2,1,0:T(8,128)(2,1)} %basis.1, bf16[6,32,32]{2,1,0:T(8,128)(2,1)} %transfer.1, ...), custom_call_target="tpu_custom_call" | custom-call | tf_op jit(solution)/shard_map/expand/pallas_call | solution.py:187
  4.8 1.6 %collective-permute-start = (bf16[4,2,16,128]{3,2,1,0:T(8,128)(2,1)S(1)}, bf16[4,2,16,128]{3,2,1,0:T(8,128)(2,1)S(1)}, u32[]{:S(2)}, u32[]{:S(2)}) collective-permute-start(bf16[4,2,16,128]{3,2,1,0:T(8,128)(2,1)S(1)} %get-tuple-element.14), channel_id=1, source_target_pairs={{0,8},{4,12},{8,0},{12,4},{16,24},{20,28},{24,16},{28,20},{1,9},{5... | collective-permute-start | bytes 98312 | tf_op jit(solution)/shard_map/ppermute | solution.py:20
  6.5 0.0 copy-done.2
  6.5 0.0 copy-done.1
  6.5 0.5 %operator.1 = (bf16[256,1024]{1,0:T(8,128)(2,1)S(1)}, bf16[256,1024]{1,0:T(8,128)(2,1)S(1)}) custom-call(bf16[6,32,32]{2,1,0:T(8,128)(2,1)S(1)} %copy-done.2, bf16[4,32,256]{2,1,0:T(8,128)(2,1)S(1)} %copy-done.1), custom_call_target="tpu_custom_call" | custom-call | tf_op jit(solution)/shard_map/operator/pallas_call | solution.py:239
  7.0 0.0 copy-done.4
  7.0 0.0 copy-done.3
  7.0 0.0 copy-done
  7.0 0.7 %arrange.1.blocks = bf16[13,256,256]{2,1,0:T(8,128)(2,1)S(1)} custom-call(s32[1,9]{1,0:T(1,128)S(1)} %copy-done.3, s32[1,9]{1,0:T(1,128)S(1)} %copy-done.4, bf16[1,9,256,256]{3,2,1,0:T(8,128)(2,1)S(1)} %copy-done), custom_call_target="tpu_custom_call" | custom-call | tf_op jit(solution)/shard_map/arrange/pallas_call | solution.py:268
  7.7 0.0 collective-permute-done.3
  7.8 0.5 %collective-permute-start.6 = (bf16[32,1024]{1,0:T(8,128)(2,1)S(1)}, bf16[32,1024]{1,0:T(8,128)(2,1)S(1)}, u32[]{:S(2)}, u32[]{:S(2)}) collective-permute-start(bf16[32,1024]{1,0:T(8,128)(2,1)S(1)} %constant_dynamic-update-slice_fusion.refs_0_), channel_id=1, source_target_pairs={{0,1},{1,0},{2,3},{3,2},{4,5},{5,4},{6,7},{7,6},{8,9},{9,8},{10,11... | collective-permute-start | bytes 196616 | tf_op jit(solution)/shard_map/ppermute | solution.py:20
  8.2 0.1 collective-permute-start.5
  8.3 1.8 %collective-permute-start.4 = (bf16[32,1024]{1,0:T(8,128)(2,1)S(1)}, bf16[32,1024]{1,0:T(8,128)(2,1)S(1)}, u32[]{:S(2)}, u32[]{:S(2)}) collective-permute-start(bf16[32,1024]{1,0:T(8,128)(2,1)S(1)} %constant_dynamic-update-slice_fusion.refs_0_), channel_id=1, source_target_pairs={{0,4},{1,5},{2,6},{3,7},{4,0},{5,1},{6,2},{7,3},{8,12},{9,13},{10,... | collective-permute-start | bytes 196616 | tf_op jit(solution)/shard_map/ppermute | solution.py:35
  10.1 0.0 collective-permute-done
  10.2 2.7 %collective-permute-start.1 = (bf16[2,2,16,128]{3,2,1,0:T(8,128)(2,1)S(1)}, bf16[2,2,16,128]{3,2,1,0:T(8,128)(2,1)S(1)}, u32[]{:S(2)}, u32[]{:S(2)}) collective-permute-start(bf16[2,2,16,128]{3,2,1,0:T(8,128)(2,1)S(1)} %fusion), channel_id=1, source_target_pairs={{0,16},{4,20},{8,24},{12,28},{16,0},{20,4},{24,8},{28,12},{1,17},{... | collective-permute-start | bytes 49160 | tf_op jit(solution)/shard_map/ppermute | solution.py:20
  12.8 0.2 collective-permute-done.4
  13.0 0.0 collective-permute-done.5
  13.0 0.1 collective-permute-start.7
  13.1 1.8 %collective-permute-done.1 = bf16[2,2,16,128]{3,2,1,0:T(8,128)(2,1)S(1)} collective-permute-done((bf16[2,2,16,128]{3,2,1,0:T(8,128)(2,1)S(1)}, bf16[2,2,16,128]{3,2,1,0:T(8,128)(2,1)S(1)}, u32[]{:S(2)}, u32[]{:S(2)}) %collective-permute-start.1) | collective-permute-done | bytes 16416 | tf_op jit(solution)/shard_map/ppermute | solution.py:20
  14.9 0.0 collective-permute-done.6.refs_2_
  14.9 0.0 collective-permute-done.7.refs_3_
  14.9 0.4 %near.1 = (f32[1,16,256]{2,1,0:T(8,128)S(1)}, bf16[2,16,256]{2,1,0:T(8,128)(2,1)S(1)}, bf16[1,16,256]{2,1,0:T(8,128)(2,1)S(1)}) custom-call(bf16[13,256,256]{2,1,0:T(8,128)(2,1)S(1)} %arrange.1.blocks, bf16[32,1024]{1,0:T(8,128)(2,1)S(1)} %constant_dynamic-update-slice_fusion.refs_0_, bf16[64,1024]{1,0:T(8,128)(2,1)S(1)} %constant_dynamic-update-slice_fusion.2.refs_1_, ...), custom_call_target="tpu_custom_call" | custom-call | tf_op jit(solution)/shard_map/near/pallas_call | solution.py:304
  15.3 0.1 collective-permute-start.8
  15.4 2.4 %collective-permute-start.2 = (bf16[1,2,16,128]{3,2,1,0:T(8,128)(2,1)S(1)}, bf16[1,2,16,128]{3,2,1,0:T(8,128)(2,1)S(1)}, u32[]{:S(2)}, u32[]{:S(2)}) collective-permute-start(bf16[1,2,16,128]{3,2,1,0:T(8,128)(2,1)S(1)} %dynamic-slice_convert_fusion.1), channel_id=1, source_target_pairs={{0,4},{4,0},{8,12},{12,8},{16,20},{20,16},{24,28},{28,24},{1,5},{5... | collective-permute-start | bytes 24584 | tf_op jit(solution)/shard_map/ppermute | solution.py:20
  17.8 0.7 %collective-permute-done.8.refs_1_ = bf16[2,16,256]{2,1,0:T(8,128)(2,1)S(1)} collective-permute-done((bf16[2,16,256]{2,1,0:T(8,128)(2,1)S(1)}, bf16[2,16,256]{2,1,0:T(8,128)(2,1)S(1)}, u32[]{:S(2)}, u32[]{:S(2)}) %collective-permute-start.8) | collective-permute-done | bytes 16416 | tf_op jit(solution)/shard_map/ppermute | solution.py:20
  18.6 0.0 collective-permute-start.9
  18.6 0.9 %collective-permute-done.2.got = bf16[1,2,16,128]{3,2,1,0:T(8,128)(2,1)S(1)} collective-permute-done((bf16[1,2,16,128]{3,2,1,0:T(8,128)(2,1)S(1)}, bf16[1,2,16,128]{3,2,1,0:T(8,128)(2,1)S(1)}, u32[]{:S(2)}, u32[]{:S(2)}) %collective-permute-start.2) | collective-permute-done | bytes 8224 | tf_op jit(solution)/shard_map/ppermute | solution.py:20
  19.5 0.3 %far.1.far_in = f32[16,1024]{1,0:T(8,128)S(1)} custom-call(f32[1,2,16,128]{3,2,1,0:T(8,128)S(1)} %constant_dynamic-slice_fusion.keep, bf16[1,2,16,128]{3,2,1,0:T(8,128)(2,1)S(1)} %collective-permute-done.2.got, bf16[256,1024]{1,0:T(8,128)(2,1)S(1)} %get-tuple-element.15.high_in, bf16[256,1024]{1,0:T(8,128)(2,1)S(1)} %get-tuple-element.16.low_in), custom_call_target="tpu_custom_call" | custom-call | tf_op jit(solution)/shard_map/far/pallas_call | solution.py:330
  19.7 0.0 collective-permute-done.9.refs_2_
  19.8 0.6 %finish.1 = bf16[16,1024]{1,0:T(8,128)(2,1)} custom-call(f32[16,1024]{1,0:T(8,128)S(1)} %far.1.far_in, f32[1,16,256]{2,1,0:T(8,128)S(1)} %get-tuple-element.18.refs_0_, bf16[2,16,256]{2,1,0:T(8,128)(2,1)S(1)} %collective-permute-done.8.refs_1_, bf16[2,16,256]{2,1,0:T(8,128)(2,1)S(1)} %collective-permute-done.9.refs_2_), custom_call_target="tpu_custom_call" | custom-call | tf_op jit(solution)/shard_map/finish/pallas_call | solution.py:354
  (15 shorter events, 0.1 us)
Async XLA Ops:
  0.0 6.5 %copy-start.2 = (bf16[6,32,32]{2,1,0:T(8,128)(2,1)S(1)}, bf16[6,32,32]{2,1,0:T(8,128)(2,1)}, u32[]{:S(2)}) copy-start(bf16[6,32,32]{2,1,0:T(8,128)(2,1)} %transfer.1) | copy-start | bytes 36868
  0.0 6.5 %copy-start.1 = (bf16[4,32,256]{2,1,0:T(8,128)(2,1)S(1)}, bf16[4,32,256]{2,1,0:T(8,128)(2,1)}, u32[]{:S(2)}) copy-start(bf16[4,32,256]{2,1,0:T(8,128)(2,1)} %basis.1) | copy-start | bytes 196612
  0.0 7.0 %copy-start.4 = (s32[1,9]{1,0:T(1,128)S(1)}, s32[1,9]{1,0:T(1,128)}, u32[]{:S(2)}) copy-start(s32[1,9]{1,0:T(1,128)} %alive.1) | copy-start | bytes 112
  0.0 7.0 %copy-start.3 = (s32[1,9]{1,0:T(1,128)S(1)}, s32[1,9]{1,0:T(1,128)}, u32[]{:S(2)}) copy-start(s32[1,9]{1,0:T(1,128)} %columns.1) | copy-start | bytes 112
  0.0 7.0 %copy-start = (bf16[1,9,256,256]{3,2,1,0:T(8,128)(2,1)S(1)}, bf16[1,9,256,256]{3,2,1,0:T(8,128)(2,1)}, u32[]{:S(2)}) copy-start(bf16[1,9,256,256]{3,2,1,0:T(8,128)(2,1)} %blocks.1) | copy-start | bytes 3538948
  0.0 7.7 %collective-permute-start.3 = (bf16[16,1024]{1,0:T(8,128)(2,1)}, bf16[16,1024]{1,0:T(8,128)(2,1)S(1)}, u32[]{:S(2)}, u32[]{:S(2)}) collective-permute-start(bf16[16,1024]{1,0:T(8,128)(2,1)} %vectors_in.1), channel_id=1, source_target_pairs={{0,3},{1,2},{2,1},{3,0},{4,7},{5,6},{6,5},{7,4},{8,11},{9,10},{10,... | collective-permute-start | bytes 98312 | tf_op jit(solution)/shard_map/ppermute | solution.py:20
  4.8 5.3 %collective-permute-start = (bf16[4,2,16,128]{3,2,1,0:T(8,128)(2,1)S(1)}, bf16[4,2,16,128]{3,2,1,0:T(8,128)(2,1)S(1)}, u32[]{:S(2)}, u32[]{:S(2)}) collective-permute-start(bf16[4,2,16,128]{3,2,1,0:T(8,128)(2,1)S(1)} %get-tuple-element.14), channel_id=1, source_target_pairs={{0,8},{4,12},{8,0},{12,4},{16,24},{20,28},{24,16},{28,20},{1,9},{5... | collective-permute-start | bytes 98312 | tf_op jit(solution)/shard_map/ppermute | solution.py:20
  7.8 7.1 %collective-permute-start.6 = (bf16[32,1024]{1,0:T(8,128)(2,1)S(1)}, bf16[32,1024]{1,0:T(8,128)(2,1)S(1)}, u32[]{:S(2)}, u32[]{:S(2)}) collective-permute-start(bf16[32,1024]{1,0:T(8,128)(2,1)S(1)} %constant_dynamic-update-slice_fusion.refs_0_), channel_id=1, source_target_pairs={{0,1},{1,0},{2,3},{3,2},{4,5},{5,4},{6,7},{7,6},{8,9},{9,8},{10,11... | collective-permute-start | bytes 196616 | tf_op jit(solution)/shard_map/ppermute | solution.py:20
  8.2 4.8 %collective-permute-start.5 = (bf16[32,1024]{1,0:T(8,128)(2,1)S(1)}, bf16[32,1024]{1,0:T(8,128)(2,1)S(1)}, u32[]{:S(2)}, u32[]{:S(2)}) collective-permute-start(bf16[32,1024]{1,0:T(8,128)(2,1)S(1)} %constant_dynamic-update-slice_fusion.refs_0_), channel_id=1, source_target_pairs={{0,1},{1,0},{2,3},{3,2},{4,8},{5,9},{6,10},{7,11},{8,4},{9,5},{10,... | collective-permute-start | bytes 196616 | tf_op jit(solution)/shard_map/ppermute | solution.py:35
  8.3 4.7 %collective-permute-start.4 = (bf16[32,1024]{1,0:T(8,128)(2,1)S(1)}, bf16[32,1024]{1,0:T(8,128)(2,1)S(1)}, u32[]{:S(2)}, u32[]{:S(2)}) collective-permute-start(bf16[32,1024]{1,0:T(8,128)(2,1)S(1)} %constant_dynamic-update-slice_fusion.refs_0_), channel_id=1, source_target_pairs={{0,4},{1,5},{2,6},{3,7},{4,0},{5,1},{6,2},{7,3},{8,12},{9,13},{10,... | collective-permute-start | bytes 196616 | tf_op jit(solution)/shard_map/ppermute | solution.py:35
  10.2 4.7 %collective-permute-start.1 = (bf16[2,2,16,128]{3,2,1,0:T(8,128)(2,1)S(1)}, bf16[2,2,16,128]{3,2,1,0:T(8,128)(2,1)S(1)}, u32[]{:S(2)}, u32[]{:S(2)}) collective-permute-start(bf16[2,2,16,128]{3,2,1,0:T(8,128)(2,1)S(1)} %fusion), channel_id=1, source_target_pairs={{0,16},{4,20},{8,24},{12,28},{16,0},{20,4},{24,8},{28,12},{1,17},{... | collective-permute-start | bytes 49160 | tf_op jit(solution)/shard_map/ppermute | solution.py:20
  13.0 1.9 %collective-permute-start.7 = (bf16[64,1024]{1,0:T(8,128)(2,1)S(1)}, bf16[64,1024]{1,0:T(8,128)(2,1)S(1)}, u32[]{:S(2)}, u32[]{:S(2)}) collective-permute-start(bf16[64,1024]{1,0:T(8,128)(2,1)S(1)} %constant_dynamic-update-slice_fusion.2.refs_1_), channel_id=1, source_target_pairs={{0,1},{1,0},{2,3},{3,2},{4,5},{5,4},{6,7},{7,6},{8,9},{9,8},{10,11... | collective-permute-start | bytes 393224 | tf_op jit(solution)/shard_map/ppermute | solution.py:20
  15.3 3.3 %collective-permute-start.8 = (bf16[2,16,256]{2,1,0:T(8,128)(2,1)S(1)}, bf16[2,16,256]{2,1,0:T(8,128)(2,1)S(1)}, u32[]{:S(2)}, u32[]{:S(2)}) collective-permute-start(bf16[2,16,256]{2,1,0:T(8,128)(2,1)S(1)} %get-tuple-element.19), channel_id=1, source_target_pairs={{0,3},{1,2},{2,1},{3,0},{4,7},{5,6},{6,5},{7,4},{8,11},{9,10},{10,... | collective-permute-start | bytes 49160 | tf_op jit(solution)/shard_map/ppermute | solution.py:20
  15.4 4.1 %collective-permute-start.2 = (bf16[1,2,16,128]{3,2,1,0:T(8,128)(2,1)S(1)}, bf16[1,2,16,128]{3,2,1,0:T(8,128)(2,1)S(1)}, u32[]{:S(2)}, u32[]{:S(2)}) collective-permute-start(bf16[1,2,16,128]{3,2,1,0:T(8,128)(2,1)S(1)} %dynamic-slice_convert_fusion.1), channel_id=1, source_target_pairs={{0,4},{4,0},{8,12},{12,8},{16,20},{20,16},{24,28},{28,24},{1,5},{5... | collective-permute-start | bytes 24584 | tf_op jit(solution)/shard_map/ppermute | solution.py:20
  18.6 1.2 %collective-permute-start.9 = (bf16[2,16,256]{2,1,0:T(8,128)(2,1)S(1)}, bf16[2,16,256]{2,1,0:T(8,128)(2,1)S(1)}, u32[]{:S(2)}, u32[]{:S(2)}) collective-permute-start(bf16[2,16,256]{2,1,0:T(8,128)(2,1)S(1)} %pad_maximum_fusion), channel_id=1, source_target_pairs={{0,1},{1,0},{2,3},{3,2},{4,5},{5,4},{6,7},{7,6},{8,9},{9,8},{10,11... | collective-permute-start | bytes 49160 | tf_op jit(solution)/shard_map/ppermute | solution.py:20

commit v8 on v7

--- a/solution.py
+++ b/solution.py
@@ -33,13 +33,6 @@
             else:
                 pairs.append((here, leaf * sub_count + (sub ^ 1)))
     return lax.ppermute(values, ("leaf", "sub"), pairs)
-
-
-def span_of(steps):
-    numbers = [0]
-    for step in steps:
-        numbers = numbers + [number ^ step for number in numbers]
-    return numbers
 
 
 def bits_of(count):
@@ -246,74 +239,51 @@
     )(transfer, basis)
 
 
-def arrange_kernel(columns, alive, blocks, out):
-    count, leaf_size = blocks.shape[1:3]
-    subtree = (out.shape[0] - 1) // 3
+def near_kernel(*refs):
+    leaves, (pair, near_side, far_side, own, away, window) = refs[:-6], refs[-6:]
+    rows, points = pair.shape
+    size = rows // 2
+    for tree, piece in enumerate((pair, near_side, far_side)):
+        window[tree] = piece[...]
     me = lax.axis_index("leaf")
-    first = me * subtree
-    partner = (me ^ 1) * subtree
-    zero = jnp.zeros((leaf_size, blocks.shape[3]), out.dtype)
-    for place in range(3 * subtree):
-        out[place] = zero
-    for k in range(count):
-        column = columns[0, k]
-        own_tree = (column >= first) & (column < first + subtree)
-        partner_tree = (column >= partner) & (column < partner + subtree)
-        tree = jnp.where(own_tree, 0, jnp.where(partner_tree, 1, 2))
-        place = tree * subtree + lax.rem(column, subtree)
-        out[jnp.where(alive[0, k] == 1, place, 3 * subtree)] = blocks[0, k]
-
-
-def arrange(blocks, columns, alive, subtree):
-    return pl.pallas_call(
-        arrange_kernel,
-        out_shape=jax.ShapeDtypeStruct((3 * subtree + 1, *blocks.shape[2:]), blocks.dtype),
-        in_specs=[SMEM, SMEM, VMEM],
-        out_specs=VMEM,
-        compiler_params=PARAMS,
-        name="arrange",
-    )(columns, alive, blocks)
-
-
-def near_kernel(places, sub_count, blocks, *refs):
-    outs, pieces = refs[-len(places) :], refs[: -len(places)]
-    middles, outers = pieces[0::2], pieces[1::2]
-    rows, points = middles[0].shape
-    leaf_size = blocks.shape[1]
-    subtree = points // leaf_size
-    total = None
-    for tree in range(3):
-        for j in range(subtree):
-            columns = slice(j * leaf_size, (j + 1) * leaf_size)
-            if tree == 0:
-                taken = [ref[:, columns] for ref in middles]
-            else:
-                taken = [ref[(tree - 1) * rows : tree * rows, columns] for ref in outers]
-            product = dot(jnp.concatenate(taken, axis=0), blocks[tree * subtree + j])
+    count = len(leaves) // 3
+    for leaf in range(count):
+        columns, alive, blocks = leaves[3 * leaf : 3 * leaf + 3]
+        entries, leaf_size = blocks.shape[1:3]
+        subtree = points // leaf_size
+        first = me * subtree
+        partner = (me ^ 1) * subtree
+        total = None
+        for k in range(entries):
+            column = columns[0, k]
+            own_tree = (column >= first) & (column < first + subtree)
+            partner_tree = (column >= partner) & (column < partner + subtree)
+            tree = jnp.where(own_tree, 0, jnp.where(partner_tree, 1, 2))
+            start = pl.multiple_of(lax.rem(column, subtree) * leaf_size, leaf_size)
+            taken = window[tree, :, pl.ds(start, leaf_size)]
+            live = alive[0, k].astype(jnp.float32).astype(jnp.bfloat16)
+            product = dot(taken * live, blocks[0, k])
             total = product if total is None else total + product
-    size = total.shape[0] // sub_count
-    for out, groups in zip(outs, places):
-        for number, group in enumerate(groups):
-            out[number] = total[group * size : (group + 1) * size].astype(out.dtype)
-
-
-def near(pieces, blocks, rows, places):
-    sub_count = lax.axis_size("sub")
-    leaf_size = blocks.shape[1]
-    flat = [array for pair in pieces for array in pair]
-    return pl.pallas_call(
-        functools.partial(near_kernel, places, sub_count),
+        own[leaf] = total[:size]
+        away[leaf] = total[size:].astype(away.dtype)
+
+
+def near(leaves, pair, near_side, far_side):
+    rows, points = pair.shape
+    leaf_size = leaves[0][2].shape[2]
+    shape = (len(leaves), rows // 2, leaf_size)
+    return pl.pallas_call(
+        near_kernel,
         out_shape=[
-            jax.ShapeDtypeStruct(
-                (len(groups), rows, leaf_size), jnp.bfloat16 if number else jnp.float32
-            )
-            for number, groups in enumerate(places)
+            jax.ShapeDtypeStruct(shape, jnp.float32),
+            jax.ShapeDtypeStruct(shape, jnp.bfloat16),
         ],
-        in_specs=[VMEM] * (1 + len(flat)),
-        out_specs=[VMEM] * len(places),
+        in_specs=[SMEM, SMEM, VMEM] * len(leaves) + [VMEM] * 3,
+        out_specs=[VMEM, VMEM],
+        scratch_shapes=[pltpu.VMEM((3, rows, points), pair.dtype)],
         compiler_params=PARAMS,
         name="near",
-    )(blocks, *flat)
+    )(*[array for leaf in leaves for array in leaf], pair, near_side, far_side)
 
 
 def far_kernel(keep, got, high_in, low_in, out):
@@ -375,28 +345,14 @@
     leaf_count = lax.axis_size("leaf")
     sub_count = lax.axis_size("sub")
     me = lax.axis_index("leaf")
-    rows = vectors.shape[0]
     steps = [bit | 1 for bit in bits_of(sub_count)]
     turn = 0
     keep, send, own = expand(vectors, leaf_basis, transfer, coupling, far_targets, far_mask)
     pair = jnp.concatenate([own, flip(vectors, "sub", steps[0])], axis=0)
     near_side = across(pair, lambda leaf: leaf ^ 1, turn)
     far_side = across(pair, lambda leaf: ((leaf + 1) ^ 1) - 1, turn)
-    sides = jnp.concatenate([near_side, far_side], axis=0)
     stages = stages_of(leaf_count)
     got = flip(send, "leaf", stages[0])
-    pieces = [(pair, sides)]
-    for step in steps[1:]:
-        pieces = pieces + [
-            (flip(middle, "sub", step), flip(outer, "sub", step))
-            for middle, outer in pieces
-        ]
-    order = span_of(steps)
-    middles = [middle for middle, _ in pieces]
-    outers = [outer for _, outer in pieces]
-    if turn:
-        outers = outers[len(outers) // 2 :] + outers[: len(outers) // 2]
-    pieces = list(zip(middles, outers))
     high, low = operator(transfer, leaf_basis, keep.shape[1] * LANES)
     for bit in sorted(stages[1:], reverse=True):
         total = (keep + got.astype(keep.dtype)).reshape(2, -1, *keep.shape[1:])
@@ -404,28 +360,19 @@
         keep = lax.dynamic_index_in_dim(total, mine, 0, keepdims=False)
         send = lax.dynamic_index_in_dim(total, 1 - mine, 0, keepdims=False)
         got = flip(send.astype(jnp.bfloat16), "leaf", bit)
-    homes = [[step ^ rest for rest in span_of(steps[n + 1 :])] for n, step in enumerate(steps)]
-    places = [[order.index(0)]] + [[order.index(home) for home in group] for group in homes]
-    blocks = arrange(near_blocks, near_cols, near_mask, leaf_basis.shape[0])
-    made = near(pieces, blocks, rows, places)
-    arrays = list(made)
-    pool = {0: [(0, 0, 0)]}
-    for number, group in enumerate(homes):
-        for row, home in enumerate(group):
-            pool[home] = [(0, number + 1, row)]
-    for step, bit in enumerate(steps):
-        sent = [(home, item) for home in homes[step] for item in pool[home]]
-        if len(sent) == arrays[sent[0][1][1]].shape[0]:
-            stack = arrays[sent[0][1][1]]
-        else:
-            stack = jnp.concatenate([arrays[at][row : row + 1] for _, (_, at, row) in sent], axis=0)
-        arrays.append(flip(stack, "sub", bit))
-        for row, (home, (source, _, _)) in enumerate(sent):
-            pool[home ^ bit].append((source ^ bit, len(arrays) - 1, row))
-    used = sorted({at for _, at, _ in pool[0]})
-    sources = [(source, used.index(at), row) for source, at, row in pool[0]]
+    leaves = [(near_cols, near_mask, near_blocks)]
+    leaves.append(
+        (
+            flip(near_cols, "sub", 1),
+            flip(near_mask, "sub", 1),
+            flip(near_blocks, "sub", 1),
+        )
+    )
+    mine, away = near(leaves, pair, near_side, far_side)
+    back = flip(away, "sub", steps[0])
+    sources = [(0, 0, 0), (1, 0, 1), (steps[0], 1, 0), (steps[0] ^ 1, 1, 1)]
     far_part = far(keep, got, high, low)
-    return finish(far_part, [arrays[at] for at in used], sources)
+    return finish(far_part, [mine, back], sources)
 
 
 def solution(mesh):

time: 20.5 us -> 28 us (1.37)
  waiting for transfers between devices: 3.59 us -> 7.44 us
  local copies, waits for them, and re-layouts: 0.07 us -> 3.47 us
  starting transfers between devices: 11.8 us -> 10.4 us
  other arithmetic: 0.02 us -> 0.85 us
  Pallas kernels: 4.79 us -> 5.34 us
    ppermute x2, waiting for transfers between devices: 0.17 us -> 2.36 us  [across(): return lax.ppermute(values, ('leaf', 'sub'), pairs)]
    unnamed x12 -> x15, local copies, waits for them, and re-layouts: 0.03 us -> 2.07 us
    ppermute x8, starting transfers between devices: 9.85 us -> 8.05 us  [flip(): return lax.ppermute(values, axis, [(i, i ^ bit) for i in range(count)])]
    ppermute x8, waiting for transfers between devices: 3.42 us -> 5.08 us  [flip(): return lax.ppermute(values, axis, [(i, i ^ bit) for i in range(count)])]
    concatenate x1, local copies, waits for them, and re-layouts: 0.01 us -> 1.37 us  [local(): pair = jnp.concatenate([own, flip(vectors, 'sub', steps[0])], axis=0)]
    add x2, other arithmetic: 0.01 us -> 0.85 us  [local(): total = (keep + got.astype(keep.dtype)).reshape(2, -1, *keep.shape[1:])]
    pallas_call x1, Pallas kernels: 2.32 us -> 2.92 us  [expand(): pl.pallas_call(functools.partial(expand_kernel, leaf_count), out_shape=[j...]
    ppermute x2, starting transfers between devices: 1.91 us -> 2.38 us  [across(): return lax.ppermute(values, ('leaf', 'sub'), pairs)]
  transfers between devices with their start and end apart: 10 -> 10, of which waited for: 4 -> 4; matrix products, arithmetic and copies ran while one was open for 0% -> 10% of each run, Pallas kernels for 18% -> 17%
where the time goes in v8:
time: 28 us; the launch traced here: 27.7 us
  starting transfers between devices  10.4 us (37%)
  waiting for transfers between devices  7.44 us (27%)
  Pallas kernels  5.34 us (19%)
  local copies, waits for them, and re-layouts  3.47 us (12%)
  other arithmetic  0.85 us (3%)
    ppermute x8, starting transfers between devices, flip(): return lax.ppermute(values, axis, [(i, i ^ bit) for i in range(count)])  8.05 us
    ppermute x8, waiting for transfers between devices, flip(): return lax.ppermute(values, axis, [(i, i ^ bit) for i in range(count)])  5.08 us
    pallas_call x1, Pallas kernels, expand(): pl.pallas_call(functools.partial(expand_kernel, leaf_count), out_shape=[j...  2.92 us
    ppermute x2, starting transfers between devices, across(): return lax.ppermute(values, ('leaf', 'sub'), pairs)  2.38 us
    ppermute x2, waiting for transfers between devices, across(): return lax.ppermute(values, ('leaf', 'sub'), pairs)  2.36 us
    unnamed x15, local copies, waits for them, and re-layouts  2.07 us
    concatenate x1, local copies, waits for them, and re-layouts, local(): pair = jnp.concatenate([own, flip(vectors, 'sub', steps[0])], axis=0)  1.37 us
    pallas_call x1, Pallas kernels, near(): pl.pallas_call(near_kernel, out_shape=[jax.ShapeDtypeStruct(shape, jnp.fl...  1.06 us
  transfers between devices with their start and end apart: 10, of which 4 were waited for; matrix products, arithmetic and copies ran while one was open for 10% of the time, Pallas kernels for 17%

profile of v8, /device:TPU:0, one launch (start us, length us, event | category | flops | bytes accessed | tf_op | source)
XLA Modules:
  0.0 27.7 jit_solution(16926621305182802801)
XLA Ops:
  0.0 0.6 %collective-permute-start.5 = (bf16[1,9,256,256]{3,2,1,0:T(8,128)(2,1)}, bf16[1,9,256,256]{3,2,1,0:T(8,128)(2,1)S(1)}, u32[]{:S(2)}, u32[]{:S(2)}) collective-permute-start(bf16[1,9,256,256]{3,2,1,0:T(8,128)(2,1)} %refs_2_.1), channel_id=1, source_target_pairs={{0,1},{1,0},{2,3},{3,2},{4,5},{5,4},{6,7},{7,6},{8,9},{9,8},{10,11... | collective-permute-start | bytes 3538952 | tf_op jit(solution)/shard_map/ppermute | solution.py:20
  0.6 0.1 collective-permute-start.3
  0.7 0.4 %collective-permute-start.4 = (s32[1,9]{1,0:T(1,128)}, s32[1,9]{1,0:T(1,128)S(1)}, u32[]{:S(2)}, u32[]{:S(2)}) collective-permute-start(s32[1,9]{1,0:T(1,128)} %refs_1_.1), channel_id=1, source_target_pairs={{0,1},{1,0},{2,3},{3,2},{4,5},{5,4},{6,7},{7,6},{8,9},{9,8},{10,11... | collective-permute-start | bytes 116 | tf_op jit(solution)/shard_map/ppermute | solution.py:20
  1.1 2.6 %collective-permute-start.6 = (bf16[16,1024]{1,0:T(8,128)(2,1)}, bf16[16,1024]{1,0:T(8,128)(2,1)}, u32[]{:S(2)}, u32[]{:S(2)}) collective-permute-start(bf16[16,1024]{1,0:T(8,128)(2,1)} %vectors_in.1), channel_id=1, source_target_pairs={{0,3},{1,2},{2,1},{3,0},{4,7},{5,6},{6,5},{7,4},{8,11},{9,10},{10,... | collective-permute-start | bytes 98312 | tf_op jit(solution)/shard_map/ppermute | solution.py:20
  3.7 2.9 %expand.1 = (f32[4,2,16,128]{3,2,1,0:T(8,128)S(1)}, bf16[4,2,16,128]{3,2,1,0:T(8,128)(2,1)}, bf16[16,1024]{1,0:T(8,128)(2,1)S(1)}) custom-call(s32[7,27]{1,0:T(8,128)} %targets_in.1, s32[7,27]{1,0:T(8,128)} %alive_in.1, bf16[16,1024]{1,0:T(8,128)(2,1)} %vectors_in.1, bf16[4,32,256]{2,1,0:T(8,128)(2,1)} %basis.1, bf16[6,32,32]{2,1,0:T(8,128)(2,1)} %transfer.1, ...), custom_call_target="tpu_custom_call" | custom-call | tf_op jit(solution)/shard_map/expand/pallas_call | solution.py:180
  6.6 0.6 %copy-done.4 = f32[4,2,16,128]{3,2,1,0:T(8,128)} copy-done((f32[4,2,16,128]{3,2,1,0:T(8,128)}, f32[4,2,16,128]{3,2,1,0:T(8,128)S(1)}, u32[]{:S(2)}) %copy-start.4) | copy-done | bytes 65560
  7.2 1.6 %collective-permute-start = (bf16[4,2,16,128]{3,2,1,0:T(8,128)(2,1)}, bf16[4,2,16,128]{3,2,1,0:T(8,128)(2,1)}, u32[]{:S(2)}, u32[]{:S(2)}) collective-permute-start(bf16[4,2,16,128]{3,2,1,0:T(8,128)(2,1)} %get-tuple-element.13), channel_id=1, source_target_pairs={{0,8},{4,12},{8,0},{12,4},{16,24},{20,28},{24,16},{28,20},{1,9},{5... | collective-permute-start | bytes 98312 | tf_op jit(solution)/shard_map/ppermute | solution.py:20
  8.8 0.6 %constant_dynamic-update-slice_fusion.1 = bf16[32,1024]{1,0:T(8,128)(2,1)} fusion(bf16[16,1024]{1,0:T(8,128)(2,1)S(1)} %get-tuple-element.16), kind=kLoop, calls=%fused_computation.6 | loop fusion | bytes 65536
  9.4 0.0 copy-done.2
  9.4 0.5 %operator.1 = (bf16[256,1024]{1,0:T(8,128)(2,1)S(1)}, bf16[256,1024]{1,0:T(8,128)(2,1)S(1)}) custom-call(bf16[6,32,32]{2,1,0:T(8,128)(2,1)S(1)} %copy-done.2, bf16[4,32,256]{2,1,0:T(8,128)(2,1)S(1)} %copy-done.1), custom_call_target="tpu_custom_call" | custom-call | tf_op jit(solution)/shard_map/operator/pallas_call | solution.py:232
  9.9 1.5 %collective-permute-done = bf16[4,2,16,128]{3,2,1,0:T(8,128)(2,1)} collective-permute-done((bf16[4,2,16,128]{3,2,1,0:T(8,128)(2,1)}, bf16[4,2,16,128]{3,2,1,0:T(8,128)(2,1)}, u32[]{:S(2)}, u32[]{:S(2)}) %collective-permute-start) | collective-permute-done | bytes 32800 | tf_op jit(solution)/shard_map/ppermute | solution.py:20
  11.5 0.8 %convert_add_fusion = f32[4,2,16,128]{3,2,1,0:T(8,128)S(1)} fusion(f32[4,2,16,128]{3,2,1,0:T(8,128)} %copy-done.4, bf16[4,2,16,128]{3,2,1,0:T(8,128)(2,1)} %collective-permute-done), kind=kLoop, calls=%fused_computation | loop fusion | flops 32768 | bytes 163840 | tf_op jit(solution)/shard_map/add | solution.py:358
  12.3 2.7 %collective-permute-start.1 = (bf16[2,2,16,128]{3,2,1,0:T(8,128)(2,1)S(1)}, bf16[2,2,16,128]{3,2,1,0:T(8,128)(2,1)S(1)}, u32[]{:S(2)}, u32[]{:S(2)}) collective-permute-start(bf16[2,2,16,128]{3,2,1,0:T(8,128)(2,1)S(1)} %fusion), channel_id=1, source_target_pairs={{0,16},{4,20},{8,24},{12,28},{16,0},{20,4},{24,8},{28,12},{1,17},{... | collective-permute-start | bytes 49160 | tf_op jit(solution)/shard_map/ppermute | solution.py:20
  15.0 0.0 collective-permute-done.6
  15.0 1.4 %constant_dynamic-update-slice_fusion.refs_6_ = bf16[32,1024]{1,0:T(8,128)(2,1)} fusion(bf16[32,1024]{1,0:T(8,128)(2,1)} %constant_dynamic-update-slice_fusion.1, bf16[16,1024]{1,0:T(8,128)(2,1)} %collective-permute-done.6), kind=kLoop, calls=%fused_computation.5 | loop fusion | bytes 65536 | tf_op jit(solution)/shard_map/concatenate | solution.py:351
  16.4 0.0 collective-permute-start.8
  16.4 0.7 %collective-permute-done.1 = bf16[2,2,16,128]{3,2,1,0:T(8,128)(2,1)S(1)} collective-permute-done((bf16[2,2,16,128]{3,2,1,0:T(8,128)(2,1)S(1)}, bf16[2,2,16,128]{3,2,1,0:T(8,128)(2,1)S(1)}, u32[]{:S(2)}, u32[]{:S(2)}) %collective-permute-start.1) | collective-permute-done | bytes 16416 | tf_op jit(solution)/shard_map/ppermute | solution.py:20
  17.0 2.4 %collective-permute-start.7 = (bf16[32,1024]{1,0:T(8,128)(2,1)}, bf16[32,1024]{1,0:T(8,128)(2,1)S(1)}, u32[]{:S(2)}, u32[]{:S(2)}) collective-permute-start(bf16[32,1024]{1,0:T(8,128)(2,1)} %constant_dynamic-update-slice_fusion.refs_6_), channel_id=1, source_target_pairs={{0,4},{1,5},{2,6},{3,7},{4,0},{5,1},{6,2},{7,3},{8,12},{9,13},{10,... | collective-permute-start | bytes 196616 | tf_op jit(solution)/shard_map/ppermute | solution.py:35
  19.4 0.0 collective-permute-done.3.refs_3_
  19.4 0.1 collective-permute-start.2
  19.5 0.0 collective-permute-done.4.refs_4_
  19.5 0.0 collective-permute-done.8.refs_8_
  19.5 2.4 %collective-permute-done.7.refs_7_ = bf16[32,1024]{1,0:T(8,128)(2,1)S(1)} collective-permute-done((bf16[32,1024]{1,0:T(8,128)(2,1)}, bf16[32,1024]{1,0:T(8,128)(2,1)S(1)}, u32[]{:S(2)}, u32[]{:S(2)}) %collective-permute-start.7) | collective-permute-done | bytes 65568 | tf_op jit(solution)/shard_map/ppermute | solution.py:35
  21.9 0.0 collective-permute-done.5.refs_5_
  21.9 0.0 copy-done
  21.9 0.8 %copy-done.3 = bf16[32,1024]{1,0:T(8,128)(2,1)S(1)} copy-done((bf16[32,1024]{1,0:T(8,128)(2,1)S(1)}, bf16[32,1024]{1,0:T(8,128)(2,1)}, u32[]{:S(2)}) %copy-start.3) | copy-done | bytes 65560
  22.8 1.1 %near.1 = (f32[2,16,256]{2,1,0:T(8,128)S(1)}, bf16[2,16,256]{2,1,0:T(8,128)(2,1)S(1)}) custom-call(s32[1,9]{1,0:T(1,128)S(1)} %copy-done.5, s32[1,9]{1,0:T(1,128)S(1)} %copy-done.6, bf16[1,9,256,256]{3,2,1,0:T(8,128)(2,1)S(1)} %copy-done, s32[1,9]{1,0:T(1,128)S(1)} %collective-permute-done.3.refs_3_, s32[1,9]{1,0:T(1,128)S(1)} %collective-permute-done.4.refs_4_, ...), custom_call_target="tpu_custom_call" | custom-call | tf_op jit(solution)/shard_map/near/pallas_call | solution.py:275
  23.8 0.0 collective-permute-start.9
  23.9 0.0 collective-permute-done.2.got
  23.9 0.3 far.1.far_in
  24.2 2.9 %collective-permute-done.9.refs_1_ = bf16[2,16,256]{2,1,0:T(8,128)(2,1)S(1)} collective-permute-done((bf16[2,16,256]{2,1,0:T(8,128)(2,1)S(1)}, bf16[2,16,256]{2,1,0:T(8,128)(2,1)S(1)}, u32[]{:S(2)}, u32[]{:S(2)}) %collective-permute-start.9) | collective-permute-done | bytes 16416 | tf_op jit(solution)/shard_map/ppermute | solution.py:20
  27.0 0.6 %finish.1 = bf16[16,1024]{1,0:T(8,128)(2,1)} custom-call(f32[16,1024]{1,0:T(8,128)S(1)} %far.1.far_in, f32[2,16,256]{2,1,0:T(8,128)S(1)} %get-tuple-element.17.refs_0_, bf16[2,16,256]{2,1,0:T(8,128)(2,1)S(1)} %collective-permute-done.9.refs_1_), custom_call_target="tpu_custom_call" | custom-call | tf_op jit(solution)/shard_map/finish/pallas_call | solution.py:324
  (14 shorter events, 0.1 us)
Async XLA Ops:
  0.0 21.9 %copy-start = (bf16[1,9,256,256]{3,2,1,0:T(8,128)(2,1)S(1)}, bf16[1,9,256,256]{3,2,1,0:T(8,128)(2,1)}, u32[]{:S(2)}) copy-start(bf16[1,9,256,256]{3,2,1,0:T(8,128)(2,1)} %refs_2_.1) | copy-start | bytes 3538948
  0.0 21.9 %copy-start.5 = (s32[1,9]{1,0:T(1,128)S(1)}, s32[1,9]{1,0:T(1,128)}, u32[]{:S(2)}) copy-start(s32[1,9]{1,0:T(1,128)} %refs_0_.1) | copy-start | bytes 112
  0.0 21.9 %copy-start.6 = (s32[1,9]{1,0:T(1,128)S(1)}, s32[1,9]{1,0:T(1,128)}, u32[]{:S(2)}) copy-start(s32[1,9]{1,0:T(1,128)} %refs_1_.1) | copy-start | bytes 112
  0.0 9.4 %copy-start.2 = (bf16[6,32,32]{2,1,0:T(8,128)(2,1)S(1)}, bf16[6,32,32]{2,1,0:T(8,128)(2,1)}, u32[]{:S(2)}) copy-start(bf16[6,32,32]{2,1,0:T(8,128)(2,1)} %transfer.1) | copy-start | bytes 36868
  0.0 9.4 %copy-start.1 = (bf16[4,32,256]{2,1,0:T(8,128)(2,1)S(1)}, bf16[4,32,256]{2,1,0:T(8,128)(2,1)}, u32[]{:S(2)}) copy-start(bf16[4,32,256]{2,1,0:T(8,128)(2,1)} %basis.1) | copy-start | bytes 196612
  0.0 21.9 %collective-permute-start.5 = (bf16[1,9,256,256]{3,2,1,0:T(8,128)(2,1)}, bf16[1,9,256,256]{3,2,1,0:T(8,128)(2,1)S(1)}, u32[]{:S(2)}, u32[]{:S(2)}) collective-permute-start(bf16[1,9,256,256]{3,2,1,0:T(8,128)(2,1)} %refs_2_.1), channel_id=1, source_target_pairs={{0,1},{1,0},{2,3},{3,2},{4,5},{5,4},{6,7},{7,6},{8,9},{9,8},{10,11... | collective-permute-start | bytes 3538952 | tf_op jit(solution)/shard_map/ppermute | solution.py:20
  0.6 18.8 %collective-permute-start.3 = (s32[1,9]{1,0:T(1,128)}, s32[1,9]{1,0:T(1,128)S(1)}, u32[]{:S(2)}, u32[]{:S(2)}) collective-permute-start(s32[1,9]{1,0:T(1,128)} %refs_0_.1), channel_id=1, source_target_pairs={{0,1},{1,0},{2,3},{3,2},{4,5},{5,4},{6,7},{7,6},{8,9},{9,8},{10,11... | collective-permute-start | bytes 116 | tf_op jit(solution)/shard_map/ppermute | solution.py:20
  0.7 18.9 %collective-permute-start.4 = (s32[1,9]{1,0:T(1,128)}, s32[1,9]{1,0:T(1,128)S(1)}, u32[]{:S(2)}, u32[]{:S(2)}) collective-permute-start(s32[1,9]{1,0:T(1,128)} %refs_1_.1), channel_id=1, source_target_pairs={{0,1},{1,0},{2,3},{3,2},{4,5},{5,4},{6,7},{7,6},{8,9},{9,8},{10,11... | collective-permute-start | bytes 116 | tf_op jit(solution)/shard_map/ppermute | solution.py:20
  1.1 13.9 %collective-permute-start.6 = (bf16[16,1024]{1,0:T(8,128)(2,1)}, bf16[16,1024]{1,0:T(8,128)(2,1)}, u32[]{:S(2)}, u32[]{:S(2)}) collective-permute-start(bf16[16,1024]{1,0:T(8,128)(2,1)} %vectors_in.1), channel_id=1, source_target_pairs={{0,3},{1,2},{2,1},{3,0},{4,7},{5,6},{6,5},{7,4},{8,11},{9,10},{10,... | collective-permute-start | bytes 98312 | tf_op jit(solution)/shard_map/ppermute | solution.py:20
  6.6 0.6 %copy-start.4 = (f32[4,2,16,128]{3,2,1,0:T(8,128)}, f32[4,2,16,128]{3,2,1,0:T(8,128)S(1)}, u32[]{:S(2)}) copy-start(f32[4,2,16,128]{3,2,1,0:T(8,128)S(1)} %get-tuple-element.12) | copy-start | bytes 196612
  7.2 4.2 %collective-permute-start = (bf16[4,2,16,128]{3,2,1,0:T(8,128)(2,1)}, bf16[4,2,16,128]{3,2,1,0:T(8,128)(2,1)}, u32[]{:S(2)}, u32[]{:S(2)}) collective-permute-start(bf16[4,2,16,128]{3,2,1,0:T(8,128)(2,1)} %get-tuple-element.13), channel_id=1, source_target_pairs={{0,8},{4,12},{8,0},{12,4},{16,24},{20,28},{24,16},{28,20},{1,9},{5... | collective-permute-start | bytes 98312 | tf_op jit(solution)/shard_map/ppermute | solution.py:20
  12.3 4.7 %collective-permute-start.1 = (bf16[2,2,16,128]{3,2,1,0:T(8,128)(2,1)S(1)}, bf16[2,2,16,128]{3,2,1,0:T(8,128)(2,1)S(1)}, u32[]{:S(2)}, u32[]{:S(2)}) collective-permute-start(bf16[2,2,16,128]{3,2,1,0:T(8,128)(2,1)S(1)} %fusion), channel_id=1, source_target_pairs={{0,16},{4,20},{8,24},{12,28},{16,0},{20,4},{24,8},{28,12},{1,17},{... | collective-permute-start | bytes 49160 | tf_op jit(solution)/shard_map/ppermute | solution.py:20
  16.4 3.2 %collective-permute-start.8 = (bf16[32,1024]{1,0:T(8,128)(2,1)}, bf16[32,1024]{1,0:T(8,128)(2,1)S(1)}, u32[]{:S(2)}, u32[]{:S(2)}) collective-permute-start(bf16[32,1024]{1,0:T(8,128)(2,1)} %constant_dynamic-update-slice_fusion.refs_6_), channel_id=1, source_target_pairs={{0,1},{1,0},{2,3},{3,2},{4,8},{5,9},{6,10},{7,11},{8,4},{9,5},{10,... | collective-permute-start | bytes 196616 | tf_op jit(solution)/shard_map/ppermute | solution.py:35
  17.0 4.9 %collective-permute-start.7 = (bf16[32,1024]{1,0:T(8,128)(2,1)}, bf16[32,1024]{1,0:T(8,128)(2,1)S(1)}, u32[]{:S(2)}, u32[]{:S(2)}) collective-permute-start(bf16[32,1024]{1,0:T(8,128)(2,1)} %constant_dynamic-update-slice_fusion.refs_6_), channel_id=1, source_target_pairs={{0,4},{1,5},{2,6},{3,7},{4,0},{5,1},{6,2},{7,3},{8,12},{9,13},{10,... | collective-permute-start | bytes 196616 | tf_op jit(solution)/shard_map/ppermute | solution.py:35
  19.4 4.5 %collective-permute-start.2 = (bf16[1,2,16,128]{3,2,1,0:T(8,128)(2,1)S(1)}, bf16[1,2,16,128]{3,2,1,0:T(8,128)(2,1)S(1)}, u32[]{:S(2)}, u32[]{:S(2)}) collective-permute-start(bf16[1,2,16,128]{3,2,1,0:T(8,128)(2,1)S(1)} %dynamic-slice_convert_fusion.1), channel_id=1, source_target_pairs={{0,4},{4,0},{8,12},{12,8},{16,20},{20,16},{24,28},{28,24},{1,5},{5... | collective-permute-start | bytes 24584 | tf_op jit(solution)/shard_map/ppermute | solution.py:20
  21.9 0.8 %copy-start.3 = (bf16[32,1024]{1,0:T(8,128)(2,1)S(1)}, bf16[32,1024]{1,0:T(8,128)(2,1)}, u32[]{:S(2)}) copy-start(bf16[32,1024]{1,0:T(8,128)(2,1)} %constant_dynamic-update-slice_fusion.refs_6_) | copy-start | bytes 196612
  23.8 3.2 %collective-permute-start.9 = (bf16[2,16,256]{2,1,0:T(8,128)(2,1)S(1)}, bf16[2,16,256]{2,1,0:T(8,128)(2,1)S(1)}, u32[]{:S(2)}, u32[]{:S(2)}) collective-permute-start(bf16[2,16,256]{2,1,0:T(8,128)(2,1)S(1)} %get-tuple-element.18), channel_id=1, source_target_pairs={{0,3},{1,2},{2,1},{3,0},{4,7},{5,6},{6,5},{7,4},{8,11},{9,10},{10,... | collective-permute-start | bytes 49160 | tf_op jit(solution)/shard_map/ppermute | solution.py:20
